TPU v7x, 32 devices: a whole 2x2x4 slice. The times are simulated.
32 devices in a mesh: dp: 8 (over z, x), view: 2 (over core), mp: 2 (over y).
Axes of the slice: x: 2, y: 2, z: 4, core: 2. Of those that a mesh axis runs over, the one named last changes fastest.
Arguments:
- tokens: bfloat16 [8, 2, 1024, 768], P('dp', 'view', 'mp'), may hold values from -6 to 6
- partner: int32 [8], replicated, may hold values from 0 to 7, each once
- mix_weight: float32 [8], P('dp'), may hold values from 0.2 to 0.8
- video_ids: int32 [8], replicated, may hold values from 0 to 3, never falling along the last dimension, each value on 1 to 4 neighbouring positions
- view_counts: int32 [2], replicated, may hold values from 256 to 1024, as said below
- self_project: bfloat16 [2, 3, 768, 768], P('view', None, None, 'mp'), may hold values from -0.21875 to 0.21875
- self_merge: bfloat16 [2, 768, 768], P('view', 'mp'), may hold values from -4 to 4
- cross_project: bfloat16 [2, 3, 768, 768], P('view', None, None, 'mp'), may hold values from -0.21875 to 0.21875
- cross_merge: bfloat16 [2, 768, 768], P('view', 'mp'), may hold values from -4 to 4
- hidden_up: bfloat16 [2, 768, 3072], P('view', None, 'mp'), may hold values from -0.21875 to 0.21875
- hidden_down: bfloat16 [2, 3072, 768], P('view', 'mp'), may hold values from -0.109375 to 0.109375
- norm_self: float32 [2, 768], P('view'), may hold values from 0.5 to 1.5
- norm_cross: float32 [2, 768], P('view'), may hold values from 0.5 to 1.5
- norm_hidden: float32 [2, 768], P('view'), may hold values from 0.5 to 1.5
- summary_project: bfloat16 [3, 768, 768], P(None, None, 'mp'), may hold values from -0.21875 to 0.21875
- summary_merge: bfloat16 [768, 768], P('mp'), may hold values from -0.375 to 0.375
- summary_up: bfloat16 [768, 3072], P(None, 'mp'), may hold values from -0.21875 to 0.21875
- summary_down: bfloat16 [3072, 768], P('mp'), may hold values from -0.109375 to 0.109375
- summary_norm_self: float32 [768], replicated, may hold values from 0.5 to 1.5
- summary_norm_hidden: float32 [768], replicated, may hold values from 0.5 to 1.5
- tokens_cotangent: bfloat16 [8, 2, 1024, 768], P('dp', 'view', 'mp'), may hold values from -6 to 6
- summary_cotangent: float32 [8, 2, 768], replicated, may hold values from -6 to 6
Outputs:
- tokens_out: bfloat16 [8, 2, 1024, 768], P('dp', 'view', 'mp')
- summary_out: float32 [8, 2, 768], replicated
- tokens_grad: float32 [8, 2, 1024, 768], P('dp', 'view', 'mp')
- self_project_grad: float32 [2, 3, 768, 768], P('view', None, None, 'mp')
- self_merge_grad: float32 [2, 768, 768], P('view', 'mp')
- cross_project_grad: float32 [2, 3, 768, 768], P('view', None, None, 'mp')
- cross_merge_grad: float32 [2, 768, 768], P('view', 'mp')
- hidden_up_grad: float32 [2, 768, 3072], P('view', None, 'mp')
- hidden_down_grad: float32 [2, 3072, 768], P('view', 'mp')
- norm_self_grad: float32 [2, 768], P('view')
- norm_cross_grad: float32 [2, 768], P('view')
- norm_hidden_grad: float32 [2, 768], P('view')
- summary_project_grad: float32 [3, 768, 768], P(None, None, 'mp')
- summary_merge_grad: float32 [768, 768], P('mp')
- summary_up_grad: float32 [768, 3072], P(None, 'mp')
- summary_down_grad: float32 [3072, 768], P('mp')
- summary_norm_self_grad: float32 [768], replicated
- summary_norm_hidden_grad: float32 [768], replicated
Inputs may be any that keep to these rules, and one draw needn't show every extreme that they name: Every clip is the partner of exactly one clip. `video_ids`: ids never fall from one clip to the next. `view_counts`: positions from a view's count on are padding; some view has all 1024 positions real.
All inputs are finite; a program needn't handle non-finite values.
Results may differ from a plain program's by a relative error of at most 0.035.
Values may be sent and summed in bfloat16 or wider, within the bound.
A program may use at most 256 MiB of HBM per device.

v0:
```python
import jax
import jax.numpy as jnp
from jax import lax
from jax.sharding import PartitionSpec as P

D = 768
HEAD = 64
BLOCK = 512


EPS = 1e-05
NEG = -1000000000.0


def shifted(value, axis, steps):
    count = lax.axis_size(axis)
    pairs = [(source, (source + steps) % count) for source in range(count)]
    return lax.ppermute(value, axis, pairs)


def layer_norm(rows, gain):
    center = rows - jnp.mean(rows, -1, keepdims=True)
    inverse = lax.rsqrt(jnp.mean(center * center, -1, keepdims=True) + EPS)
    unit = center * inverse
    return (unit * gain, unit, inverse)


def layer_norm_back(grad_out, unit, inverse, gain):
    gain_grad = jnp.sum(grad_out * unit, axis=tuple(range(grad_out.ndim - 1)))
    scaled = grad_out * gain
    centered = scaled - jnp.mean(scaled, -1, keepdims=True)
    return (inverse * (centered - unit * jnp.mean(scaled * unit, -1, keepdims=True)), gain_grad)


def gelu_exact(values):
    return jax.nn.gelu(values, approximate=False)


def product(left, right, form):
    return jnp.einsum(form, left, right, preferred_element_type=jnp.float32)


def split_heads(rows):
    return rows.reshape(rows.shape[:-1] + (rows.shape[-1] // HEAD, HEAD))


def merge_heads(rows):
    return rows.reshape(rows.shape[:-2] + (rows.shape[-2] * rows.shape[-1],))


def token_rows(pieces):
    return lax.all_gather(pieces, "mp", axis=1, tiled=True)


def token_sums(terms):
    return lax.psum_scatter(
        terms.astype(jnp.bfloat16), "mp", scatter_dimension=1, tiled=True
    ).astype(jnp.float32)


def keep_local(values):
    return values


def to_blocks(array, block):
    array_shape = array.shape
    return jnp.swapaxes(
        array.reshape((array_shape[0], array_shape[1] // block, block) + array_shape[2:]), 0, 1
    )


def from_blocks(array):
    moved = jnp.swapaxes(array, 0, 1)
    array_shape = moved.shape
    return moved.reshape((array_shape[0], array_shape[1] * array_shape[2]) + array_shape[3:])


def attend_block(query_block, key_rows, value_rows, valid):
    scores = jnp.where(valid, product(query_block, key_rows, "cqhe,ckhe->chqk"), NEG)
    highest = jnp.max(scores, -1, keepdims=True)
    raised = jnp.exp(scores - highest)
    totals = jnp.sum(raised, -1, keepdims=True)
    weights = (raised / totals).astype(jnp.bfloat16)
    result = product(weights, value_rows, "chqk,ckhe->cqhe").astype(jnp.bfloat16)
    return (result, (highest + jnp.log(totals))[..., 0])


def attend(query, key_rows, value_rows, valid, block):

    def one_block(query_block):
        return attend_block(query_block, key_rows, value_rows, valid)

    blocks_out, block_sums = lax.map(one_block, to_blocks(query, block))
    log_sums = jnp.moveaxis(block_sums, 0, 2)
    return (from_blocks(blocks_out), log_sums.reshape(log_sums.shape[:2] + (-1,)))


def attend_back(query, key_rows, value_rows, valid, block, grad_out, log_sums):
    lse_blocks = jnp.moveaxis(log_sums.reshape(log_sums.shape[:2] + (-1, block)), 2, 0)

    def step(carry, inputs):
        key_grad, value_grad = carry
        query_block, grad_block, lse_block = inputs
        scores = jnp.where(valid, product(query_block, key_rows, "cqhe,ckhe->chqk"), NEG)
        weights = jnp.exp(scores - lse_block[..., None])
        grad_weights = product(grad_block, value_rows, "cqhe,ckhe->chqk")
        grad_scores = (
            weights * (grad_weights - jnp.sum(weights * grad_weights, -1, keepdims=True))
        ).astype(jnp.bfloat16)
        query_grad = product(grad_scores, key_rows, "chqk,ckhe->cqhe").astype(jnp.bfloat16)
        key_grad = key_grad + product(grad_scores, query_block, "chqk,cqhe->ckhe")
        value_grad = value_grad + product(
            weights.astype(jnp.bfloat16), grad_block, "chqk,cqhe->ckhe"
        )
        return ((key_grad, value_grad), query_grad)

    empty = jnp.zeros(key_rows.shape, jnp.float32)
    (key_grad, value_grad), query_grads = lax.scan(
        step, (empty, empty), (to_blocks(query, block), to_blocks(grad_out, block), lse_blocks)
    )
    return (
        from_blocks(query_grads),
        key_grad.astype(jnp.bfloat16),
        value_grad.astype(jnp.bfloat16),
    )


def qkv_rows(query_source, key_source, weights):
    scale = HEAD ** (-0.5)
    query = (product(query_source, weights[0], "csd,de->cse") * scale).astype(jnp.bfloat16)
    key_rows = product(key_source, weights[1], "csd,de->cse").astype(jnp.bfloat16)
    value_rows = product(key_source, weights[2], "csd,de->cse").astype(jnp.bfloat16)
    return (split_heads(query), split_heads(key_rows), split_heads(value_rows))


def qkv_back(query_source, key_source, weights, grads):
    scale = HEAD ** (-0.5)
    query_grad = merge_heads(grads[0]) * scale
    key_grad = merge_heads(grads[1])
    value_grad = merge_heads(grads[2])
    weight_grad = jnp.stack(
        [
            product(query_source, query_grad, "csd,cse->de"),
            product(key_source, key_grad, "csd,cse->de"),
            product(key_source, value_grad, "csd,cse->de"),
        ]
    )
    query_term = product(query_grad, weights[0], "cse,de->csd")
    key_term = product(key_grad, weights[1], "cse,de->csd") + product(
        value_grad, weights[2], "cse,de->csd"
    )
    return (weight_grad, query_term, key_term)


def summary_layer(
    summary_rows, top_grad, weights, gain_top, gain_last, summary_valid, row_total, reducers
):
    use_project, use_merge, use_up, use_down = weights
    reduce_merge, reduce_down, reduce_up, reduce_project = reducers
    top_normed, top_unit, top_inverse = layer_norm(summary_rows, gain_top)
    top_low = top_normed.astype(jnp.bfloat16)[None]
    top_query, top_key, top_value = qkv_rows(top_low, top_low, use_project)
    top_heads, top_sums = attend(top_query, top_key, top_value, summary_valid, row_total)
    top_flat = merge_heads(top_heads)
    summary_mid = summary_rows + reduce_merge(product(top_flat, use_merge, "cse,ed->csd")[0])
    mid_normed, mid_unit, mid_inverse = layer_norm(summary_mid, gain_last)
    mid_low = mid_normed.astype(jnp.bfloat16)[None]
    top_before = product(mid_low, use_up, "csd,df->csf")
    top_hidden = gelu_exact(top_before).astype(jnp.bfloat16)
    summary_final = summary_mid + reduce_down(product(top_hidden, use_down, "csf,fd->csd")[0])
    down_input = top_grad.astype(jnp.bfloat16)[None]
    down_grad = product(top_hidden, down_input, "csf,csd->fd")
    act_grad = jax.vjp(gelu_exact, top_before)[1](product(down_input, use_down, "csd,fd->csf"))[
        0
    ].astype(jnp.bfloat16)
    up_grad = product(mid_low, act_grad, "csd,csf->df")
    mid_rows_grad, last_gain_grad = layer_norm_back(
        reduce_up(product(act_grad, use_up, "csf,df->csd")[0]), mid_unit, mid_inverse, gain_last
    )
    mid_grad = top_grad + mid_rows_grad
    merge_input = mid_grad.astype(jnp.bfloat16)[None]
    merge_grad = product(top_flat, merge_input, "cse,csd->ed")
    top_heads_grad = split_heads(
        product(merge_input, use_merge, "csd,ed->cse").astype(jnp.bfloat16)
    )
    top_grads = attend_back(
        top_query, top_key, top_value, summary_valid, row_total, top_heads_grad, top_sums
    )
    project_grad, top_query_term, top_key_term = qkv_back(top_low, top_low, use_project, top_grads)
    first_top_grad, top_gain_grad = layer_norm_back(
        reduce_project((top_query_term + top_key_term)[0]), top_unit, top_inverse, gain_top
    )
    class_grad = mid_grad + first_top_grad
    return (
        summary_final,
        class_grad,
        (project_grad, merge_grad, up_grad, down_grad),
        top_gain_grad,
        last_gain_grad,
    )


def shards(
    tokens,
    partner,
    mix_weight,
    video_ids,
    view_counts,
    self_project,
    self_merge,
    cross_project,
    cross_merge,
    hidden_up,
    hidden_down,
    norm_self,
    norm_cross,
    norm_hidden,
    summary_project,
    summary_merge,
    summary_up,
    summary_down,
    summary_norm_self,
    summary_norm_hidden,
    tokens_cotangent,
    summary_cotangent,
):
    local_tokens = tokens[:, 0]
    clip_count = local_tokens.shape[0]
    data_index = lax.axis_index("dp")
    view_index = lax.axis_index("view")
    model_index = lax.axis_index("mp")
    view_total = lax.axis_size("view")
    clip_total = clip_count * lax.axis_size("dp")
    seq_length = local_tokens.shape[1] * lax.axis_size("mp")
    block_rows = min(BLOCK, seq_length)
    own_clips = data_index * clip_count + jnp.arange(clip_count, dtype=jnp.int32)
    wanted = lax.dynamic_slice_in_dim(partner, data_index * clip_count, clip_count)
    piece = lax.all_gather(local_tokens, "dp", axis=0, tiled=True)
    chooser = (wanted[:, None] == jnp.arange(piece.shape[0], dtype=jnp.int32)[None, :]).astype(
        jnp.bfloat16
    )
    partner_tokens = product(chooser, piece, "cr,rsd->csd")
    mixing = mix_weight[:, None, None]
    mixed_rows = mixing * local_tokens.astype(jnp.float32) + (1.0 - mixing) * partner_tokens
    positions = jnp.arange(seq_length)
    own_valid = (positions < view_counts[view_index])[None, None, None, :]
    next_valid = (positions < view_counts[(view_index + 1) % view_total])[None, None, None, :]
    normed_self, unit_self, inverse_self = layer_norm(mixed_rows, norm_self[0])
    gathered_self = token_rows(normed_self.astype(jnp.bfloat16))
    query_self, key_self, value_self = qkv_rows(gathered_self, gathered_self, self_project[0])
    heads_self, sums_self = attend(query_self, key_self, value_self, own_valid, block_rows)
    flat_self = merge_heads(heads_self)
    first_rows = mixed_rows + token_sums(product(flat_self, self_merge[0], "cse,ed->csd"))
    normed_cross, unit_cross, inverse_cross = layer_norm(first_rows, norm_cross[0])
    shard_cross = normed_cross.astype(jnp.bfloat16)
    gathered_cross = token_rows(shard_cross)
    next_cross = shifted(gathered_cross, "view", -1)
    query_cross, key_cross, value_cross = qkv_rows(gathered_cross, next_cross, cross_project[0])
    heads_cross, sums_cross = attend(query_cross, key_cross, value_cross, next_valid, block_rows)
    flat_cross = merge_heads(heads_cross)
    second_rows = first_rows + token_sums(product(flat_cross, cross_merge[0], "cse,ed->csd"))
    normed_hidden, unit_hidden, inverse_hidden = layer_norm(second_rows, norm_hidden[0])
    gathered_hidden = token_rows(normed_hidden.astype(jnp.bfloat16))
    before_hidden = product(gathered_hidden, hidden_up[0], "csd,df->csf")
    hidden_rows = gelu_exact(before_hidden).astype(jnp.bfloat16)
    third_rows = second_rows + token_sums(product(hidden_rows, hidden_down[0], "csf,fd->csd"))
    first_model = (model_index == 0).astype(jnp.float32)
    clip_match = (jnp.arange(clip_total, dtype=jnp.int32)[:, None] == own_clips[None, :]).astype(
        jnp.float32
    )
    view_match = (jnp.arange(view_total) == view_index).astype(jnp.float32)
    class_own = third_rows[:, 0, :] * first_model
    placed = jnp.sum(clip_match[:, :, None] * class_own[None, :, :], axis=1)
    placed = placed[:, None, :] * view_match[None, :, None]
    class_grid = lax.psum(placed, ("dp", "view", "mp"))
    row_total = clip_total * view_total
    summary_rows = class_grid.reshape(row_total, D)
    token_video = jnp.repeat(video_ids, view_total)
    summary_valid = (token_video[:, None] == token_video[None, :])[None, None]
    top_grad = summary_cotangent.reshape(row_total, D)
    full_weights = (
        lax.all_gather(summary_project, "mp", axis=2, tiled=True),
        lax.all_gather(summary_merge, "mp", axis=0, tiled=True),
        lax.all_gather(summary_up, "mp", axis=1, tiled=True),
        lax.all_gather(summary_down, "mp", axis=0, tiled=True),
    )
    summary_final, class_flat, full_grads, summary_norm_self_grad, summary_norm_hidden_grad = (
        summary_layer(
            summary_rows,
            top_grad,
            full_weights,
            summary_norm_self,
            summary_norm_hidden,
            summary_valid,
            row_total,
            (keep_local, keep_local, keep_local, keep_local),
        )
    )
    project_full, merge_full, up_full, down_full = full_grads
    width = summary_project.shape[2]
    hidden_width = summary_up.shape[1]
    summary_project_grad = lax.dynamic_slice_in_dim(project_full, model_index * width, width, 2)
    summary_merge_grad = lax.dynamic_slice_in_dim(merge_full, model_index * width, width, 0)
    summary_up_grad = lax.dynamic_slice_in_dim(up_full, model_index * hidden_width, hidden_width, 1)
    summary_down_grad = lax.dynamic_slice_in_dim(
        down_full, model_index * hidden_width, hidden_width, 0
    )
    summary_out = summary_final.reshape(clip_total, view_total, D)
    class_grad = class_flat.reshape(clip_total, view_total, D)
    view_pick = jnp.sum(class_grad * view_match[None, :, None], axis=1)
    own_class = jnp.sum(clip_match[:, :, None] * view_pick[:, None, :], axis=0) * first_model
    third_grad = tokens_cotangent[:, 0].astype(jnp.float32)
    third_grad = third_grad.at[:, 0].add(own_class)
    down_rows = token_rows(third_grad.astype(jnp.bfloat16))
    down_grad = product(hidden_rows, down_rows, "csf,csd->fd")
    act_grad = jax.vjp(gelu_exact, before_hidden)[1](
        product(down_rows, hidden_down[0], "csd,fd->csf")
    )[0].astype(jnp.bfloat16)
    up_grad = product(gathered_hidden, act_grad, "csd,csf->df")
    hidden_norm_grad = token_sums(product(act_grad, hidden_up[0], "csf,df->csd"))
    rows_grad_hidden, gain_hidden_grad = layer_norm_back(
        hidden_norm_grad, unit_hidden, inverse_hidden, norm_hidden[0]
    )
    second_grad = third_grad + rows_grad_hidden
    cross_rows = token_rows(second_grad.astype(jnp.bfloat16))
    cross_merge_grad = product(flat_cross, cross_rows, "cse,csd->ed")
    cross_heads_grad = split_heads(
        product(cross_rows, cross_merge[0], "csd,ed->cse").astype(jnp.bfloat16)
    )
    cross_grads = attend_back(
        query_cross, key_cross, value_cross, next_valid, block_rows, cross_heads_grad, sums_cross
    )
    cross_project_grad, own_term, next_term = qkv_back(
        gathered_cross, next_cross, cross_project[0], cross_grads
    )
    returned = shifted(next_term.astype(jnp.bfloat16), "view", 1).astype(next_term.dtype)
    cross_norm_grad = token_sums(own_term + returned)
    rows_grad_cross, gain_cross_grad = layer_norm_back(
        cross_norm_grad, unit_cross, inverse_cross, norm_cross[0]
    )
    first_grad = second_grad + rows_grad_cross
    self_rows = token_rows(first_grad.astype(jnp.bfloat16))
    self_merge_grad = product(flat_self, self_rows, "cse,csd->ed")
    self_heads_grad = split_heads(
        product(self_rows, self_merge[0], "csd,ed->cse").astype(jnp.bfloat16)
    )
    self_grads = attend_back(
        query_self, key_self, value_self, own_valid, block_rows, self_heads_grad, sums_self
    )
    self_project_grad, self_query_term, self_key_term = qkv_back(
        gathered_self, gathered_self, self_project[0], self_grads
    )
    self_norm_grad = token_sums(self_query_term + self_key_term)
    rows_grad_self, gain_self_grad = layer_norm_back(
        self_norm_grad, unit_self, inverse_self, norm_self[0]
    )
    mixed_grad = first_grad + rows_grad_self
    sent_rows = ((1.0 - mixing) * mixed_grad).astype(jnp.bfloat16)
    chooser = (own_clips[:, None] == partner[None, :]).astype(jnp.bfloat16)
    returned_rows = product(
        chooser, lax.all_gather(sent_rows, "dp", axis=0, tiled=True), "cr,rsd->csd"
    )
    tokens_grad = (mixing * mixed_grad + returned_rows)[:, None]
    self_project_grad, self_merge_grad, cross_project_grad, cross_merge_grad, up_grad, down_grad = (
        lax.psum(self_project_grad.astype(jnp.bfloat16), "dp").astype(jnp.float32),
        lax.psum(self_merge_grad.astype(jnp.bfloat16), "dp").astype(jnp.float32),
        lax.psum(cross_project_grad.astype(jnp.bfloat16), "dp").astype(jnp.float32),
        lax.psum(cross_merge_grad.astype(jnp.bfloat16), "dp").astype(jnp.float32),
        lax.psum(up_grad.astype(jnp.bfloat16), "dp").astype(jnp.float32),
        lax.psum(down_grad.astype(jnp.bfloat16), "dp").astype(jnp.float32),
    )
    gain_self_grad, gain_cross_grad, gain_hidden_grad = lax.psum(
        (gain_self_grad, gain_cross_grad, gain_hidden_grad), ("dp", "mp")
    )
    tokens_out = third_rows.astype(jnp.bfloat16)[:, None]
    return (
        tokens_out,
        summary_out,
        tokens_grad,
        self_project_grad[None],
        self_merge_grad[None],
        cross_project_grad[None],
        cross_merge_grad[None],
        up_grad[None],
        down_grad[None],
        gain_self_grad[None],
        gain_cross_grad[None],
        gain_hidden_grad[None],
        summary_project_grad,
        summary_merge_grad,
        summary_up_grad,
        summary_down_grad,
        summary_norm_self_grad,
        summary_norm_hidden_grad,
    )


def solution(mesh):
    in_specs = (
        P("dp", "view", "mp", None),
        P(),
        P("dp"),
        P(),
        P(),
        P("view", None, None, "mp"),
        P("view", "mp", None),
        P("view", None, None, "mp"),
        P("view", "mp", None),
        P("view", None, "mp"),
        P("view", "mp", None),
        P("view", None),
        P("view", None),
        P("view", None),
        P(None, None, "mp"),
        P("mp", None),
        P(None, "mp"),
        P("mp", None),
        P(),
        P(),
        P("dp", "view", "mp", None),
        P(),
    )
    out_specs = (
        P("dp", "view", "mp", None),
        P(),
        P("dp", "view", "mp", None),
        P("view", None, None, "mp"),
        P("view", "mp", None),
        P("view", None, None, "mp"),
        P("view", "mp", None),
        P("view", None, "mp"),
        P("view", "mp", None),
        P("view", None),
        P("view", None),
        P("view", None),
        P(None, None, "mp"),
        P("mp", None),
        P(None, "mp"),
        P("mp", None),
        P(),
        P(),
    )
    return jax.shard_map(shards, mesh=mesh, in_specs=in_specs, out_specs=out_specs, check_vma=False)
```

profile of v0, /device:TPU:0, one launch (start us, length us, event | category | flops | bytes accessed | tf_op | source)
XLA Modules:
  0.0 1366.4 jit_solution(577607166449798390)
XLA Ops:
  10.6 101.1 %all-gather.35.cloned.1.call-done = bf16[8,1,512,768]{3,2,1,0:T(8,128)(2,1)} async-done(((bf16[1,1,512,768]{3,2,1,0:T(8,128)(2,1)}), bf16[8,1,512,768]{3,2,1,0:T(8,128)(2,1)}) %all-gather.35.cloned.1.call-update) | async-done | bytes 6291472 | tf_op jit(solution)/shard_map/all_gather | solution.py:238
  123.4 24.6 %all-gather.37.cloned.1.call-done = bf16[1024,768]{1,0:T(8,128)(2,1)} async-done(((bf16[512,768]{1,0:T(8,128)(2,1)}), bf16[1024,768]{1,0:T(8,128)(2,1)}) %all-gather.37.cloned.1.call-update) | async-done | bytes 1572880 | tf_op jit(solution)/shard_map/all_gather | solution.py:52
  162.6 22.0 %while.68 = (s32[]{:T(128)}, bf16[2,1,512,6,64]{2,4,3,1,0:T(8,128)(2,1)}, f32[2,1,6,512]{3,2,1,0:T(8,128)S(1)}, bf16[2,1,512,6,64]{2,4,3,1,0:T(8,128)(2,1)}, bf1...) while((s32[]{:T(128)}, ...), condition=%wide.region_5.6_spmd.clone, body=%wide.region_2.5_spmd.clone.sunk | while | flops 833812480 | bytes 49668288 | solution.py:93
  190.2 26.2 %reduce-scatter.7.cloned.1.call-done = bf16[1,512,768]{2,1,0:T(8,128)(2,1)} async-done(((bf16[1,1024,768]{2,1,0:T(8,128)(2,1)}), bf16[1,512,768]{2,1,0:T(8,128)(2,1)}) %reduce-scatter.7.cloned.1.call-update) | async-done | bytes 786448 | tf_op jit(solution)/shard_map/reduce_scatter | solution.py:56
  221.5 27.1 %all-gather.15.cloned.1.call-done = bf16[1,1024,768]{2,1,0:T(8,128)(2,1)} async-done(((bf16[1,512,768]{2,1,0:T(8,128)(2,1)}), bf16[1,1024,768]{2,1,0:T(8,128)(2,1)}) %all-gather.15.cloned.1.call-update) | async-done | bytes 1572880 | tf_op jit(solution)/shard_map/all_gather | solution.py:52
  263.5 21.9 %while.69 = (s32[]{:T(128)}, bf16[2,1,512,6,64]{2,4,3,1,0:T(8,128)(2,1)}, f32[2,1,6,512]{3,2,1,0:T(8,128)S(1)}, bf16[2,1,512,6,64]{2,4,3,1,0:T(8,128)(2,1)}, bf1...) while((s32[]{:T(128)}, ...), condition=%wide.region_12.13_spmd.clone, body=%wide.region_9.12_spmd.clone.sunk | while | flops 833812480 | bytes 49668288 | solution.py:93
  291.0 26.4 %reduce-scatter.9.cloned.1.call-done = bf16[1,512,768]{2,1,0:T(8,128)(2,1)} async-done(((bf16[1,1024,768]{2,1,0:T(8,128)(2,1)}), bf16[1,512,768]{2,1,0:T(8,128)(2,1)}) %reduce-scatter.9.cloned.1.call-update) | async-done | bytes 786448 | tf_op jit(solution)/shard_map/reduce_scatter | solution.py:56
  321.6 27.3 %all-gather.17.cloned.1.call-done = bf16[1,1024,768]{2,1,0:T(8,128)(2,1)} async-done(((bf16[1,512,768]{2,1,0:T(8,128)(2,1)}), bf16[1,1024,768]{2,1,0:T(8,128)(2,1)}) %all-gather.17.cloned.1.call-update) | async-done | bytes 1572880 | tf_op jit(solution)/shard_map/all_gather | solution.py:52
  348.9 18.2 %multiply_convert_fusion.2 = (bf16[1024,1536]{1,0:T(8,128)(2,1)S(1)}, f32[1024,1536]{1,0:T(8,128)}, f32[1024,1536]{1,0:T(8,128)}) fusion(bf16[1,768,1536]{2,1,0:T(8,128)(2,1)S(1)} %copy-done, bf16[1,1024,768]{2,1,0:T(8,128)(2,1)} %all-gather.17.cloned.1.call-done), kind=kOutput, calls=%fused_computation.114 | convolution fusion | flops 2518155264 | bytes 19660800 | tf_op jit(solution)/shard_map/csd,df->csf/dot_general | solution.py:40
  376.9 21.8 %reduce-scatter.11.cloned.1.call-done = bf16[1,512,768]{2,1,0:T(8,128)(2,1)} async-done(((bf16[1,1024,768]{2,1,0:T(8,128)(2,1)}), bf16[1,512,768]{2,1,0:T(8,128)(2,1)}) %reduce-scatter.11.cloned.1.call-update) | async-done | bytes 786448 | tf_op jit(solution)/shard_map/reduce_scatter | solution.py:56
  401.5 41.1 %psum.70 = f32[8,2,768]{2,1,0:T(2,128)S(1)} all-reduce(f32[8,2,768]{2,1,0:T(2,128)S(1)} %broadcast_multiply_fusion.2), channel_id=1, replica_groups=mesh['dp'=8,'view'=2,'mp'=2] {'dp','view','mp'}, use_global_device_ids=true, to_apply=%region_17.18 | all-reduce | flops 12288 | bytes 98304 | tf_op jit(solution)/shard_map/psum | solution.py:275
  456.1 18.7 %all-gather.21.cloned.1.call-done = bf16[768,768]{1,0:T(8,128)(2,1)} async-done(((bf16[384,768]{1,0:T(8,128)(2,1)}), bf16[768,768]{1,0:T(8,128)(2,1)}) %all-gather.21.cloned.1.call-update) | async-done | bytes 1179664 | tf_op jit(solution)/shard_map/all_gather | solution.py:283
  477.2 61.8 %all-gather.23.cloned.1.call-done = bf16[768,3072]{1,0:T(8,128)(2,1)} async-done(((bf16[768,1536]{1,0:T(8,128)(2,1)}), bf16[768,3072]{1,0:T(8,128)(2,1)}) %all-gather.23.cloned.1.call-update) | async-done | bytes 4718608 | tf_op jit(solution)/shard_map/all_gather | solution.py:284
  542.0 61.1 %all-gather.25.cloned.1.call-done = bf16[3072,768]{1,0:T(8,128)(2,1)} async-done(((bf16[1536,768]{1,0:T(8,128)(2,1)}), bf16[3072,768]{1,0:T(8,128)(2,1)}) %all-gather.25.cloned.1.call-update) | async-done | bytes 4718608 | tf_op jit(solution)/shard_map/all_gather | solution.py:285
  621.5 27.3 %all-gather.27.cloned.1.call-done = bf16[1,1024,768]{2,1,0:T(8,128)(2,1)} async-done(((bf16[1,512,768]{2,1,0:T(8,128)(2,1)}), bf16[1,1024,768]{2,1,0:T(8,128)(2,1)}) %all-gather.27.cloned.1.call-update) | async-done | bytes 1572880 | tf_op jit(solution)/shard_map/all_gather | solution.py:52
  664.3 26.1 %reduce-scatter.13.cloned.1.call-done = bf16[1,512,768]{2,1,0:T(8,128)(2,1)} async-done(((bf16[1,1024,768]{2,1,0:T(8,128)(2,1)}), bf16[1,512,768]{2,1,0:T(8,128)(2,1)}) %reduce-scatter.13.cloned.1.call-update) | async-done | bytes 786448 | tf_op jit(solution)/shard_map/reduce_scatter | solution.py:56
  695.0 27.3 %all-gather.29.cloned.1.call-done = bf16[1,1024,768]{2,1,0:T(8,128)(2,1)} async-done(((bf16[1,512,768]{2,1,0:T(8,128)(2,1)}), bf16[1,1024,768]{2,1,0:T(8,128)(2,1)}) %all-gather.29.cloned.1.call-update) | async-done | bytes 1572880 | tf_op jit(solution)/shard_map/all_gather | solution.py:52
  732.4 48.8 %while.70 = (s32[]{:T(128)}, f32[1,1024,6,64]{1,3,2,0:T(8,128)S(1)}, f32[1,1024,6,64]{1,3,2,0:T(8,128)}, bf16[2,1,512,6,64]{2,4,3,1,0:T(8,128)(2,1)}, bf16[2,1,5...) while((s32[]{:T(128)}, ...), condition=%wide.region_36.37_spmd.clone, body=%wide.region_34.36_spmd.clone.sunk | while | flops 2052782080 | bytes 139686160 | solution.py:118
  791.2 26.2 %reduce-scatter.15.cloned.1.call-done = bf16[1,512,768]{2,1,0:T(8,128)(2,1)} async-done(((bf16[1,1024,768]{2,1,0:T(8,128)(2,1)}), bf16[1,512,768]{2,1,0:T(8,128)(2,1)}) %reduce-scatter.15.cloned.1.call-update) | async-done | bytes 786448 | tf_op jit(solution)/shard_map/reduce_scatter | solution.py:56
  822.2 27.3 %all-gather.31.cloned.1.call-done = bf16[1,1024,768]{2,1,0:T(8,128)(2,1)} async-done(((bf16[1,512,768]{2,1,0:T(8,128)(2,1)}), bf16[1,1024,768]{2,1,0:T(8,128)(2,1)}) %all-gather.31.cloned.1.call-update) | async-done | bytes 1572880 | tf_op jit(solution)/shard_map/all_gather | solution.py:52
  859.7 49.1 %while.71 = (s32[]{:T(128)}, f32[1,1024,6,64]{1,3,2,0:T(8,128)S(1)}, f32[1,1024,6,64]{1,3,2,0:T(8,128)}, bf16[2,1,512,6,64]{2,4,3,1,0:T(8,128)(2,1)}, bf16[2,1,5...) while((s32[]{:T(128)}, ...), condition=%wide.region_42.43_spmd.clone, body=%wide.region_40.42_spmd.clone.sunk | while | flops 2052782080 | bytes 139686160 | solution.py:118
  968.8 46.2 %all-reduce = (f32[1,768]{1,0:T(1,128)}, f32[1,768]{1,0:T(1,128)}, f32[1,768]{1,0:T(1,128)}) all-reduce(f32[1,768]{1,0:T(1,128)S(1)} %broadcast_in_dim.224, f32[1,768]{1,0:T(1,128)S(1)} %broadcast_in_dim.225, f32[1,768]{1,0:T(1,128)S(1)} %broadcast_in_dim.226), channel_id=1, replica_groups=mesh['dp'=8,'view'=2,'mp'=2] {'dp','mp'}, use_global_device_ids=true, to_apply=%region_53.54 | all-reduce | flops 2304 | bytes 18432 | tf_op jit(solution)/shard_map/psum | solution.py:372
  1015.0 235.5 %all-reduce.4.cloned.1.call-done = (bf16[1,3,768,384]{3,2,1,0:T(8,128)(2,1)}, bf16[1,384,768]{2,1,0:T(8,128)(2,1)}, bf16[1,3,768,384]{3,2,1,0:T(8,128)(2,1)}, bf...) async-done(((bf16[1,3,768,384]{3,2,1,0:T(8,128)(2,1)}, bf16[1,384,768]{2,1,0:T(8,128)(2,1)}, ...) | async-done | bytes 9437200 | tf_op jit(solution)/shard_map/psum | solution.py:365
  1265.4 84.9 %all-gather.33.cloned.1.call-done = bf16[8,512,768]{2,1,0:T(8,128)(2,1)} async-done(((bf16[1,512,768]{2,1,0:T(8,128)(2,1)}), bf16[8,512,768]{2,1,0:T(8,128)(2,1)}) %all-gather.33.cloned.1.call-update) | async-done | bytes 6291472 | tf_op jit(solution)/shard_map/all_gather | solution.py:361
  (554 shorter events, 392.7 us)
Async XLA Ops:
  7.2 341.7 %copy-start = (bf16[1,768,1536]{2,1,0:T(8,128)(2,1)S(1)}, bf16[1,768,1536]{2,1,0:T(8,128)(2,1)}, u32[]{:S(2)}) copy-start(bf16[1,768,1536]{2,1,0:T(8,128)(2,1)} %param.41) | copy-start | bytes 7077892
  7.2 104.4 %all-gather.35.cloned.1.call-start = ((), (), s32[]{:S(2)}) async-start(), calls=%async_computation.22 | async-start | bytes 7077888 | tf_op jit(solution)/shard_map/all_gather | solution.py:238
  7.9 140.1 %all-gather.37.cloned.1.call-start = ((), (), s32[]{:S(2)}) async-start(), calls=%async_computation.23 | async-start | bytes 2359296 | tf_op jit(solution)/shard_map/all_gather | solution.py:52
  10.6 109.4 %copy-start.84 = (f32[768]{0:T(1024)}, f32[768]{0:T(1024)S(1)}, u32[]{:S(2)}) copy-start(f32[768]{0:T(1024)S(1)} %reduce.43) | copy-start | bytes 9220
  122.5 93.9 %reduce-scatter.7.cloned.1.call-start = ((), (), s32[]{:S(2)}) async-start(), calls=%async_computation.6 | async-start | bytes 2359296 | tf_op jit(solution)/shard_map/reduce_scatter | solution.py:56
  190.1 58.4 %all-gather.15.cloned.1.call-start = ((), (), s32[]{:S(2)}) async-start(), calls=%async_computation.7 | async-start | bytes 2359296 | tf_op jit(solution)/shard_map/all_gather | solution.py:52
  221.2 96.2 %reduce-scatter.9.cloned.1.call-start = ((), (), s32[]{:S(2)}) async-start(), calls=%async_computation.8 | async-start | bytes 2359296 | tf_op jit(solution)/shard_map/reduce_scatter | solution.py:56
  248.6 8.4 collective-permute-start
  290.9 58.0 %all-gather.17.cloned.1.call-start = ((), (), s32[]{:S(2)}) async-start(), calls=%async_computation.9 | async-start | bytes 2359296 | tf_op jit(solution)/shard_map/all_gather | solution.py:52
  321.5 77.2 %reduce-scatter.11.cloned.1.call-start = ((), (), s32[]{:S(2)}) async-start(), calls=%async_computation.10 | async-start | bytes 2359296 | tf_op jit(solution)/shard_map/reduce_scatter | solution.py:56
  372.4 78.1 %all-gather.19.cloned.1.call-start = ((), (), s32[]{:S(2)}) async-start(), calls=%async_computation.11 | async-start | bytes 5308416 | tf_op jit(solution)/shard_map/all_gather | solution.py:282
  373.1 101.7 %all-gather.21.cloned.1.call-start = ((), (), s32[]{:S(2)}) async-start(), calls=%async_computation.12 | async-start | bytes 1769472 | tf_op jit(solution)/shard_map/all_gather | solution.py:283
  373.9 165.0 %all-gather.23.cloned.1.call-start = ((), (), s32[]{:S(2)}) async-start(), calls=%async_computation.13 | async-start | bytes 7077888 | tf_op jit(solution)/shard_map/all_gather | solution.py:284
  374.5 228.6 %all-gather.25.cloned.1.call-start = ((), (), s32[]{:S(2)}) async-start(), calls=%async_computation.14 | async-start | bytes 7077888 | tf_op jit(solution)/shard_map/all_gather | solution.py:285
  375.2 273.6 %all-gather.27.cloned.1.call-start = ((), (), s32[]{:S(2)}) async-start(), calls=%async_computation.15 | async-start | bytes 2359296 | tf_op jit(solution)/shard_map/all_gather | solution.py:52
  477.2 131.8 %copy-start.53 = (f32[16,768]{1,0:T(8,128)}, f32[16,768]{1,0:T(8,128)S(1)}, u32[]{:S(2)}) copy-start(f32[16,768]{1,0:T(8,128)S(1)} %subtract_multiply_fusion.4) | copy-start | bytes 147460
  621.5 68.9 %reduce-scatter.13.cloned.1.call-start = ((), (), s32[]{:S(2)}) async-start(), calls=%async_computation.16 | async-start | bytes 2359296 | tf_op jit(solution)/shard_map/reduce_scatter | solution.py:56
  664.0 58.2 %all-gather.29.cloned.1.call-start = ((), (), s32[]{:S(2)}) async-start(), calls=%async_computation.17 | async-start | bytes 2359296 | tf_op jit(solution)/shard_map/all_gather | solution.py:52
  694.9 122.6 %reduce-scatter.15.cloned.1.call-start = ((), (), s32[]{:S(2)}) async-start(), calls=%async_computation.18 | async-start | bytes 2359296 | tf_op jit(solution)/shard_map/reduce_scatter | solution.py:56
  785.5 3.5 collective-permute-start.1
  791.2 58.2 %all-gather.31.cloned.1.call-start = ((), (), s32[]{:S(2)}) async-start(), calls=%async_computation.19 | async-start | bytes 2359296 | tf_op jit(solution)/shard_map/all_gather | solution.py:52
  822.1 124.0 %reduce-scatter.17.cloned.1.call-start = ((), (), s32[]{:S(2)}) async-start(), calls=%async_computation.20 | async-start | bytes 2359296 | tf_op jit(solution)/shard_map/reduce_scatter | solution.py:56
  917.8 332.7 %all-reduce.4.cloned.1.call-start = ((), (), s32[]{:S(2)}) async-start(), calls=%async_computation.24 | async-start | bytes 18874368 | tf_op jit(solution)/shard_map/psum | solution.py:365
  945.8 404.6 %all-gather.33.cloned.1.call-start = ((), (), s32[]{:S(2)}) async-start(), calls=%async_computation.21 | async-start | bytes 7077888 | tf_op jit(solution)/shard_map/all_gather | solution.py:361
  (127 other events, 989.5 us)
Sparse Core Ops, SparseCore 0:
  10.2 101.3 all-gather.34
  122.6 25.3 all-gather.36
  190.3 26.1 reduce-scatter.6
  221.3 27.1 all-gather.14
  291.0 26.2 reduce-scatter.8
  321.6 27.1 all-gather.16
  372.5 26.1 reduce-scatter.10
  400.2 50.2 all-gather.18
  452.0 22.7 all-gather.20
  476.2 62.6 all-gather.22
  540.5 62.6 all-gather.24
  621.6 27.1 all-gather.26
  664.2 26.1 reduce-scatter.12
  695.0 27.1 all-gather.28
  791.3 26.1 reduce-scatter.14
  822.2 27.1 all-gather.30
  918.0 26.1 reduce-scatter.16
  950.3 300.1 all-reduce.3
  1252.7 97.6 all-gather.32
where the time goes:
time: 1370 us
  waiting for transfers between devices  864 us (63%)
  matrix products  241 us (18%)
  other arithmetic  92.4 us (7%)
  blocking collectives  87.3 us (6%)
  local copies, waits for them, and re-layouts  63.2 us (5%)
  between operations  16.4 us (1%)
    dot_general x84, matrix products, product(): return jnp.einsum(form, left, right, preferred_element_type=jnp.float32)  241 us
    psum x1, waiting for transfers between devices, shards(): lax.psum(self_project_grad.astype(jnp.bfloat16), 'dp').astype(jnp.float32)  236 us
    all_gather x6, waiting for transfers between devices, token_rows(): return lax.all_gather(pieces, 'mp', axis=1, tiled=True)  161 us
    reduce_scatter x6, waiting for transfers between devices, token_sums(): lax.psum_scatter(terms.astype(jnp.bfloat16), 'mp', scatter_dimension=1, t...  127 us
    all_gather x1, waiting for transfers between devices, shards(): piece = lax.all_gather(local_tokens, 'dp', axis=0, tiled=True)  101 us
    all_gather x1, waiting for transfers between devices, shards(): lax.all_gather(sent_rows, 'dp', axis=0, tiled=True)  84.9 us
    all_gather x1, waiting for transfers between devices, shards(): lax.all_gather(summary_up, 'mp', axis=1, tiled=True)  61.8 us
    all_gather x1, waiting for transfers between devices, shards(): lax.all_gather(summary_down, 'mp', axis=0, tiled=True)  61.1 us
  transfers between devices with their start and end apart: 21, of which 19 were waited for; matrix products, arithmetic and copies ran while one was open for 6% of the time, Pallas kernels for 0%

commit v1 on v0

v1 whole, which is shorter than its diff:
```python
import functools

import jax
import jax.numpy as jnp
from jax import lax
from jax.experimental import pallas as pl
from jax.experimental.pallas import tpu as pltpu
from jax.sharding import PartitionSpec as P

D = 768
HEAD = 64
MESH = pl.DeviceIdType.MESH


EPS = 1e-05
NEG = -1000000000.0


def shifted(value, axis, steps):
    count = lax.axis_size(axis)
    pairs = [(source, (source + steps) % count) for source in range(count)]
    return lax.ppermute(value, axis, pairs)


def layer_norm(rows, gain):
    center = rows - jnp.mean(rows, -1, keepdims=True)
    inverse = lax.rsqrt(jnp.mean(center * center, -1, keepdims=True) + EPS)
    unit = center * inverse
    return (unit * gain, unit, inverse)


def layer_norm_back(grad_out, unit, inverse, gain):
    gain_grad = jnp.sum(grad_out * unit, axis=tuple(range(grad_out.ndim - 1)))
    scaled = grad_out * gain
    centered = scaled - jnp.mean(scaled, -1, keepdims=True)
    return (inverse * (centered - unit * jnp.mean(scaled * unit, -1, keepdims=True)), gain_grad)


def gelu_exact(values):
    return jax.nn.gelu(values, approximate=False)


def product(left, right, form):
    return jnp.einsum(form, left, right, preferred_element_type=jnp.float32)


def split_heads(rows):
    return rows.reshape(rows.shape[:-1] + (rows.shape[-1] // HEAD, HEAD))


def merge_heads(rows):
    return rows.reshape(rows.shape[:-2] + (rows.shape[-2] * rows.shape[-1],))


def peer_of(axes, index):
    place = {}
    for axis in reversed(axes):
        count = lax.axis_size(axis)
        place[axis] = index % count
        index = index // count
    return place


def flat_index(axes):
    index = 0
    for axis in axes:
        index = index * lax.axis_size(axis) + lax.axis_index(axis)
    return index


def trade_kernel(axes, total, split, source, target, send_sem, recv_sem, own_sem):
    me = flat_index(axes)
    barrier = pltpu.get_barrier_semaphore()
    for step in range(1, total):
        peer = peer_of(axes, (me + step) % total)
        pl.semaphore_signal(barrier, inc=1, device_id=peer, device_id_type=MESH)
    pl.semaphore_wait(barrier, total - 1)

    def piece(index):
        return source.at[index] if split else source

    own = pltpu.make_async_copy(piece(me), target.at[me], own_sem)
    own.start()
    copies = []
    for step in range(1, total):
        to = (me + step) % total
        copies.append(
            pltpu.make_async_remote_copy(
                src_ref=piece(to),
                dst_ref=target.at[me],
                send_sem=send_sem.at[step],
                recv_sem=recv_sem.at[step],
                device_id=peer_of(axes, to),
                device_id_type=MESH,
            )
        )
        copies[-1].start()
    own.wait()
    for copy in copies:
        copy.wait()


def trade(value, axes, split, collective_id):
    total = 1
    for axis in axes:
        total *= lax.axis_size(axis)
    piece = value.shape[1:] if split else value.shape
    return pl.pallas_call(
        functools.partial(trade_kernel, axes, total, split),
        out_shape=jax.ShapeDtypeStruct((total,) + piece, value.dtype),
        in_specs=[pl.BlockSpec(memory_space=pltpu.VMEM)],
        out_specs=pl.BlockSpec(memory_space=pltpu.VMEM),
        scratch_shapes=[
            pltpu.SemaphoreType.DMA((total,)),
            pltpu.SemaphoreType.DMA((total,)),
            pltpu.SemaphoreType.DMA,
        ],
        compiler_params=pltpu.CompilerParams(collective_id=collective_id, has_side_effects=True),
    )(value)


def clip_rows(rows, wanted, collective_id):
    count = lax.axis_size("dp")
    clips, length, width = rows.shape
    pieces = jnp.swapaxes(rows.reshape(clips, count, length // count, width), 0, 1)
    held = trade(pieces, ("dp",), True, collective_id)
    held = held.reshape(count * clips, length // count, width)
    picked = jnp.concatenate(
        [lax.dynamic_slice_in_dim(held, wanted[clip], 1) for clip in range(count * clips)]
    )
    back = trade(picked.reshape(pieces.shape), ("dp",), True, collective_id + 1)
    return jnp.swapaxes(back, 0, 1).reshape(rows.shape)


def row_blocks(piece):
    count = lax.axis_size("mp")
    return [piece] + [shifted(piece, "mp", -step) for step in range(1, count)]


def own_sum(parts):
    total = parts[0]
    for step in range(1, len(parts)):
        total = total + shifted(parts[step].astype(jnp.bfloat16), "mp", step).astype(jnp.float32)
    return total


def whole_sum(value):
    parts = jnp.stack(row_blocks(value))
    if parts.shape[0] > 2:
        parts = jnp.roll(parts, lax.axis_index("mp"), 0)
    return jnp.sum(parts, 0)


def far_first(count):
    return list(range(1, count)) + [0]


def attend_block(query_block, key_rows, value_rows, valid):
    scores = jnp.where(valid, product(query_block, key_rows, "cqhe,ckhe->chqk"), NEG)
    highest = jnp.max(scores, -1, keepdims=True)
    raised = jnp.exp(scores - highest)
    totals = jnp.sum(raised, -1, keepdims=True)
    weights = (raised / totals).astype(jnp.bfloat16)
    result = product(weights, value_rows, "chqk,ckhe->cqhe").astype(jnp.bfloat16)
    return (result, highest + jnp.log(totals))


def attend_block_back(query_block, key_rows, value_rows, valid, grad_block, log_sums):
    scores = jnp.where(valid, product(query_block, key_rows, "cqhe,ckhe->chqk"), NEG)
    weights = jnp.exp(scores - log_sums)
    grad_weights = product(grad_block, value_rows, "cqhe,ckhe->chqk")
    grad_scores = (
        weights * (grad_weights - jnp.sum(weights * grad_weights, -1, keepdims=True))
    ).astype(jnp.bfloat16)
    query_grad = product(grad_scores, key_rows, "chqk,ckhe->cqhe").astype(jnp.bfloat16)
    key_grad = product(grad_scores, query_block, "chqk,cqhe->ckhe")
    value_grad = product(weights.astype(jnp.bfloat16), grad_block, "chqk,cqhe->ckhe")
    return (query_grad, key_grad, value_grad)


def attend(queries, keys, values, valid):
    key_rows = split_heads(jnp.concatenate(keys, 1))
    value_rows = split_heads(jnp.concatenate(values, 1))
    heads = [None] * len(queries)
    sums = [None] * len(queries)
    for j in far_first(len(queries)):
        result, sums[j] = attend_block(split_heads(queries[j]), key_rows, value_rows, valid)
        heads[j] = merge_heads(result)
    return (heads, sums)


def attend_back(queries, keys, values, valid, grads, sums):
    key_rows = split_heads(jnp.concatenate(keys, 1))
    value_rows = split_heads(jnp.concatenate(values, 1))
    query_grads = [None] * len(queries)
    key_grad = value_grad = 0.0
    for j in far_first(len(queries)):
        query_grad, key_term, value_term = attend_block_back(
            split_heads(queries[j]), key_rows, value_rows, valid, split_heads(grads[j]), sums[j]
        )
        query_grads[j] = merge_heads(query_grad)
        key_grad = key_grad + key_term
        value_grad = value_grad + value_term
    parts = len(keys)
    return (
        query_grads,
        jnp.split(merge_heads(key_grad.astype(jnp.bfloat16)), parts, 1),
        jnp.split(merge_heads(value_grad.astype(jnp.bfloat16)), parts, 1),
    )


def project_rows(source, weight):
    return product(source, weight, "csd,de->cse")


def query_rows(source, weight):
    return (project_rows(source, weight) * HEAD ** (-0.5)).astype(jnp.bfloat16)


def back_rows(grad, weight):
    return product(grad, weight, "cse,de->csd")


def weight_sums(sources, grads):
    return sum(product(source, grad, "csd,cse->de") for source, grad in zip(sources, grads))


def scaled_grads(grads):
    return [grad * HEAD ** (-0.5) for grad in grads]


def summary_layer(
    summary_rows, top_grad, weights, gain_top, gain_last, summary_valid
):
    use_project, use_merge, use_up, use_down = weights
    top_normed, top_unit, top_inverse = layer_norm(summary_rows, gain_top)
    top_low = top_normed.astype(jnp.bfloat16)[None]
    top_query = query_rows(top_low, use_project[0])
    top_key = project_rows(top_low, use_project[1]).astype(jnp.bfloat16)
    top_value = project_rows(top_low, use_project[2]).astype(jnp.bfloat16)
    (top_flat,), top_sums = attend([top_query], [top_key], [top_value], summary_valid)
    summary_mid = summary_rows + whole_sum(product(top_flat, use_merge, "cse,ed->csd")[0])
    mid_normed, mid_unit, mid_inverse = layer_norm(summary_mid, gain_last)
    mid_low = mid_normed.astype(jnp.bfloat16)[None]
    top_before = product(mid_low, use_up, "csd,df->csf")
    top_hidden = gelu_exact(top_before).astype(jnp.bfloat16)
    summary_final = summary_mid + whole_sum(product(top_hidden, use_down, "csf,fd->csd")[0])
    down_input = top_grad.astype(jnp.bfloat16)[None]
    down_grad = product(top_hidden, down_input, "csf,csd->fd")
    act_grad = jax.vjp(gelu_exact, top_before)[1](product(down_input, use_down, "csd,fd->csf"))[
        0
    ].astype(jnp.bfloat16)
    up_grad = product(mid_low, act_grad, "csd,csf->df")
    mid_rows_grad, last_gain_grad = layer_norm_back(
        whole_sum(product(act_grad, use_up, "csf,df->csd")[0]), mid_unit, mid_inverse, gain_last
    )
    mid_grad = top_grad + mid_rows_grad
    merge_input = mid_grad.astype(jnp.bfloat16)[None]
    merge_grad = product(top_flat, merge_input, "cse,csd->ed")
    top_heads_grad = product(merge_input, use_merge, "csd,ed->cse").astype(jnp.bfloat16)
    (query_grad,), (key_grad,), (value_grad,) = attend_back(
        [top_query], [top_key], [top_value], summary_valid, [top_heads_grad], top_sums
    )
    query_grad = query_grad * HEAD ** (-0.5)
    project_grad = jnp.stack(
        [product(top_low, grad, "csd,cse->de") for grad in (query_grad, key_grad, value_grad)]
    )
    project_terms = (
        back_rows(query_grad, use_project[0])
        + back_rows(key_grad, use_project[1])
        + back_rows(value_grad, use_project[2])
    )
    first_top_grad, top_gain_grad = layer_norm_back(
        whole_sum(project_terms[0]), top_unit, top_inverse, gain_top
    )
    class_grad = mid_grad + first_top_grad
    return (
        summary_final,
        class_grad,
        (project_grad, merge_grad, up_grad, down_grad),
        top_gain_grad,
        last_gain_grad,
    )


def shards(
    tokens,
    partner,
    mix_weight,
    video_ids,
    view_counts,
    self_project,
    self_merge,
    cross_project,
    cross_merge,
    hidden_up,
    hidden_down,
    norm_self,
    norm_cross,
    norm_hidden,
    summary_project,
    summary_merge,
    summary_up,
    summary_down,
    summary_norm_self,
    summary_norm_hidden,
    tokens_cotangent,
    summary_cotangent,
):
    local_tokens = tokens[:, 0]
    clip_count = local_tokens.shape[0]
    data_index = lax.axis_index("dp")
    view_index = lax.axis_index("view")
    model_index = lax.axis_index("mp")
    view_total = lax.axis_size("view")
    model_total = lax.axis_size("mp")
    clip_total = clip_count * lax.axis_size("dp")
    length = local_tokens.shape[1]
    order = far_first(model_total)
    own_clips = data_index * clip_count + jnp.arange(clip_count, dtype=jnp.int32)
    partner_tokens = clip_rows(local_tokens, partner, 0).astype(jnp.float32)
    grad_blocks = row_blocks(tokens_cotangent[:, 0])
    mixing = mix_weight[:, None, None]
    mixed_rows = mixing * local_tokens.astype(jnp.float32) + (1.0 - mixing) * partner_tokens
    owners = [(model_index + step) % model_total for step in range(model_total)]
    positions = jnp.concatenate([owner * length + jnp.arange(length) for owner in owners])
    own_valid = (positions < view_counts[view_index])[None, None, None, :]
    next_valid = (positions < view_counts[(view_index + 1) % view_total])[None, None, None, :]

    normed_self, unit_self, inverse_self = layer_norm(mixed_rows, norm_self[0])
    self_blocks = row_blocks(normed_self.astype(jnp.bfloat16))
    self_weights = self_project[0]
    self_queries = [query_rows(block, self_weights[0]) for block in self_blocks]
    self_keys = [project_rows(block, self_weights[1]).astype(jnp.bfloat16) for block in self_blocks]
    self_values = [
        project_rows(block, self_weights[2]).astype(jnp.bfloat16) for block in self_blocks
    ]
    self_heads, self_sums = attend(self_queries, self_keys, self_values, own_valid)
    first_rows = mixed_rows + own_sum(
        [product(heads, self_merge[0], "cse,ed->csd") for heads in self_heads]
    )

    normed_cross, unit_cross, inverse_cross = layer_norm(first_rows, norm_cross[0])
    cross_blocks = row_blocks(normed_cross.astype(jnp.bfloat16))
    next_blocks = [shifted(block, "view", -1) for block in cross_blocks]
    cross_weights = cross_project[0]
    cross_queries = [query_rows(block, cross_weights[0]) for block in cross_blocks]
    cross_keys = [
        project_rows(block, cross_weights[1]).astype(jnp.bfloat16) for block in next_blocks
    ]
    cross_values = [
        project_rows(block, cross_weights[2]).astype(jnp.bfloat16) for block in next_blocks
    ]
    cross_heads, cross_sums = attend(cross_queries, cross_keys, cross_values, next_valid)
    second_rows = first_rows + own_sum(
        [product(heads, cross_merge[0], "cse,ed->csd") for heads in cross_heads]
    )

    normed_hidden, unit_hidden, inverse_hidden = layer_norm(second_rows, norm_hidden[0])
    hidden_blocks = row_blocks(normed_hidden.astype(jnp.bfloat16))
    befores = [product(block, hidden_up[0], "csd,df->csf") for block in hidden_blocks]
    hiddens = [gelu_exact(before).astype(jnp.bfloat16) for before in befores]
    third_rows = second_rows + own_sum(
        [product(hidden, hidden_down[0], "csf,fd->csd") for hidden in hiddens]
    )

    everyone = ("dp", "view", "mp")
    class_all = trade(third_rows[:, 0, :], everyone, False, 2)
    class_all = class_all.reshape(clip_total // clip_count, view_total, model_total, clip_count, D)
    class_grid = jnp.swapaxes(class_all[:, :, 0], 1, 2).reshape(clip_total, view_total, D)
    row_total = clip_total * view_total
    token_video = jnp.repeat(video_ids, view_total)
    summary_valid = (token_video[:, None] == token_video[None, :])[None, None]
    summary_final, class_flat, summary_grads, summary_norm_self_grad, summary_norm_hidden_grad = (
        summary_layer(
            class_grid.reshape(row_total, D),
            summary_cotangent.reshape(row_total, D),
            (summary_project, summary_merge, summary_up, summary_down),
            summary_norm_self,
            summary_norm_hidden,
            summary_valid,
        )
    )
    summary_project_grad, summary_merge_grad, summary_up_grad, summary_down_grad = summary_grads
    summary_out = summary_final.reshape(clip_total, view_total, D)
    clip_match = (jnp.arange(clip_total, dtype=jnp.int32)[:, None] == own_clips[None, :]).astype(
        jnp.float32
    )
    view_match = (jnp.arange(view_total) == view_index).astype(jnp.float32)
    class_grad = class_flat.reshape(clip_total, view_total, D)
    view_pick = jnp.sum(class_grad * view_match[None, :, None], axis=1)
    own_class = jnp.sum(clip_match[:, :, None] * view_pick[:, None, :], axis=0)

    third_grads = [
        block.astype(jnp.float32).at[:, 0].add(own_class * (owner == 0).astype(jnp.float32))
        for block, owner in zip(grad_blocks, owners)
    ]
    third_grad = third_grads[0]
    down_rows = [block.astype(jnp.bfloat16) for block in third_grads]
    act_grads = [
        jax.vjp(gelu_exact, before)[1](product(rows, hidden_down[0], "csd,fd->csf"))[0].astype(
            jnp.bfloat16
        )
        for before, rows in zip(befores, down_rows)
    ]
    hidden_norm_grad = own_sum(
        [product(act_grad, hidden_up[0], "csf,df->csd") for act_grad in act_grads]
    )
    down_grad = sum(product(h, r, "csf,csd->fd") for h, r in zip(hiddens, down_rows))
    up_grad = sum(product(b, g, "csd,csf->df") for b, g in zip(hidden_blocks, act_grads))
    up_sum, down_sum = lax.psum(
        (up_grad.astype(jnp.bfloat16), down_grad.astype(jnp.bfloat16)), "dp"
    )
    rows_grad_hidden, gain_hidden_grad = layer_norm_back(
        hidden_norm_grad, unit_hidden, inverse_hidden, norm_hidden[0]
    )
    second_grad = third_grad + rows_grad_hidden

    merge_blocks = row_blocks(second_grad.astype(jnp.bfloat16))
    heads_grads = [
        product(block, cross_merge[0], "csd,ed->cse").astype(jnp.bfloat16)
        for block in merge_blocks
    ]
    query_grads, key_grads, value_grads = attend_back(
        cross_queries, cross_keys, cross_values, next_valid, heads_grads, cross_sums
    )
    query_grads = scaled_grads(query_grads)
    terms = [None] * model_total
    for step in order:
        next_term = back_rows(key_grads[step], cross_weights[1]) + back_rows(
            value_grads[step], cross_weights[2]
        )
        returned = shifted(next_term.astype(jnp.bfloat16), "view", 1).astype(jnp.float32)
        terms[step] = back_rows(query_grads[step], cross_weights[0]) + returned
    cross_norm_grad = own_sum(terms)
    cross_merge_grad = weight_sums(cross_heads, merge_blocks)
    cross_project_grad = jnp.stack(
        [
            weight_sums(cross_blocks, query_grads),
            weight_sums(next_blocks, key_grads),
            weight_sums(next_blocks, value_grads),
        ]
    )
    cross_low = (cross_project_grad.astype(jnp.bfloat16), cross_merge_grad.astype(jnp.bfloat16))
    cross_low, (up_sum, down_sum) = lax.optimization_barrier((cross_low, (up_sum, down_sum)))
    cross_project_sum, cross_merge_sum = lax.psum(cross_low, "dp")
    rows_grad_cross, gain_cross_grad = layer_norm_back(
        cross_norm_grad, unit_cross, inverse_cross, norm_cross[0]
    )
    first_grad = second_grad + rows_grad_cross

    merge_blocks = row_blocks(first_grad.astype(jnp.bfloat16))
    heads_grads = [
        product(block, self_merge[0], "csd,ed->cse").astype(jnp.bfloat16) for block in merge_blocks
    ]
    query_grads, key_grads, value_grads = attend_back(
        self_queries, self_keys, self_values, own_valid, heads_grads, self_sums
    )
    query_grads = scaled_grads(query_grads)
    self_norm_grad = own_sum(
        [
            back_rows(query_grads[step], self_weights[0])
            + back_rows(key_grads[step], self_weights[1])
            + back_rows(value_grads[step], self_weights[2])
            for step in range(model_total)
        ]
    )
    self_merge_grad = weight_sums(self_heads, merge_blocks)
    self_project_grad = jnp.stack(
        [
            weight_sums(self_blocks, query_grads),
            weight_sums(self_blocks, key_grads),
            weight_sums(self_blocks, value_grads),
        ]
    )
    self_low = (self_project_grad.astype(jnp.bfloat16), self_merge_grad.astype(jnp.bfloat16))
    self_low, (cross_project_sum, cross_merge_sum) = lax.optimization_barrier(
        (self_low, (cross_project_sum, cross_merge_sum))
    )
    self_project_sum, self_merge_sum = lax.psum(self_low, "dp")
    rows_grad_self, gain_self_grad = layer_norm_back(
        self_norm_grad, unit_self, inverse_self, norm_self[0]
    )
    mixed_grad = first_grad + rows_grad_self
    gains = jnp.stack([gain_self_grad, gain_cross_grad, gain_hidden_grad])
    gains = jnp.sum(trade(gains, ("dp", "mp"), False, 3), 0)

    sent_rows = ((1.0 - mixing) * mixed_grad).astype(jnp.bfloat16)
    clips = jnp.arange(clip_total, dtype=jnp.int32)
    inverse_partner = jnp.sum(
        jnp.where(partner[None, :] == clips[:, None], clips[None, :], 0), 1
    )
    returned_rows = clip_rows(sent_rows, inverse_partner, 4).astype(jnp.float32)
    tokens_grad = (mixing * mixed_grad + returned_rows)[:, None]
    tokens_out = third_rows.astype(jnp.bfloat16)[:, None]
    return (
        tokens_out,
        summary_out,
        tokens_grad,
        self_project_sum.astype(jnp.float32)[None],
        self_merge_sum.astype(jnp.float32)[None],
        cross_project_sum.astype(jnp.float32)[None],
        cross_merge_sum.astype(jnp.float32)[None],
        up_sum.astype(jnp.float32)[None],
        down_sum.astype(jnp.float32)[None],
        gains[0][None],
        gains[1][None],
        gains[2][None],
        summary_project_grad,
        summary_merge_grad,
        summary_up_grad,
        summary_down_grad,
        summary_norm_self_grad,
        summary_norm_hidden_grad,
    )


def solution(mesh):
    in_specs = (
        P("dp", "view", "mp", None),
        P(),
        P("dp"),
        P(),
        P(),
        P("view", None, None, "mp"),
        P("view", "mp", None),
        P("view", None, None, "mp"),
        P("view", "mp", None),
        P("view", None, "mp"),
        P("view", "mp", None),
        P("view", None),
        P("view", None),
        P("view", None),
        P(None, None, "mp"),
        P("mp", None),
        P(None, "mp"),
        P("mp", None),
        P(),
        P(),
        P("dp", "view", "mp", None),
        P(),
    )
    out_specs = (
        P("dp", "view", "mp", None),
        P(),
        P("dp", "view", "mp", None),
        P("view", None, None, "mp"),
        P("view", "mp", None),
        P("view", None, None, "mp"),
        P("view", "mp", None),
        P("view", None, "mp"),
        P("view", "mp", None),
        P("view", None),
        P("view", None),
        P("view", None),
        P(None, None, "mp"),
        P("mp", None),
        P(None, "mp"),
        P("mp", None),
        P(),
        P(),
    )
    return jax.shard_map(shards, mesh=mesh, in_specs=in_specs, out_specs=out_specs, check_vma=False)
```

time: 1370 us -> 854 us (0.62)
  waiting for transfers between devices: 864 us -> 225 us
  Pallas kernels: 0 us -> 136 us
  blocking collectives: 87.3 us -> 0 us
  between operations: 16.4 us -> 48.2 us
  local copies, waits for them, and re-layouts: 63.2 us -> 45.4 us
  starting transfers between devices: 1.62 us -> 19.3 us
  other arithmetic: 92.4 us -> 110 us
  matrix products: 241 us -> 258 us
    all_gather x12 -> x0, waiting for transfers between devices: 496 us -> none  [the longest x6 161 us: token_rows(): return lax.all_gather(pieces, 'mp', axis=1, tiled=True)]
    pallas_call x0 -> x6, Pallas kernels: none -> 136 us  [trade(): pl.pallas_call(functools.partial(trade_kernel, axes, total, split), out_s...]
    reduce_scatter x6 -> x0, waiting for transfers between devices: 127 us -> none  [token_sums(): lax.psum_scatter(terms.astype(jnp.bfloat16), 'mp', scatter_dimension=1, t...]
    psum x1 -> x3, waiting for transfers between devices: 236 us -> 130 us  [the longest x1 94.3 us: shards(): cross_project_sum, cross_merge_sum = lax.psum(cross_low, 'dp')]
    ppermute x2 -> x20, waiting for transfers between devices: 2.35 us -> 95.1 us  [shifted(): return lax.ppermute(value, axis, pairs)]
    psum x2 -> x0, blocking collectives: 87.3 us -> none  [the longest x1 46.2 us: shards(): lax.psum((gain_self_grad, gain_cross_grad, gain_hidden_grad), ('dp', 'mp'))]
    ppermute x2 -> x20, starting transfers between devices: 0.07 us -> 19.2 us  [shifted(): return lax.ppermute(value, axis, pairs)]
    convert_element_type x17 -> x12, other arithmetic: 34 us -> 52.1 us  [the longest x3 39.8 us: attend_block_back(): grad_scores = (weights * (grad_weights - jnp.sum(weights * grad_weights,...]
  transfers between devices with their start and end apart: 21 -> 23, of which waited for: 19 -> 12; matrix products, arithmetic and copies ran while one was open for 6% -> 40% of each run, Pallas kernels for 0% -> 9%
where the time goes in v1:
time: 854 us; the launch traced here: 842 us
  matrix products  258 us (30%)
  waiting for transfers between devices  225 us (26%)
  Pallas kernels  136 us (16%)
  other arithmetic  110 us (13%)
  between operations  48.2 us (6%)
  local copies, waits for them, and re-layouts  45.4 us (5%)
  starting transfers between devices  19.3 us (2%)
    dot_general x108, matrix products, product(): return jnp.einsum(form, left, right, preferred_element_type=jnp.float32)  258 us
    pallas_call x6, Pallas kernels, trade(): pl.pallas_call(functools.partial(trade_kernel, axes, total, split), out_s...  136 us
    ppermute x20, waiting for transfers between devices, shifted(): return lax.ppermute(value, axis, pairs)  95.1 us
    psum x1, waiting for transfers between devices, shards(): cross_project_sum, cross_merge_sum = lax.psum(cross_low, 'dp')  94.3 us
    convert_element_type x3, other arithmetic, attend_block_back(): grad_scores = (weights * (grad_weights - jnp.sum(weights * grad_weights,...  39.8 us
    psum x1, waiting for transfers between devices, shards(): self_project_sum, self_merge_sum = lax.psum(self_low, 'dp')  35.4 us
    unnamed x362, local copies, waits for them, and re-layouts  24.8 us
    ppermute x20, starting transfers between devices, shifted(): return lax.ppermute(value, axis, pairs)  19.2 us
  transfers between devices with their start and end apart: 23, of which 12 were waited for; matrix products, arithmetic and copies ran while one was open for 40% of the time, Pallas kernels for 9%

profile of v1, /device:TPU:0, one launch (start us, length us, event | category | flops | bytes accessed | tf_op | source)
XLA Modules:
  0.0 841.9 jit_solution(9174840271186507981)
XLA Ops:
  19.2 20.9 %shard_map.349 = bf16[8,1,64,768]{3,2,1,0:T(8,128)(2,1)} custom-call(bf16[8,1,64,768]{3,2,1,0:T(8,128)(2,1)} %bitcast.665), custom_call_target="tpu_custom_call" | custom-call | tf_op jit(solution)/shard_map/pallas_call | solution.py:108
  56.1 22.6 %shard_map.350 = bf16[8,1,64,768]{3,2,1,0:T(8,128)(2,1)} custom-call(bf16[8,1,64,768]{3,2,1,0:T(8,128)(2,1)} %bitcast.735), custom_call_target="tpu_custom_call" | custom-call | tf_op jit(solution)/shard_map/pallas_call | solution.py:108
  94.5 11.4 %collective-permute-done = bf16[1,512,768]{2,1,0:T(8,128)(2,1)S(1)} collective-permute-done((bf16[1,512,768]{2,1,0:T(8,128)(2,1)}, bf16[1,512,768]{2,1,0:T(8,128)(2,1)S(1)}, u32[]{:S(2)}, u32[]{:S(2)}) %collective-permute-start) | collective-permute-done | bytes 786464 | tf_op jit(solution)/shard_map/ppermute | solution.py:22
  108.9 7.8 fusion
  135.7 10.3 %collective-permute-done.1 = bf16[1,512,768]{2,1,0:T(8,128)(2,1)S(1)} collective-permute-done((bf16[1,512,768]{2,1,0:T(8,128)(2,1)S(1)}, bf16[1,512,768]{2,1,0:T(8,128)(2,1)S(1)}, u32[]{:S(2)}, u32[]{:S(2)}) %collective-permute-start.1) | collective-permute-done | bytes 786464 | tf_op jit(solution)/shard_map/ppermute | solution.py:22
  177.6 8.1 fusion.2
  203.3 15.7 %collective-permute-done.5 = bf16[1,512,768]{2,1,0:T(8,128)(2,1)S(1)} collective-permute-done((bf16[1,512,768]{2,1,0:T(8,128)(2,1)S(1)}, bf16[1,512,768]{2,1,0:T(8,128)(2,1)S(1)}, u32[]{:S(2)}, u32[]{:S(2)}) %collective-permute-start.5) | collective-permute-done | bytes 786464 | tf_op jit(solution)/shard_map/ppermute | solution.py:22
  225.2 13.9 %collective-permute-done.6 = bf16[1,512,768]{2,1,0:T(8,128)(2,1)S(1)} collective-permute-done((bf16[1,512,768]{2,1,0:T(8,128)(2,1)S(1)}, bf16[1,512,768]{2,1,0:T(8,128)(2,1)S(1)}, u32[]{:S(2)}, u32[]{:S(2)}) %collective-permute-start.6) | collective-permute-done | bytes 786464 | tf_op jit(solution)/shard_map/ppermute | solution.py:22
  239.1 9.6 %multiply_convert_fusion.4 = (bf16[512,1536]{1,0:T(8,128)(2,1)S(1)}, f32[512,1536]{1,0:T(8,128)}, f32[512,1536]{1,0:T(8,128)}) fusion(bf16[1,768,1536]{2,1,0:T(8,128)(2,1)S(1)} %copy-done, bf16[1,512,768]{2,1,0:T(8,128)(2,1)S(1)} %collective-permute-done.6), kind=kOutput, calls=%fused_computation.61 | convolution fusion | flops 1259077632 | bytes 11010048 | tf_op jit(solution)/shard_map/csd,df->csf/dot_general | solution.py:44
  250.6 9.7 %multiply_convert_fusion.5 = (bf16[512,1536]{1,0:T(8,128)(2,1)S(1)}, f32[512,1536]{1,0:T(8,128)}, f32[512,1536]{1,0:T(8,128)}) fusion(bf16[1,768,1536]{2,1,0:T(8,128)(2,1)S(1)} %copy-done, bf16[1,512,768]{2,1,0:T(8,128)(2,1)S(1)} %multiply_convert_fusion.7), kind=kOutput, calls=%fused_computation.74 | convolution fusion | flops 1259077632 | bytes 11010048 | tf_op jit(solution)/shard_map/csd,df->csf/dot_general | solution.py:44
  260.4 7.6 collective-permute-done.7
  270.9 17.1 %shard_map.351 = f32[32,1,768]{2,1,0:T(1,128)} custom-call(f32[1,768]{1,0:T(1,128)} %slice_bitcast_fusion.24.source), custom_call_target="tpu_custom_call" | custom-call | tf_op jit(solution)/shard_map/pallas_call | solution.py:108
  392.0 7.8 collective-permute-done.14
  404.1 19.3 %multiply_reduce_fusion.2 = (f32[6,512]{1,0:T(8,128)S(1)}, f32[6,512]{1,0:T(8,128)S(1)}, f32[6,512,1024]{2,1,0:T(8,128)}) fusion(f32[6,512,1024]{2,1,0:T(8,128)} %get-tuple-element.143, f32[6,512]{1,0:T(8,128)S(1)} %copy-done.109, pred[1024]{0:T(1024)(128)(4,1)S(1)} %copy-done.125, f32[6,512,1024]{2,1,0:T(8,128)} %fusion.224, ...), kind=kOutput, calls=%fused_computation.7 | convolution fusion | flops 429385728 | bytes 51561472 | tf_op jit(solution)/shard_map/cqhe,ckhe->chqk/dot_general | solution.py:44
  423.4 17.5 %multiply_convert_fusion.3 = (bf16[6,512,1024]{2,1,0:T(8,128)(2,1)S(1)}, bf16[6,512,1024]{2,1,0:T(8,128)(2,1)S(1)}) fusion(f32[6,512,1024]{2,1,0:T(8,128)} %fusion.224, f32[6,512,1024]{2,1,0:T(8,128)} %copy-done.3, f32[6,512]{1,0:T(8,128)S(1)} %get-tuple-element.76, f32[6,512]{1,0:T(8,128)S(1)} %log_add_fusion.3, pred[1024]{0:T(1024)(128)(4,1)S(1)} %copy-done.125, ...), kind=kLoop, calls=%fused_computation.9 | loop fusion | flops 31457280 | bytes 62964736 | tf_op jit(solution)/shard_map/convert_element_type | solution.py:174
  468.7 13.5 %collective-permute-done.17 = bf16[1,512,768]{2,1,0:T(8,128)(2,1)S(1)} collective-permute-done((bf16[1,512,768]{2,1,0:T(8,128)(2,1)S(1)}, bf16[1,512,768]{2,1,0:T(8,128)(2,1)S(1)}, u32[]{:S(2)}, u32[]{:S(2)}) %collective-permute-start.17) | collective-permute-done | bytes 786464 | tf_op jit(solution)/shard_map/ppermute | solution.py:22
  491.6 12.3 %collective-permute-done.18 = bf16[1,512,768]{2,1,0:T(8,128)(2,1)} collective-permute-done((bf16[1,512,768]{2,1,0:T(8,128)(2,1)S(1)}, bf16[1,512,768]{2,1,0:T(8,128)(2,1)}, u32[]{:S(2)}, u32[]{:S(2)}) %collective-permute-start.18) | collective-permute-done | bytes 786464 | tf_op jit(solution)/shard_map/ppermute | solution.py:22
  511.9 18.9 %multiply_reduce_fusion.1 = (f32[6,512]{1,0:T(8,128)S(1)}, f32[6,512]{1,0:T(8,128)S(1)}, f32[6,512,1024]{2,1,0:T(8,128)}) fusion(f32[6,512,1024]{2,1,0:T(8,128)} %copy-done.2, f32[6,512]{1,0:T(8,128)S(1)} %copy-done.106, pred[1024]{0:T(1024)(128)(4,1)S(1)} %copy-done.122, f32[6,512,1024]{2,1,0:T(8,128)} %fusion.221, f32[6,512]{1,0:T(8,128)S(1)} %copy-done.107, ...), kind=kOutput, calls=%fused_computation.4 | convolution fusion | flops 429385728 | bytes 51561472 | tf_op jit(solution)/shard_map/cqhe,ckhe->chqk/dot_general | solution.py:44
  530.9 22.2 %multiply_convert_fusion.1 = (bf16[6,512,1024]{2,1,0:T(8,128)(2,1)}, bf16[6,512,1024]{2,1,0:T(8,128)(2,1)}) fusion(f32[6,512,1024]{2,1,0:T(8,128)} %get-tuple-element.154, f32[6,512,1024]{2,1,0:T(8,128)} %copy-done.2, f32[6,512]{1,0:T(8,128)S(1)} %get-tuple-element.73, f32[6,512]{1,0:T(8,128)S(1)} %copy-done.106, pred[1024]{0:T(1024)(128)(4,1)S(1)} %copy-done.122, ...), kind=kLoop, calls=%fused_computation.3 | loop fusion | flops 31457280 | bytes 62964736 | tf_op jit(solution)/shard_map/convert_element_type | solution.py:174
  605.7 94.3 %all-reduce.9.cloned.1.call-done = (bf16[3,768,384]{2,1,0:T(8,128)(2,1)}, bf16[384,768]{1,0:T(8,128)(2,1)}) async-done(((bf16[3,768,384]{2,1,0:T(8,128)(2,1)}, bf16[384,768]{1,0:T(8,128)(2,1)}), (bf16[3,768,384]{2,1,0:T(8,128)(2,1)}, bf16[384,768]{1,0:T(8,128)(2,1)})) %all-reduce.9.cloned.1.call-update) | async-done | bytes 2359312 | tf_op jit(solution)/shard_map/psum | solution.py:446
  703.8 30.2 %shard_map.352 = bf16[8,1,64,768]{3,2,1,0:T(8,128)(2,1)} custom-call(bf16[8,1,64,768]{3,2,1,0:T(8,128)(2,1)} %bitcast.693), custom_call_target="tpu_custom_call" | custom-call | tf_op jit(solution)/shard_map/pallas_call | solution.py:108
  742.2 29.0 %shard_map.353 = bf16[8,1,64,768]{3,2,1,0:T(8,128)(2,1)} custom-call(bf16[8,1,64,768]{3,2,1,0:T(8,128)(2,1)} %bitcast.736), custom_call_target="tpu_custom_call" | custom-call | tf_op jit(solution)/shard_map/pallas_call | solution.py:108
  771.9 15.9 %shard_map.354 = f32[16,3,768]{2,1,0:T(4,128)} custom-call(f32[3,768]{1,0:T(4,128)} %pad_maximum_fusion.9.source), custom_call_target="tpu_custom_call" | custom-call | tf_op jit(solution)/shard_map/pallas_call | solution.py:108
  795.0 35.4 %all-reduce.7.cloned.1.call-done = (bf16[1,3,768,384]{3,2,1,0:T(8,128)(2,1)}, bf16[1,384,768]{2,1,0:T(8,128)(2,1)}) async-done(((bf16[1,3,768,384]{3,2,1,0:T(8,128)(2,1)}, bf16[1,384,768]{2,1,0:T(8,128)(2,1)}), (bf16[1,3,768,384]{3,2,1,0:T(8,128)(2,1)}, bf16[1,384,768]{2,1,0:T(8,128)(2,1)})) %all-reduce.7.cloned.1.call-update) | async-done | bytes 2359312 | tf_op jit(solution)/shard_map/psum | solution.py:480
  (632 shorter events, 322.7 us)
Async XLA Ops:
  7.2 231.9 %copy-start = (bf16[1,768,1536]{2,1,0:T(8,128)(2,1)S(1)}, bf16[1,768,1536]{2,1,0:T(8,128)(2,1)}, u32[]{:S(2)}) copy-start(bf16[1,768,1536]{2,1,0:T(8,128)(2,1)} %param.35) | copy-start | bytes 7077892
  7.2 584.9 %all-reduce.11.cloned.1.call-start = ((), (), s32[]{:S(2)}) async-start(), calls=%async_computation.2 | async-start | bytes 9437184 | tf_op jit(solution)/shard_map/psum | solution.py:411
  85.2 20.6 %collective-permute-start = (bf16[1,512,768]{2,1,0:T(8,128)(2,1)}, bf16[1,512,768]{2,1,0:T(8,128)(2,1)S(1)}, u32[]{:S(2)}, u32[]{:S(2)}) collective-permute-start(bf16[1,512,768]{2,1,0:T(8,128)(2,1)} %multiply_convert_fusion.9), channel_id=1, source_target_pairs={{0,1},{1,0},{2,3},{3,2},{4,5},{5,4},{6,7},{7,6},{8,9},{9,8},{10,11... | collective-permute-start | bytes 2359304 | tf_op jit(solution)/shard_map/ppermute | solution.py:22
  86.7 134.8 %collective-permute-start.12 = (bf16[1,512,768]{2,1,0:T(8,128)(2,1)}, bf16[1,512,768]{2,1,0:T(8,128)(2,1)}, u32[]{:S(2)}, u32[]{:S(2)}) collective-permute-start(bf16[1,512,768]{2,1,0:T(8,128)(2,1)} %bitcast.737), channel_id=1, source_target_pairs={{0,1},{1,0},{2,3},{3,2},{4,5},{5,4},{6,7},{7,6},{8,9},{9,8},{10,11... | collective-permute-start | bytes 2359304 | tf_op jit(solution)/shard_map/ppermute | solution.py:22
  130.4 15.6 %collective-permute-start.1 = (bf16[1,512,768]{2,1,0:T(8,128)(2,1)S(1)}, bf16[1,512,768]{2,1,0:T(8,128)(2,1)S(1)}, u32[]{:S(2)}, u32[]{:S(2)}) collective-permute-start(bf16[1,512,768]{2,1,0:T(8,128)(2,1)S(1)} %fusion.92), channel_id=1, source_target_pairs={{0,1},{1,0},{2,3},{3,2},{4,5},{5,4},{6,7},{7,6},{8,9},{9,8},{10,11... | collective-permute-start | bytes 2359304 | tf_op jit(solution)/shard_map/ppermute | solution.py:22
  148.1 20.9 %collective-permute-start.3 = (bf16[1,512,768]{2,1,0:T(8,128)(2,1)S(1)}, bf16[1,512,768]{2,1,0:T(8,128)(2,1)}, u32[]{:S(2)}, u32[]{:S(2)}) collective-permute-start(bf16[1,512,768]{2,1,0:T(8,128)(2,1)S(1)} %multiply_convert_fusion.8), channel_id=1, source_target_pairs={{0,1},{1,0},{2,3},{3,2},{4,5},{5,4},{6,7},{7,6},{8,9},{9,8},{10,11... | collective-permute-start | bytes 2359304 | tf_op jit(solution)/shard_map/ppermute | solution.py:22
  150.9 20.6 %collective-permute-start.2 = (bf16[1,512,768]{2,1,0:T(8,128)(2,1)S(1)}, bf16[1,512,768]{2,1,0:T(8,128)(2,1)}, u32[]{:S(2)}, u32[]{:S(2)}) collective-permute-start(bf16[1,512,768]{2,1,0:T(8,128)(2,1)S(1)} %multiply_convert_fusion.8), channel_id=1, source_target_pairs={{0,2},{2,0},{1,3},{3,1},{4,6},{6,4},{5,7},{7,5},{8,10},{10,8},{9,1... | collective-permute-start | bytes 2359304 | tf_op jit(solution)/shard_map/ppermute | solution.py:22
  169.1 6.0 collective-permute-start.4
  199.4 19.6 %collective-permute-start.5 = (bf16[1,512,768]{2,1,0:T(8,128)(2,1)S(1)}, bf16[1,512,768]{2,1,0:T(8,128)(2,1)S(1)}, u32[]{:S(2)}, u32[]{:S(2)}) collective-permute-start(bf16[1,512,768]{2,1,0:T(8,128)(2,1)S(1)} %fusion.93), channel_id=1, source_target_pairs={{0,1},{1,0},{2,3},{3,2},{4,5},{5,4},{6,7},{7,6},{8,9},{9,8},{10,11... | collective-permute-start | bytes 2359304 | tf_op jit(solution)/shard_map/ppermute | solution.py:22
  220.4 18.7 %collective-permute-start.6 = (bf16[1,512,768]{2,1,0:T(8,128)(2,1)S(1)}, bf16[1,512,768]{2,1,0:T(8,128)(2,1)S(1)}, u32[]{:S(2)}, u32[]{:S(2)}) collective-permute-start(bf16[1,512,768]{2,1,0:T(8,128)(2,1)S(1)} %multiply_convert_fusion.7), channel_id=1, source_target_pairs={{0,1},{1,0},{2,3},{3,2},{4,5},{5,4},{6,7},{7,6},{8,9},{9,8},{10,11... | collective-permute-start | bytes 2359304 | tf_op jit(solution)/shard_map/ppermute | solution.py:22
  250.1 17.9 %collective-permute-start.7 = (bf16[1,512,768]{2,1,0:T(8,128)(2,1)S(1)}, bf16[1,512,768]{2,1,0:T(8,128)(2,1)S(1)}, u32[]{:S(2)}, u32[]{:S(2)}) collective-permute-start(bf16[1,512,768]{2,1,0:T(8,128)(2,1)S(1)} %fusion.94), channel_id=1, source_target_pairs={{0,1},{1,0},{2,3},{3,2},{4,5},{5,4},{6,7},{7,6},{8,9},{9,8},{10,11... | collective-permute-start | bytes 2359304 | tf_op jit(solution)/shard_map/ppermute | solution.py:22
  294.1 4.1 collective-permute-start.8
  307.1 4.2 collective-permute-start.10
  309.5 28.2 %collective-permute-start.9 = (f32[16,768]{1,0:T(8,128)}, f32[16,768]{1,0:T(8,128)}, u32[]{:S(2)}, u32[]{:S(2)}) collective-permute-start(f32[16,768]{1,0:T(8,128)} %fusion.313), channel_id=1, source_target_pairs={{0,1},{1,0},{2,3},{3,2},{4,5},{5,4},{6,7},{7,6},{8,9},{9,8},{10,11... | collective-permute-start | bytes 147464 | tf_op jit(solution)/shard_map/ppermute | solution.py:22
  332.9 5.7 collective-permute-start.11
  355.5 22.0 %collective-permute-start.13 = (bf16[1,512,768]{2,1,0:T(8,128)(2,1)}, bf16[1,512,768]{2,1,0:T(8,128)(2,1)}, u32[]{:S(2)}, u32[]{:S(2)}) collective-permute-start(bf16[1,512,768]{2,1,0:T(8,128)(2,1)} %fusion.97), channel_id=1, source_target_pairs={{0,1},{1,0},{2,3},{3,2},{4,5},{5,4},{6,7},{7,6},{8,9},{9,8},{10,11... | collective-permute-start | bytes 2359304 | tf_op jit(solution)/shard_map/ppermute | solution.py:22
  373.6 326.3 %all-reduce.9.cloned.1.call-start = ((), (), s32[]{:S(2)}) async-start(), calls=%async_computation.1 | async-start | bytes 4718592 | tf_op jit(solution)/shard_map/psum | solution.py:446
  382.4 17.4 %collective-permute-start.14 = (bf16[1,512,768]{2,1,0:T(8,128)(2,1)S(1)}, bf16[1,512,768]{2,1,0:T(8,128)(2,1)S(1)}, u32[]{:S(2)}, u32[]{:S(2)}) collective-permute-start(bf16[1,512,768]{2,1,0:T(8,128)(2,1)S(1)} %get-tuple-element.92), channel_id=1, source_target_pairs={{0,1},{1,0},{2,3},{3,2},{4,5},{5,4},{6,7},{7,6},{8,9},{9,8},{10,11... | collective-permute-start | bytes 2359304 | tf_op jit(solution)/shard_map/ppermute | solution.py:22
  453.6 8.1 collective-permute-start.16
  454.3 14.4 %collective-permute-start.15 = (bf16[1,512,768]{2,1,0:T(8,128)(2,1)S(1)}, bf16[1,512,768]{2,1,0:T(8,128)(2,1)S(1)}, u32[]{:S(2)}, u32[]{:S(2)}) collective-permute-start(bf16[1,512,768]{2,1,0:T(8,128)(2,1)S(1)} %fusion.100), channel_id=1, source_target_pairs={{0,2},{2,0},{1,3},{3,1},{4,6},{6,4},{5,7},{7,5},{8,10},{10,8},{9,1... | collective-permute-start | bytes 2359304 | tf_op jit(solution)/shard_map/ppermute | solution.py:22
  462.3 19.9 %collective-permute-start.17 = (bf16[1,512,768]{2,1,0:T(8,128)(2,1)S(1)}, bf16[1,512,768]{2,1,0:T(8,128)(2,1)S(1)}, u32[]{:S(2)}, u32[]{:S(2)}) collective-permute-start(bf16[1,512,768]{2,1,0:T(8,128)(2,1)S(1)} %fusion.65), channel_id=1, source_target_pairs={{0,1},{1,0},{2,3},{3,2},{4,5},{5,4},{6,7},{7,6},{8,9},{9,8},{10,11... | collective-permute-start | bytes 2359304 | tf_op jit(solution)/shard_map/ppermute | solution.py:22
  485.0 18.8 %collective-permute-start.18 = (bf16[1,512,768]{2,1,0:T(8,128)(2,1)S(1)}, bf16[1,512,768]{2,1,0:T(8,128)(2,1)}, u32[]{:S(2)}, u32[]{:S(2)}) collective-permute-start(bf16[1,512,768]{2,1,0:T(8,128)(2,1)S(1)} %get-tuple-element.89), channel_id=1, source_target_pairs={{0,1},{1,0},{2,3},{3,2},{4,5},{5,4},{6,7},{7,6},{8,9},{9,8},{10,11... | collective-permute-start | bytes 2359304 | tf_op jit(solution)/shard_map/ppermute | solution.py:22
  576.5 24.4 %collective-permute-start.19 = (bf16[1,512,768]{2,1,0:T(8,128)(2,1)}, bf16[1,512,768]{2,1,0:T(8,128)(2,1)}, u32[]{:S(2)}, u32[]{:S(2)}) collective-permute-start(bf16[1,512,768]{2,1,0:T(8,128)(2,1)} %fusion.102), channel_id=1, source_target_pairs={{0,1},{1,0},{2,3},{3,2},{4,5},{5,4},{6,7},{7,6},{8,9},{9,8},{10,11... | collective-permute-start | bytes 2359304 | tf_op jit(solution)/shard_map/ppermute | solution.py:22
  592.2 238.3 %all-reduce.7.cloned.1.call-start = ((), (), s32[]{:S(2)}) async-start(), calls=%async_computation | async-start | bytes 4718592 | tf_op jit(solution)/shard_map/psum | solution.py:480
  (173 other events, 1931.0 us)
Sparse Core Ops, SparseCore 0:
  373.7 169.6 all-reduce.10
  592.3 107.6 all-reduce.8
  704.1 126.2 all-reduce.6

commit v2 on v1

--- a/solution.py
+++ b/solution.py
@@ -119,15 +119,31 @@
     )(value)
 
 
+def pick_kernel(wanted_ref, held_ref, out_ref):
+    out_ref[...] = held_ref[...]
+
+
+def pick(held, wanted):
+    block = (1,) + held.shape[1:]
+    return pl.pallas_call(
+        pick_kernel,
+        grid_spec=pltpu.PrefetchScalarGridSpec(
+            num_scalar_prefetch=1,
+            grid=(held.shape[0],),
+            in_specs=[pl.BlockSpec(block, lambda i, wanted_ref: (wanted_ref[i], 0, 0))],
+            out_specs=pl.BlockSpec(block, lambda i, wanted_ref: (i, 0, 0)),
+        ),
+        out_shape=jax.ShapeDtypeStruct(held.shape, held.dtype),
+    )(wanted, held)
+
+
 def clip_rows(rows, wanted, collective_id):
     count = lax.axis_size("dp")
     clips, length, width = rows.shape
     pieces = jnp.swapaxes(rows.reshape(clips, count, length // count, width), 0, 1)
     held = trade(pieces, ("dp",), True, collective_id)
     held = held.reshape(count * clips, length // count, width)
-    picked = jnp.concatenate(
-        [lax.dynamic_slice_in_dim(held, wanted[clip], 1) for clip in range(count * clips)]
-    )
+    picked = pick(held, wanted)
     back = trade(picked.reshape(pieces.shape), ("dp",), True, collective_id + 1)
     return jnp.swapaxes(back, 0, 1).reshape(rows.shape)
 
@@ -178,35 +194,140 @@
     return (query_grad, key_grad, value_grad)
 
 
-def attend(queries, keys, values, valid):
-    key_rows = split_heads(jnp.concatenate(keys, 1))
-    value_rows = split_heads(jnp.concatenate(values, 1))
-    heads = [None] * len(queries)
-    sums = [None] * len(queries)
-    for j in far_first(len(queries)):
-        result, sums[j] = attend_block(split_heads(queries[j]), key_rows, value_rows, valid)
-        heads[j] = merge_heads(result)
+def joined(left, right, left_dim, right_dim):
+    return lax.dot_general(
+        left, right, (((left_dim,), (right_dim,)), ((), ())), preferred_element_type=jnp.float32
+    )
+
+
+def wide_bias(bias_ref, start, length, width):
+    part = bias_ref[start : start + length, :]
+    return jnp.concatenate([part] * (width // part.shape[1]), 1)
+
+
+def attend_kernel(parts, chunk, query_ref, *refs):
+    key_refs, value_refs = refs[:parts], refs[parts : 2 * parts]
+    bias_ref, out_ref, sums_ref = refs[2 * parts :]
+    length = key_refs[0].shape[1]
+    for half in range(2):
+        lanes = slice(HEAD * half, HEAD * half + HEAD)
+        keys = [ref[0, :, lanes] for ref in key_refs]
+        values = [ref[0, :, lanes] for ref in value_refs]
+        for start in range(0, query_ref.shape[1], chunk):
+            query = query_ref[0, start : start + chunk, lanes]
+            scores = [
+                joined(key, query, 1, 1) + wide_bias(bias_ref, j * length, length, chunk)
+                for j, key in enumerate(keys)
+            ]
+            highest = functools.reduce(
+                jnp.maximum, [jnp.max(score, 0, keepdims=True) for score in scores]
+            )
+            raised = [jnp.exp(score - highest) for score in scores]
+            totals = sum(jnp.sum(part, 0, keepdims=True) for part in raised)
+            result = sum(
+                joined(value, part.astype(jnp.bfloat16), 0, 0)
+                for value, part in zip(values, raised)
+            )
+            out_ref[0, start : start + chunk, lanes] = (result / totals).T.astype(jnp.bfloat16)
+            sums_ref[0, 0, half : half + 1, start : start + chunk] = highest + jnp.log(totals)
+
+
+def attend_back_kernel(parts, chunk, first, query_ref, grad_ref, heads_ref, sums_ref, *refs):
+    key_refs, value_refs = refs[:parts], refs[parts : 2 * parts]
+    bias_ref = refs[2 * parts]
+    refs = refs[2 * parts + 1 :]
+    held, outs = ((), refs) if first else (refs[: 2 * parts], refs[2 * parts :])
+    query_grad_ref, grad_refs = outs[0], outs[1:]
+    length = key_refs[0].shape[1]
+    for half in range(2):
+        lanes = slice(HEAD * half, HEAD * half + HEAD)
+        keys = [ref[0, :, lanes] for ref in key_refs]
+        values = [ref[0, :, lanes] for ref in value_refs]
+        totals = [0.0 if first else ref[0, :, lanes] for ref in held] or [0.0] * (2 * parts)
+        for start in range(0, query_ref.shape[1], chunk):
+            rows = slice(start, start + chunk)
+            query = query_ref[0, rows, lanes]
+            grad = grad_ref[0, rows, lanes]
+            shared = grad.astype(jnp.float32) * heads_ref[0, rows, lanes].astype(jnp.float32)
+            delta = jnp.sum(shared.T, 0, keepdims=True)
+            log_sums = sums_ref[0, 0, half : half + 1, rows]
+            query_grad = 0.0
+            for j in range(parts):
+                scores = joined(keys[j], query, 1, 1) + wide_bias(
+                    bias_ref, j * length, length, chunk
+                )
+                weights = jnp.exp(scores - log_sums)
+                grad_scores = (weights * (joined(values[j], grad, 1, 1) - delta)).astype(
+                    jnp.bfloat16
+                )
+                totals[j] = totals[j] + joined(grad_scores, query, 1, 0)
+                totals[parts + j] = totals[parts + j] + joined(
+                    weights.astype(jnp.bfloat16), grad, 1, 0
+                )
+                query_grad = query_grad + joined(keys[j], grad_scores, 0, 0)
+            query_grad_ref[0, rows, lanes] = query_grad.T.astype(jnp.bfloat16)
+        for total, ref in zip(totals, grad_refs):
+            ref[0, :, lanes] = total.astype(ref.dtype)
+
+
+def pair_spec(length):
+    return pl.BlockSpec((1, length, 2 * HEAD), lambda clip, pair: (clip, 0, pair))
+
+
+def sums_spec(length):
+    return pl.BlockSpec((1, 1, 2, length), lambda clip, pair: (clip, pair, 0, 0))
+
+
+def bias_spec(length):
+    return pl.BlockSpec((length, 2 * HEAD), lambda clip, pair: (0, 0))
+
+
+CHUNK = 256
+
+
+def attend(queries, keys, values, bias):
+    parts = len(keys)
+    clips, length, width = queries[0].shape
+    pairs = width // (2 * HEAD)
+    heads = [None] * parts
+    sums = [None] * parts
+    for j in far_first(parts):
+        heads[j], sums[j] = pl.pallas_call(
+            functools.partial(attend_kernel, parts, min(CHUNK, length)),
+            grid=(clips, pairs),
+            out_shape=(
+                jax.ShapeDtypeStruct((clips, length, width), jnp.bfloat16),
+                jax.ShapeDtypeStruct((clips, pairs, 2, length), jnp.float32),
+            ),
+            in_specs=[pair_spec(length)] * (1 + 2 * parts) + [bias_spec(parts * length)],
+            out_specs=(pair_spec(length), sums_spec(length)),
+        )(queries[j], *keys, *values, bias)
     return (heads, sums)
 
 
-def attend_back(queries, keys, values, valid, grads, sums):
-    key_rows = split_heads(jnp.concatenate(keys, 1))
-    value_rows = split_heads(jnp.concatenate(values, 1))
-    query_grads = [None] * len(queries)
-    key_grad = value_grad = 0.0
-    for j in far_first(len(queries)):
-        query_grad, key_term, value_term = attend_block_back(
-            split_heads(queries[j]), key_rows, value_rows, valid, split_heads(grads[j]), sums[j]
-        )
-        query_grads[j] = merge_heads(query_grad)
-        key_grad = key_grad + key_term
-        value_grad = value_grad + value_term
+def attend_back(queries, keys, values, bias, grads, heads, sums):
     parts = len(keys)
-    return (
-        query_grads,
-        jnp.split(merge_heads(key_grad.astype(jnp.bfloat16)), parts, 1),
-        jnp.split(merge_heads(value_grad.astype(jnp.bfloat16)), parts, 1),
-    )
+    clips, length, width = queries[0].shape
+    pairs = width // (2 * HEAD)
+    query_grads = []
+    held = []
+    for j in range(parts):
+        kind = jnp.bfloat16 if j == parts - 1 else jnp.float32
+        outs = pl.pallas_call(
+            functools.partial(attend_back_kernel, parts, min(CHUNK, length), j == 0),
+            grid=(clips, pairs),
+            out_shape=[jax.ShapeDtypeStruct((clips, length, width), jnp.bfloat16)]
+            + [jax.ShapeDtypeStruct((clips, length, width), kind)] * (2 * parts),
+            in_specs=[pair_spec(length)] * 3
+            + [sums_spec(length)]
+            + [pair_spec(length)] * (2 * parts)
+            + [bias_spec(parts * length)]
+            + [pair_spec(length)] * len(held),
+            out_specs=[pair_spec(length)] * (1 + 2 * parts),
+        )(queries[j], grads[j], heads[j], sums[j], *keys, *values, bias, *held)
+        query_grads.append(outs[0])
+        held = list(outs[1:])
+    return (query_grads, held[:parts], held[parts:])
 
 
 def project_rows(source, weight):
@@ -238,7 +359,9 @@
     top_query = query_rows(top_low, use_project[0])
     top_key = project_rows(top_low, use_project[1]).astype(jnp.bfloat16)
     top_value = project_rows(top_low, use_project[2]).astype(jnp.bfloat16)
-    (top_flat,), top_sums = attend([top_query], [top_key], [top_value], summary_valid)
+    top_key, top_value = split_heads(top_key), split_heads(top_value)
+    top_heads, top_sums = attend_block(split_heads(top_query), top_key, top_value, summary_valid)
+    top_flat = merge_heads(top_heads)
     summary_mid = summary_rows + whole_sum(product(top_flat, use_merge, "cse,ed->csd")[0])
     mid_normed, mid_unit, mid_inverse = layer_norm(summary_mid, gain_last)
     mid_low = mid_normed.astype(jnp.bfloat16)[None]
@@ -258,9 +381,17 @@
     merge_input = mid_grad.astype(jnp.bfloat16)[None]
     merge_grad = product(top_flat, merge_input, "cse,csd->ed")
     top_heads_grad = product(merge_input, use_merge, "csd,ed->cse").astype(jnp.bfloat16)
-    (query_grad,), (key_grad,), (value_grad,) = attend_back(
-        [top_query], [top_key], [top_value], summary_valid, [top_heads_grad], top_sums
-    )
+    query_grad, key_grad, value_grad = attend_block_back(
+        split_heads(top_query),
+        top_key,
+        top_value,
+        summary_valid,
+        split_heads(top_heads_grad),
+        top_sums,
+    )
+    query_grad = merge_heads(query_grad)
+    key_grad = merge_heads(key_grad).astype(jnp.bfloat16)
+    value_grad = merge_heads(value_grad).astype(jnp.bfloat16)
     query_grad = query_grad * HEAD ** (-0.5)
     project_grad = jnp.stack(
         [product(top_low, grad, "csd,cse->de") for grad in (query_grad, key_grad, value_grad)]
@@ -324,8 +455,12 @@
     mixed_rows = mixing * local_tokens.astype(jnp.float32) + (1.0 - mixing) * partner_tokens
     owners = [(model_index + step) % model_total for step in range(model_total)]
     positions = jnp.concatenate([owner * length + jnp.arange(length) for owner in owners])
-    own_valid = (positions < view_counts[view_index])[None, None, None, :]
-    next_valid = (positions < view_counts[(view_index + 1) % view_total])[None, None, None, :]
+    own_valid = positions < view_counts[view_index]
+    next_valid = positions < view_counts[(view_index + 1) % view_total]
+    own_bias, next_bias = (
+        jnp.broadcast_to(jnp.where(valid, 0.0, NEG)[:, None], (positions.shape[0], 2 * HEAD))
+        for valid in (own_valid, next_valid)
+    )
 
     normed_self, unit_self, inverse_self = layer_norm(mixed_rows, norm_self[0])
     self_blocks = row_blocks(normed_self.astype(jnp.bfloat16))
@@ -335,7 +470,7 @@
     self_values = [
         project_rows(block, self_weights[2]).astype(jnp.bfloat16) for block in self_blocks
     ]
-    self_heads, self_sums = attend(self_queries, self_keys, self_values, own_valid)
+    self_heads, self_sums = attend(self_queries, self_keys, self_values, own_bias)
     first_rows = mixed_rows + own_sum(
         [product(heads, self_merge[0], "cse,ed->csd") for heads in self_heads]
     )
@@ -351,7 +486,7 @@
     cross_values = [
         project_rows(block, cross_weights[2]).astype(jnp.bfloat16) for block in next_blocks
     ]
-    cross_heads, cross_sums = attend(cross_queries, cross_keys, cross_values, next_valid)
+    cross_heads, cross_sums = attend(cross_queries, cross_keys, cross_values, next_bias)
     second_rows = first_rows + own_sum(
         [product(heads, cross_merge[0], "cse,ed->csd") for heads in cross_heads]
     )
@@ -422,7 +557,7 @@
         for block in merge_blocks
     ]
     query_grads, key_grads, value_grads = attend_back(
-        cross_queries, cross_keys, cross_values, next_valid, heads_grads, cross_sums
+        cross_queries, cross_keys, cross_values, next_bias, heads_grads, cross_heads, cross_sums
     )
     query_grads = scaled_grads(query_grads)
     terms = [None] * model_total
@@ -454,7 +589,7 @@
         product(block, self_merge[0], "csd,ed->cse").astype(jnp.bfloat16) for block in merge_blocks
     ]
     query_grads, key_grads, value_grads = attend_back(
-        self_queries, self_keys, self_values, own_valid, heads_grads, self_sums
+        self_queries, self_keys, self_values, own_bias, heads_grads, self_heads, self_sums
     )
     query_grads = scaled_grads(query_grads)
     self_norm_grad = own_sum(

time: 854 us -> 792 us (0.927)
  Pallas kernels: 136 us -> 245 us
  matrix products: 258 us -> 177 us
  other arithmetic: 110 us -> 62 us
  between operations: 48.2 us -> 16.3 us
  local copies, waits for them, and re-layouts: 45.4 us -> 21.4 us
  waiting for transfers between devices: 225 us -> 240 us
    pallas_call x0 -> x10, Pallas kernels: none -> 101 us  [the longest x4 49.7 us: attend_back(): pl.pallas_call(functools.partial(attend_back_kernel, parts, min(CHUNK, le...]
    dot_general x108 -> x84, matrix products: 258 us -> 177 us  [product(): return jnp.einsum(form, left, right, preferred_element_type=jnp.float32)]
    psum x1, waiting for transfers between devices: 0.01 us -> 40.1 us  [shards(): lax.psum((up_grad.astype(jnp.bfloat16), down_grad.astype(jnp.bfloat16)),...]
    convert_element_type x3 -> x1, other arithmetic: 39.8 us -> 0.71 us  [attend_block_back(): grad_scores = (weights * (grad_weights - jnp.sum(weights * grad_weights,...]
    ppermute x20, waiting for transfers between devices: 95.1 us -> 71.6 us  [shifted(): return lax.ppermute(value, axis, pairs)]
    unnamed x362 -> x248, local copies, waits for them, and re-layouts: 24.8 us -> 9.41 us
    reduce_sum x3 -> x1, other arithmetic: 12.5 us -> 0.03 us  [attend_block(): totals = jnp.sum(raised, -1, keepdims=True)]
    pallas_call x6, Pallas kernels: 136 us -> 145 us  [trade(): pl.pallas_call(functools.partial(trade_kernel, axes, total, split), out_s...]
  transfers between devices with their start and end apart: 23 -> 23, of which waited for: 12 -> 13; matrix products, arithmetic and copies ran while one was open for 40% -> 22% of each run, Pallas kernels for 9% -> 20%
where the time goes in v2:
time: 792 us; the launch traced here: 782 us
  Pallas kernels  245 us (31%)
  waiting for transfers between devices  240 us (30%)
  matrix products  177 us (22%)
  other arithmetic  62 us (8%)
  local copies, waits for them, and re-layouts  21.4 us (3%)
  starting transfers between devices  20.1 us (3%)
  between operations  16.3 us (2%)
    dot_general x84, matrix products, product(): return jnp.einsum(form, left, right, preferred_element_type=jnp.float32)  177 us
    pallas_call x6, Pallas kernels, trade(): pl.pallas_call(functools.partial(trade_kernel, axes, total, split), out_s...  145 us
    psum x1, waiting for transfers between devices, shards(): cross_project_sum, cross_merge_sum = lax.psum(cross_low, 'dp')  94.4 us
    ppermute x20, waiting for transfers between devices, shifted(): return lax.ppermute(value, axis, pairs)  71.6 us
    pallas_call x4, Pallas kernels, attend_back(): pl.pallas_call(functools.partial(attend_back_kernel, parts, min(CHUNK, le...  49.7 us
    psum x1, waiting for transfers between devices, shards(): lax.psum((up_grad.astype(jnp.bfloat16), down_grad.astype(jnp.bfloat16)),...  40.1 us
    pallas_call x4, Pallas kernels, attend(): pl.pallas_call(functools.partial(attend_kernel, parts, min(CHUNK, length)...  39.7 us
    psum x1, waiting for transfers between devices, shards(): self_project_sum, self_merge_sum = lax.psum(self_low, 'dp')  34 us
  transfers between devices with their start and end apart: 23, of which 13 were waited for; matrix products, arithmetic and copies ran while one was open for 22% of the time, Pallas kernels for 20%

profile of v2, /device:TPU:0, one launch (start us, length us, event | category | flops | bytes accessed | tf_op | source)
XLA Modules:
  0.0 782.1 jit_solution(5065634984265869486)
XLA Ops:
  7.2 21.1 %shard_map.349 = bf16[8,1,64,768]{3,2,1,0:T(8,128)(2,1)} custom-call(bf16[8,1,64,768]{3,2,1,0:T(8,128)(2,1)} %bitcast.529), custom_call_target="tpu_custom_call" | custom-call | tf_op jit(solution)/shard_map/pallas_call | solution.py:108
  34.1 22.7 %shard_map.351 = bf16[8,1,64,768]{3,2,1,0:T(8,128)(2,1)} custom-call(bf16[8,1,64,768]{3,2,1,0:T(8,128)(2,1)} %bitcast.532), custom_call_target="tpu_custom_call" | custom-call | tf_op jit(solution)/shard_map/pallas_call | solution.py:108
  72.1 9.1 %collective-permute-done = bf16[1,512,768]{2,1,0:T(8,128)(2,1)} collective-permute-done((bf16[1,512,768]{2,1,0:T(8,128)(2,1)}, bf16[1,512,768]{2,1,0:T(8,128)(2,1)}, u32[]{:S(2)}, u32[]{:S(2)}) %collective-permute-start) | collective-permute-done | bytes 786464 | tf_op jit(solution)/shard_map/ppermute | solution.py:22
  89.5 9.8 %shard_map.353 = (bf16[1,512,384]{2,1,0:T(8,128)(2,1)}, f32[1,3,2,512]{3,2,1,0:T(2,128)}) custom-call(bf16[1,512,384]{2,1,0:T(8,128)(2,1)} %fusion.79.query_ref, bf16[1,512,384]{2,1,0:T(8,128)(2,1)} %fusion.81.refs_0_, bf16[1,512,384]{2,1,0:T(8,128)(2,1)} %fusion.82.refs_1_, bf16[1,512,384]{2,1,0:T(8,128)(2,1)} %fusion.83.refs_2_, ...), custom_call_target="tpu_custom_call" | custom-call | tf_op jit(solution)/shard_map/pallas_call | solution.py:295
  105.9 10.3 %shard_map.352 = (bf16[1,512,384]{2,1,0:T(8,128)(2,1)}, f32[1,3,2,512]{3,2,1,0:T(2,128)}) custom-call(bf16[1,512,384]{2,1,0:T(8,128)(2,1)} %fusion.80.query_ref, bf16[1,512,384]{2,1,0:T(8,128)(2,1)} %fusion.81.refs_0_, bf16[1,512,384]{2,1,0:T(8,128)(2,1)} %fusion.82.refs_1_, bf16[1,512,384]{2,1,0:T(8,128)(2,1)} %fusion.83.refs_2_, ...), custom_call_target="tpu_custom_call" | custom-call | tf_op jit(solution)/shard_map/pallas_call | solution.py:295
  123.5 13.6 %collective-permute-done.3 = bf16[1,512,768]{2,1,0:T(8,128)(2,1)S(1)} collective-permute-done((bf16[1,512,768]{2,1,0:T(8,128)(2,1)S(1)}, bf16[1,512,768]{2,1,0:T(8,128)(2,1)S(1)}, u32[]{:S(2)}, u32[]{:S(2)}) %collective-permute-start.3) | collective-permute-done | bytes 786464 | tf_op jit(solution)/shard_map/ppermute | solution.py:22
  144.8 9.8 %shard_map.355 = (bf16[1,512,384]{2,1,0:T(8,128)(2,1)}, f32[1,3,2,512]{3,2,1,0:T(2,128)}) custom-call(bf16[1,512,384]{2,1,0:T(8,128)(2,1)} %fusion.77.query_ref, bf16[1,512,384]{2,1,0:T(8,128)(2,1)} %fusion.85.refs_0_, bf16[1,512,384]{2,1,0:T(8,128)(2,1)} %fusion.86.refs_1_, bf16[1,512,384]{2,1,0:T(8,128)(2,1)} %fusion.87.refs_2_, ...), custom_call_target="tpu_custom_call" | custom-call | tf_op jit(solution)/shard_map/pallas_call | solution.py:295
  162.0 9.8 %shard_map.354 = (bf16[1,512,384]{2,1,0:T(8,128)(2,1)}, f32[1,3,2,512]{3,2,1,0:T(2,128)}) custom-call(bf16[1,512,384]{2,1,0:T(8,128)(2,1)} %fusion.78.query_ref, bf16[1,512,384]{2,1,0:T(8,128)(2,1)} %fusion.85.refs_0_, bf16[1,512,384]{2,1,0:T(8,128)(2,1)} %fusion.86.refs_1_, bf16[1,512,384]{2,1,0:T(8,128)(2,1)} %fusion.87.refs_2_, ...), custom_call_target="tpu_custom_call" | custom-call | tf_op jit(solution)/shard_map/pallas_call | solution.py:295
  197.3 14.0 %collective-permute-done.6 = bf16[1,512,768]{2,1,0:T(8,128)(2,1)} collective-permute-done((bf16[1,512,768]{2,1,0:T(8,128)(2,1)}, bf16[1,512,768]{2,1,0:T(8,128)(2,1)}, u32[]{:S(2)}, u32[]{:S(2)}) %collective-permute-start.6) | collective-permute-done | bytes 786464 | tf_op jit(solution)/shard_map/ppermute | solution.py:22
  211.3 10.7 %multiply_convert_fusion = (bf16[512,1536]{1,0:T(8,128)(2,1)S(1)}, f32[512,1536]{1,0:T(8,128)}, f32[512,1536]{1,0:T(8,128)}) fusion(bf16[1,768,1536]{2,1,0:T(8,128)(2,1)S(1)} %copy-done, bf16[1,512,768]{2,1,0:T(8,128)(2,1)} %collective-permute-done.6), kind=kOutput, calls=%fused_computation.9 | convolution fusion | flops 1259077632 | bytes 11010048 | tf_op jit(solution)/shard_map/csd,df->csf/dot_general | solution.py:44
  226.1 10.8 %multiply_convert_fusion.1 = (bf16[512,1536]{1,0:T(8,128)(2,1)S(1)}, f32[512,1536]{1,0:T(8,128)}, f32[512,1536]{1,0:T(8,128)}) fusion(bf16[1,768,1536]{2,1,0:T(8,128)(2,1)S(1)} %copy-done, bf16[1,512,768]{2,1,0:T(8,128)(2,1)} %multiply_convert_fusion.3), kind=kOutput, calls=%fused_computation.22 | convolution fusion | flops 1259077632 | bytes 11010048 | tf_op jit(solution)/shard_map/csd,df->csf/dot_general | solution.py:44
  236.9 6.7 collective-permute-done.7
  246.6 18.9 %shard_map.356 = f32[32,1,768]{2,1,0:T(1,128)} custom-call(f32[1,768]{1,0:T(1,128)} %slice_bitcast_fusion.source), custom_call_target="tpu_custom_call" | custom-call | tf_op jit(solution)/shard_map/pallas_call | solution.py:108
  365.0 12.8 %shard_map.357 = (bf16[1,512,384]{2,1,0:T(8,128)(2,1)}, f32[1,512,384]{2,1,0:T(8,128)}, f32[1,512,384]{2,1,0:T(8,128)}, f32[1,512,384]{2,1,0:T(8,128)}, f32[1,512,384]{2,1,0:T(8,128)}) custom-call(bf16[1,512,384]{2,1,0:T(8,128)(2,1)} %fusion.78.query_ref, bf16[1,512,384]{2,1,0:T(8,128)(2,1)} %fusion.89.grad_ref, ...), custom_call_target="tpu_custom_call" | custom-call | tf_op jit(solution)/shard_map/pallas_call | solution.py:316
  387.6 12.3 %shard_map.358 = (bf16[1,512,384]{2,1,0:T(8,128)(2,1)}, bf16[1,512,384]{2,1,0:T(8,128)(2,1)}, bf16[1,512,384]{2,1,0:T(8,128)(2,1)}, bf16[1,512,384]{2,1,0:T(8,128)(2,1)}, bf16[1,512,384]{2,1,0:T(8,128)(2,1)}) custom-call(bf16[1,512,384]{2,1,0:T(8,128)(2,1)} %fusion.77.query_ref, bf16[1,512,384]{2,1,0:T(8,128)(2,1)} %fusion.90.grad_ref, ...), custom_call_target="tpu_custom_call" | custom-call | tf_op jit(solution)/shard_map/pallas_call | solution.py:316
  416.2 12.6 %collective-permute-done.17 = bf16[1,512,768]{2,1,0:T(8,128)(2,1)} collective-permute-done((bf16[1,512,768]{2,1,0:T(8,128)(2,1)}, bf16[1,512,768]{2,1,0:T(8,128)(2,1)}, u32[]{:S(2)}, u32[]{:S(2)}) %collective-permute-start.17) | collective-permute-done | bytes 786464 | tf_op jit(solution)/shard_map/ppermute | solution.py:22
  438.4 12.6 %shard_map.359 = (bf16[1,512,384]{2,1,0:T(8,128)(2,1)}, f32[1,512,384]{2,1,0:T(8,128)}, f32[1,512,384]{2,1,0:T(8,128)}, f32[1,512,384]{2,1,0:T(8,128)}, f32[1,512,384]{2,1,0:T(8,128)}) custom-call(bf16[1,512,384]{2,1,0:T(8,128)(2,1)} %fusion.80.query_ref, bf16[1,512,384]{2,1,0:T(8,128)(2,1)} %fusion.91.grad_ref, ...), custom_call_target="tpu_custom_call" | custom-call | tf_op jit(solution)/shard_map/pallas_call | solution.py:316
  460.7 12.0 %shard_map.360 = (bf16[1,512,384]{2,1,0:T(8,128)(2,1)}, bf16[1,512,384]{2,1,0:T(8,128)(2,1)}, bf16[1,512,384]{2,1,0:T(8,128)(2,1)}, bf16[1,512,384]{2,1,0:T(8,128)(2,1)}, bf16[1,512,384]{2,1,0:T(8,128)(2,1)}) custom-call(bf16[1,512,384]{2,1,0:T(8,128)(2,1)} %fusion.79.query_ref, bf16[1,512,384]{2,1,0:T(8,128)(2,1)} %fusion.92.grad_ref, ...), custom_call_target="tpu_custom_call" | custom-call | tf_op jit(solution)/shard_map/pallas_call | solution.py:316
  482.3 40.1 %all-reduce.11.cloned.1.call-done = (bf16[768,1536]{1,0:T(8,128)(2,1)}, bf16[1536,768]{1,0:T(8,128)(2,1)}) async-done(((bf16[768,1536]{1,0:T(8,128)(2,1)}, bf16[1536,768]{1,0:T(8,128)(2,1)}), (bf16[768,1536]{1,0:T(8,128)(2,1)}, bf16[1536,768]{1,0:T(8,128)(2,1)})) %all-reduce.11.cloned.1.call-update) | async-done | bytes 4718608 | tf_op jit(solution)/shard_map/psum | solution.py:546
  539.4 94.4 %all-reduce.9.cloned.1.call-done = (bf16[3,768,384]{2,1,0:T(8,128)(2,1)}, bf16[384,768]{1,0:T(8,128)(2,1)}) async-done(((bf16[3,768,384]{2,1,0:T(8,128)(2,1)}, bf16[384,768]{1,0:T(8,128)(2,1)}), (bf16[3,768,384]{2,1,0:T(8,128)(2,1)}, bf16[384,768]{1,0:T(8,128)(2,1)})) %all-reduce.9.cloned.1.call-update) | async-done | bytes 2359312 | tf_op jit(solution)/shard_map/psum | solution.py:581
  639.9 29.7 %shard_map.361 = bf16[8,1,64,768]{3,2,1,0:T(8,128)(2,1)} custom-call(bf16[8,1,64,768]{3,2,1,0:T(8,128)(2,1)} %bitcast.537), custom_call_target="tpu_custom_call" | custom-call | tf_op jit(solution)/shard_map/pallas_call | solution.py:108
  675.3 36.3 %shard_map.363 = bf16[8,1,64,768]{3,2,1,0:T(8,128)(2,1)} custom-call(bf16[8,1,64,768]{3,2,1,0:T(8,128)(2,1)} %bitcast.531), custom_call_target="tpu_custom_call" | custom-call | tf_op jit(solution)/shard_map/pallas_call | solution.py:108
  712.3 15.8 %shard_map.364 = f32[16,3,768]{2,1,0:T(4,128)} custom-call(f32[3,768]{1,0:T(4,128)} %pad_maximum_fusion.3.source), custom_call_target="tpu_custom_call" | custom-call | tf_op jit(solution)/shard_map/pallas_call | solution.py:108
  736.7 34.0 %all-reduce.7.cloned.1.call-done = (bf16[1,3,768,384]{3,2,1,0:T(8,128)(2,1)}, bf16[1,384,768]{2,1,0:T(8,128)(2,1)}) async-done(((bf16[1,3,768,384]{3,2,1,0:T(8,128)(2,1)}, bf16[1,384,768]{2,1,0:T(8,128)(2,1)}), (bf16[1,3,768,384]{3,2,1,0:T(8,128)(2,1)}, bf16[1,384,768]{2,1,0:T(8,128)(2,1)})) %all-reduce.7.cloned.1.call-update) | async-done | bytes 2359312 | tf_op jit(solution)/shard_map/psum | solution.py:615
  (489 shorter events, 285.7 us)
Async XLA Ops:
  7.2 204.1 %copy-start = (bf16[1,768,1536]{2,1,0:T(8,128)(2,1)S(1)}, bf16[1,768,1536]{2,1,0:T(8,128)(2,1)}, u32[]{:S(2)}) copy-start(bf16[1,768,1536]{2,1,0:T(8,128)(2,1)} %param.35) | copy-start | bytes 7077892
  7.2 515.3 %all-reduce.11.cloned.1.call-start = ((), (), s32[]{:S(2)}) async-start(), calls=%async_computation.2 | async-start | bytes 9437184 | tf_op jit(solution)/shard_map/psum | solution.py:546
  64.0 17.1 %collective-permute-start = (bf16[1,512,768]{2,1,0:T(8,128)(2,1)}, bf16[1,512,768]{2,1,0:T(8,128)(2,1)}, u32[]{:S(2)}, u32[]{:S(2)}) collective-permute-start(bf16[1,512,768]{2,1,0:T(8,128)(2,1)} %multiply_convert_fusion.5), channel_id=1, source_target_pairs={{0,1},{1,0},{2,3},{3,2},{4,5},{5,4},{6,7},{7,6},{8,9},{9,8},{10,11... | collective-permute-start | bytes 2359304 | tf_op jit(solution)/shard_map/ppermute | solution.py:22
  102.0 16.3 %collective-permute-start.1 = (bf16[1,512,768]{2,1,0:T(8,128)(2,1)}, bf16[1,512,768]{2,1,0:T(8,128)(2,1)}, u32[]{:S(2)}, u32[]{:S(2)}) collective-permute-start(bf16[1,512,768]{2,1,0:T(8,128)(2,1)} %fusion.56), channel_id=1, source_target_pairs={{0,1},{1,0},{2,3},{3,2},{4,5},{5,4},{6,7},{7,6},{8,9},{9,8},{10,11... | collective-permute-start | bytes 2359304 | tf_op jit(solution)/shard_map/ppermute | solution.py:22
  122.0 15.1 %collective-permute-start.3 = (bf16[1,512,768]{2,1,0:T(8,128)(2,1)S(1)}, bf16[1,512,768]{2,1,0:T(8,128)(2,1)S(1)}, u32[]{:S(2)}, u32[]{:S(2)}) collective-permute-start(bf16[1,512,768]{2,1,0:T(8,128)(2,1)S(1)} %multiply_convert_fusion.4), channel_id=1, source_target_pairs={{0,1},{1,0},{2,3},{3,2},{4,5},{5,4},{6,7},{7,6},{8,9},{9,8},{10,11... | collective-permute-start | bytes 2359304 | tf_op jit(solution)/shard_map/ppermute | solution.py:22
  123.5 13.6 %collective-permute-start.2 = (bf16[1,512,768]{2,1,0:T(8,128)(2,1)S(1)}, bf16[1,512,768]{2,1,0:T(8,128)(2,1)S(1)}, u32[]{:S(2)}, u32[]{:S(2)}) collective-permute-start(bf16[1,512,768]{2,1,0:T(8,128)(2,1)S(1)} %multiply_convert_fusion.4), channel_id=1, source_target_pairs={{0,2},{2,0},{1,3},{3,1},{4,6},{6,4},{5,7},{7,5},{8,10},{10,8},{9,1... | collective-permute-start | bytes 2359304 | tf_op jit(solution)/shard_map/ppermute | solution.py:22
  137.1 4.1 collective-permute-start.4
  157.3 20.7 %collective-permute-start.5 = (bf16[1,512,768]{2,1,0:T(8,128)(2,1)}, bf16[1,512,768]{2,1,0:T(8,128)(2,1)}, u32[]{:S(2)}, u32[]{:S(2)}) collective-permute-start(bf16[1,512,768]{2,1,0:T(8,128)(2,1)} %fusion.57), channel_id=1, source_target_pairs={{0,1},{1,0},{2,3},{3,2},{4,5},{5,4},{6,7},{7,6},{8,9},{9,8},{10,11... | collective-permute-start | bytes 2359304 | tf_op jit(solution)/shard_map/ppermute | solution.py:22
  158.8 36.1 %collective-permute-start.12 = (bf16[1,512,768]{2,1,0:T(8,128)(2,1)}, bf16[1,512,768]{2,1,0:T(8,128)(2,1)}, u32[]{:S(2)}, u32[]{:S(2)}) collective-permute-start(bf16[1,512,768]{2,1,0:T(8,128)(2,1)} %bitcast.59), channel_id=1, source_target_pairs={{0,1},{1,0},{2,3},{3,2},{4,5},{5,4},{6,7},{7,6},{8,9},{9,8},{10,11... | collective-permute-start | bytes 2359304 | tf_op jit(solution)/shard_map/ppermute | solution.py:22
  182.2 29.1 %collective-permute-start.6 = (bf16[1,512,768]{2,1,0:T(8,128)(2,1)}, bf16[1,512,768]{2,1,0:T(8,128)(2,1)}, u32[]{:S(2)}, u32[]{:S(2)}) collective-permute-start(bf16[1,512,768]{2,1,0:T(8,128)(2,1)} %multiply_convert_fusion.3), channel_id=1, source_target_pairs={{0,1},{1,0},{2,3},{3,2},{4,5},{5,4},{6,7},{7,6},{8,9},{9,8},{10,11... | collective-permute-start | bytes 2359304 | tf_op jit(solution)/shard_map/ppermute | solution.py:22
  224.5 19.1 %collective-permute-start.7 = (bf16[1,512,768]{2,1,0:T(8,128)(2,1)S(1)}, bf16[1,512,768]{2,1,0:T(8,128)(2,1)S(1)}, u32[]{:S(2)}, u32[]{:S(2)}) collective-permute-start(bf16[1,512,768]{2,1,0:T(8,128)(2,1)S(1)} %fusion.58), channel_id=1, source_target_pairs={{0,1},{1,0},{2,3},{3,2},{4,5},{5,4},{6,7},{7,6},{8,9},{9,8},{10,11... | collective-permute-start | bytes 2359304 | tf_op jit(solution)/shard_map/ppermute | solution.py:22
  273.2 4.1 collective-permute-start.8
  287.2 4.3 collective-permute-start.10
  290.5 25.2 %collective-permute-start.9 = (f32[16,768]{1,0:T(8,128)}, f32[16,768]{1,0:T(8,128)}, u32[]{:S(2)}, u32[]{:S(2)}) collective-permute-start(f32[16,768]{1,0:T(8,128)} %fusion.316), channel_id=1, source_target_pairs={{0,1},{1,0},{2,3},{3,2},{4,5},{5,4},{6,7},{7,6},{8,9},{9,8},{10,11... | collective-permute-start | bytes 147464 | tf_op jit(solution)/shard_map/ppermute | solution.py:22
  309.7 6.9 collective-permute-start.11
  333.9 23.1 %collective-permute-start.13 = (bf16[1,512,768]{2,1,0:T(8,128)(2,1)}, bf16[1,512,768]{2,1,0:T(8,128)(2,1)}, u32[]{:S(2)}, u32[]{:S(2)}) collective-permute-start(bf16[1,512,768]{2,1,0:T(8,128)(2,1)} %fusion.61), channel_id=1, source_target_pairs={{0,1},{1,0},{2,3},{3,2},{4,5},{5,4},{6,7},{7,6},{8,9},{9,8},{10,11... | collective-permute-start | bytes 2359304 | tf_op jit(solution)/shard_map/ppermute | solution.py:22
  353.9 279.9 %all-reduce.9.cloned.1.call-start = ((), (), s32[]{:S(2)}) async-start(), calls=%async_computation.1 | async-start | bytes 4718592 | tf_op jit(solution)/shard_map/psum | solution.py:581
  362.2 22.9 %collective-permute-start.14 = (bf16[1,512,768]{2,1,0:T(8,128)(2,1)}, bf16[1,512,768]{2,1,0:T(8,128)(2,1)}, u32[]{:S(2)}, u32[]{:S(2)}) collective-permute-start(bf16[1,512,768]{2,1,0:T(8,128)(2,1)} %get-tuple-element.140), channel_id=1, source_target_pairs={{0,1},{1,0},{2,3},{3,2},{4,5},{5,4},{6,7},{7,6},{8,9},{9,8},{10,11... | collective-permute-start | bytes 2359304 | tf_op jit(solution)/shard_map/ppermute | solution.py:22
  402.4 4.9 collective-permute-start.16
  405.0 11.2 %collective-permute-start.15 = (bf16[1,512,768]{2,1,0:T(8,128)(2,1)}, bf16[1,512,768]{2,1,0:T(8,128)(2,1)}, u32[]{:S(2)}, u32[]{:S(2)}) collective-permute-start(bf16[1,512,768]{2,1,0:T(8,128)(2,1)} %fusion.64), channel_id=1, source_target_pairs={{0,2},{2,0},{1,3},{3,1},{4,6},{6,4},{5,7},{7,5},{8,10},{10,8},{9,1... | collective-permute-start | bytes 2359304 | tf_op jit(solution)/shard_map/ppermute | solution.py:22
  408.9 19.9 %collective-permute-start.17 = (bf16[1,512,768]{2,1,0:T(8,128)(2,1)}, bf16[1,512,768]{2,1,0:T(8,128)(2,1)}, u32[]{:S(2)}, u32[]{:S(2)}) collective-permute-start(bf16[1,512,768]{2,1,0:T(8,128)(2,1)} %fusion.33), channel_id=1, source_target_pairs={{0,1},{1,0},{2,3},{3,2},{4,5},{5,4},{6,7},{7,6},{8,9},{9,8},{10,11... | collective-permute-start | bytes 2359304 | tf_op jit(solution)/shard_map/ppermute | solution.py:22
  434.1 24.1 %collective-permute-start.18 = (bf16[1,512,768]{2,1,0:T(8,128)(2,1)}, bf16[1,512,768]{2,1,0:T(8,128)(2,1)}, u32[]{:S(2)}, u32[]{:S(2)}) collective-permute-start(bf16[1,512,768]{2,1,0:T(8,128)(2,1)} %get-tuple-element.137), channel_id=1, source_target_pairs={{0,1},{1,0},{2,3},{3,2},{4,5},{5,4},{6,7},{7,6},{8,9},{9,8},{10,11... | collective-permute-start | bytes 2359304 | tf_op jit(solution)/shard_map/ppermute | solution.py:22
  477.2 156.6 %collective-permute-start.19 = (bf16[1,512,768]{2,1,0:T(8,128)(2,1)}, bf16[1,512,768]{2,1,0:T(8,128)(2,1)}, u32[]{:S(2)}, u32[]{:S(2)}) collective-permute-start(bf16[1,512,768]{2,1,0:T(8,128)(2,1)} %fusion.66), channel_id=1, source_target_pairs={{0,1},{1,0},{2,3},{3,2},{4,5},{5,4},{6,7},{7,6},{8,9},{9,8},{10,11... | collective-permute-start | bytes 2359304 | tf_op jit(solution)/shard_map/ppermute | solution.py:22
  522.5 248.1 %all-reduce.7.cloned.1.call-start = ((), (), s32[]{:S(2)}) async-start(), calls=%async_computation | async-start | bytes 4718592 | tf_op jit(solution)/shard_map/psum | solution.py:615
  (123 other events, 1075.2 us)
Sparse Core Ops, SparseCore 0:
  354.0 168.4 all-reduce.10
  526.1 107.6 all-reduce.8
  638.0 132.6 all-reduce.6

commit v3 on v2

--- a/solution.py
+++ b/solution.py
@@ -328,6 +328,33 @@
         query_grads.append(outs[0])
         held = list(outs[1:])
     return (query_grads, held[:parts], held[parts:])
+
+
+def act_back(before, rows, weight):
+    grad = product(rows, weight, "...d,fd->...f")
+    return jax.vjp(gelu_exact, before)[1](grad)[0].astype(jnp.bfloat16)
+
+
+def first_row(blocks, owners):
+    row = blocks[0][:, 0]
+    for block, owner in zip(blocks[1:], owners[1:]):
+        row = jnp.where(owner == 0, block[:, 0], row)
+    return row
+
+
+def clip_ring(rows):
+    count = lax.axis_size("dp")
+    return jnp.concatenate([rows] + [shifted(rows, "dp", step) for step in range(1, count)])
+
+
+def with_class(rows, class_rows):
+    return (rows.astype(jnp.float32) + class_rows).astype(jnp.bfloat16)
+
+
+def replaced(left, fresh, stale):
+    return product(
+        jnp.concatenate([left, -left]), jnp.concatenate([fresh, stale]), "ca,cb->ab"
+    )
 
 
 def project_rows(source, weight):
@@ -499,6 +526,21 @@
         [product(hidden, hidden_down[0], "csf,fd->csd") for hidden in hiddens]
     )
 
+    down_rows = grad_blocks
+    act_grads = [act_back(before, rows, hidden_down[0]) for before, rows in zip(befores, down_rows)]
+    hidden_norm_grad = own_sum(
+        [product(act_grad, hidden_up[0], "csf,df->csd") for act_grad in act_grads]
+    )
+    down_grad = sum(product(h, r, "csf,csd->fd") for h, r in zip(hiddens, down_rows))
+    up_grad = sum(product(b, g, "csd,csf->df") for b, g in zip(hidden_blocks, act_grads))
+    up_sum, down_sum = lax.psum(
+        (up_grad.astype(jnp.bfloat16), down_grad.astype(jnp.bfloat16)), "dp"
+    )
+    rows_first = [
+        first_row(blocks, owners) for blocks in (hidden_blocks, befores, grad_blocks)
+    ]
+    clip_firsts = [clip_ring(rows) for rows in rows_first]
+
     everyone = ("dp", "view", "mp")
     class_all = trade(third_rows[:, 0, :], everyone, False, 2)
     class_all = class_all.reshape(clip_total // clip_count, view_total, model_total, clip_count, D)
@@ -526,25 +568,15 @@
     view_pick = jnp.sum(class_grad * view_match[None, :, None], axis=1)
     own_class = jnp.sum(clip_match[:, :, None] * view_pick[:, None, :], axis=0)
 
-    third_grads = [
-        block.astype(jnp.float32).at[:, 0].add(own_class * (owner == 0).astype(jnp.float32))
-        for block, owner in zip(grad_blocks, owners)
-    ]
-    third_grad = third_grads[0]
-    down_rows = [block.astype(jnp.bfloat16) for block in third_grads]
-    act_grads = [
-        jax.vjp(gelu_exact, before)[1](product(rows, hidden_down[0], "csd,fd->csf"))[0].astype(
-            jnp.bfloat16
-        )
-        for before, rows in zip(befores, down_rows)
-    ]
-    hidden_norm_grad = own_sum(
-        [product(act_grad, hidden_up[0], "csf,df->csd") for act_grad in act_grads]
-    )
-    down_grad = sum(product(h, r, "csf,csd->fd") for h, r in zip(hiddens, down_rows))
-    up_grad = sum(product(b, g, "csd,csf->df") for b, g in zip(hidden_blocks, act_grads))
-    up_sum, down_sum = lax.psum(
-        (up_grad.astype(jnp.bfloat16), down_grad.astype(jnp.bfloat16)), "dp"
+    first_model = (model_index == 0).astype(jnp.float32)
+    third_grad = tokens_cotangent[:, 0].astype(jnp.float32)
+    third_grad = third_grad.at[:, 0].add(own_class * first_model)
+    true_act = act_back(
+        rows_first[1], with_class(rows_first[2], own_class), hidden_down[0]
+    )
+    true_term = whole_sum(product(true_act, hidden_up[0], "cf,df->cd"))
+    hidden_norm_grad = hidden_norm_grad.at[:, 0].set(
+        jnp.where(model_index == 0, true_term, hidden_norm_grad[:, 0])
     )
     rows_grad_hidden, gain_hidden_grad = layer_norm_back(
         hidden_norm_grad, unit_hidden, inverse_hidden, norm_hidden[0]
@@ -577,8 +609,6 @@
         ]
     )
     cross_low = (cross_project_grad.astype(jnp.bfloat16), cross_merge_grad.astype(jnp.bfloat16))
-    cross_low, (up_sum, down_sum) = lax.optimization_barrier((cross_low, (up_sum, down_sum)))
-    cross_project_sum, cross_merge_sum = lax.psum(cross_low, "dp")
     rows_grad_cross, gain_cross_grad = layer_norm_back(
         cross_norm_grad, unit_cross, inverse_cross, norm_cross[0]
     )
@@ -609,10 +639,23 @@
         ]
     )
     self_low = (self_project_grad.astype(jnp.bfloat16), self_merge_grad.astype(jnp.bfloat16))
-    self_low, (cross_project_sum, cross_merge_sum) = lax.optimization_barrier(
-        (self_low, (cross_project_sum, cross_merge_sum))
-    )
-    self_project_sum, self_merge_sum = lax.psum(self_low, "dp")
+    self_low, (up_sum, down_sum) = lax.optimization_barrier((self_low, (up_sum, down_sum)))
+    (cross_project_sum, cross_merge_sum), (self_project_sum, self_merge_sum) = lax.psum(
+        (cross_low, self_low), "dp"
+    )
+    clip_order = (data_index - jnp.arange(clip_total // clip_count)) % (clip_total // clip_count)
+    class_ring = jnp.take(view_pick.reshape(-1, clip_count, D), clip_order, axis=0).reshape(-1, D)
+    normed_firsts, before_firsts, raw_firsts = clip_firsts
+    true_firsts = with_class(raw_firsts, class_ring)
+    hidden_firsts = gelu_exact(before_firsts).astype(jnp.bfloat16)
+    down_sum = down_sum.astype(jnp.float32) + replaced(
+        hidden_firsts, true_firsts, raw_firsts
+    )
+    up_sum = up_sum.astype(jnp.float32) + replaced(
+        normed_firsts,
+        act_back(before_firsts, true_firsts, hidden_down[0]),
+        act_back(before_firsts, raw_firsts, hidden_down[0]),
+    )
     rows_grad_self, gain_self_grad = layer_norm_back(
         self_norm_grad, unit_self, inverse_self, norm_self[0]
     )
@@ -636,8 +679,8 @@
         self_merge_sum.astype(jnp.float32)[None],
         cross_project_sum.astype(jnp.float32)[None],
         cross_merge_sum.astype(jnp.float32)[None],
-        up_sum.astype(jnp.float32)[None],
-        down_sum.astype(jnp.float32)[None],
+        up_sum[None],
+        down_sum[None],
         gains[0][None],
         gains[1][None],
         gains[2][None],

time: 792 us -> 728 us (0.919)
  waiting for transfers between devices: 240 us -> 134 us
  starting transfers between devices: 20.1 us -> 55.6 us
    psum x2 -> x1, waiting for transfers between devices: 128 us -> 67.4 us  [shards(): lax.psum((cross_low, self_low), 'dp')]
    psum x1, waiting for transfers between devices: 40.1 us -> 0.01 us  [shards(): lax.psum((up_grad.astype(jnp.bfloat16), down_grad.astype(jnp.bfloat16)),...]
    ppermute x20 -> x42, starting transfers between devices: 19.7 us -> 55.3 us  [shifted(): return lax.ppermute(value, axis, pairs)]
    ppermute x20 -> x42, waiting for transfers between devices: 71.6 us -> 66.7 us  [shifted(): return lax.ppermute(value, axis, pairs)]
    dot_general x84 -> x90, matrix products: 177 us -> 180 us  [product(): return jnp.einsum(form, left, right, preferred_element_type=jnp.float32)]
  transfers between devices with their start and end apart: 23 -> 44, of which waited for: 13 -> 13; matrix products, arithmetic and copies ran while one was open for 22% -> 31% of each run, Pallas kernels for 20% -> 26%
where the time goes in v3:
time: 728 us; the launch traced here: 717 us
  Pallas kernels  244 us (34%)
  matrix products  180 us (25%)
  waiting for transfers between devices  134 us (18%)
  other arithmetic  60.4 us (8%)
  starting transfers between devices  55.6 us (8%)
  local copies, waits for them, and re-layouts  25.7 us (4%)
  between operations  17 us (2%)
    dot_general x90, matrix products, product(): return jnp.einsum(form, left, right, preferred_element_type=jnp.float32)  180 us
    pallas_call x6, Pallas kernels, trade(): pl.pallas_call(functools.partial(trade_kernel, axes, total, split), out_s...  144 us
    psum x1, waiting for transfers between devices, shards(): lax.psum((cross_low, self_low), 'dp')  67.4 us
    ppermute x42, waiting for transfers between devices, shifted(): return lax.ppermute(value, axis, pairs)  66.7 us
    ppermute x42, starting transfers between devices, shifted(): return lax.ppermute(value, axis, pairs)  55.3 us
    pallas_call x4, Pallas kernels, attend_back(): pl.pallas_call(functools.partial(attend_back_kernel, parts, min(CHUNK, le...  49.4 us
    pallas_call x4, Pallas kernels, attend(): pl.pallas_call(functools.partial(attend_kernel, parts, min(CHUNK, length)...  39.7 us
  transfers between devices with their start and end apart: 44, of which 13 were waited for; matrix products, arithmetic and copies ran while one was open for 31% of the time, Pallas kernels for 26%

profile of v3, /device:TPU:0, one launch (start us, length us, event | category | flops | bytes accessed | tf_op | source)
XLA Modules:
  0.0 717.0 jit_solution(17481656677767923800)
XLA Ops:
  8.0 20.9 %shard_map.349 = bf16[8,1,64,768]{3,2,1,0:T(8,128)(2,1)} custom-call(bf16[8,1,64,768]{3,2,1,0:T(8,128)(2,1)} %bitcast.578), custom_call_target="tpu_custom_call" | custom-call | tf_op jit(solution)/shard_map/pallas_call | solution.py:108
  34.7 22.7 %shard_map.351 = bf16[8,1,64,768]{3,2,1,0:T(8,128)(2,1)} custom-call(bf16[8,1,64,768]{3,2,1,0:T(8,128)(2,1)} %bitcast.581), custom_call_target="tpu_custom_call" | custom-call | tf_op jit(solution)/shard_map/pallas_call | solution.py:108
  72.0 9.0 %collective-permute-done = bf16[1,512,768]{2,1,0:T(8,128)(2,1)} collective-permute-done((bf16[1,512,768]{2,1,0:T(8,128)(2,1)}, bf16[1,512,768]{2,1,0:T(8,128)(2,1)}, u32[]{:S(2)}, u32[]{:S(2)}) %collective-permute-start) | collective-permute-done | bytes 786464 | tf_op jit(solution)/shard_map/ppermute | solution.py:22
  89.4 9.8 %shard_map.353 = (bf16[1,512,384]{2,1,0:T(8,128)(2,1)}, f32[1,3,2,512]{3,2,1,0:T(2,128)}) custom-call(bf16[1,512,384]{2,1,0:T(8,128)(2,1)} %fusion.88.query_ref, bf16[1,512,384]{2,1,0:T(8,128)(2,1)} %fusion.90.refs_0_, bf16[1,512,384]{2,1,0:T(8,128)(2,1)} %fusion.91.refs_1_, bf16[1,512,384]{2,1,0:T(8,128)(2,1)} %fusion.92.refs_2_, ...), custom_call_target="tpu_custom_call" | custom-call | tf_op jit(solution)/shard_map/pallas_call | solution.py:295
  105.8 10.0 %shard_map.352 = (bf16[1,512,384]{2,1,0:T(8,128)(2,1)}, f32[1,3,2,512]{3,2,1,0:T(2,128)}) custom-call(bf16[1,512,384]{2,1,0:T(8,128)(2,1)} %fusion.89.query_ref, bf16[1,512,384]{2,1,0:T(8,128)(2,1)} %fusion.90.refs_0_, bf16[1,512,384]{2,1,0:T(8,128)(2,1)} %fusion.91.refs_1_, bf16[1,512,384]{2,1,0:T(8,128)(2,1)} %fusion.92.refs_2_, ...), custom_call_target="tpu_custom_call" | custom-call | tf_op jit(solution)/shard_map/pallas_call | solution.py:295
  127.5 15.5 %collective-permute-done.3 = bf16[1,512,768]{2,1,0:T(8,128)(2,1)} collective-permute-done((bf16[1,512,768]{2,1,0:T(8,128)(2,1)}, bf16[1,512,768]{2,1,0:T(8,128)(2,1)}, u32[]{:S(2)}, u32[]{:S(2)}) %collective-permute-start.3) | collective-permute-done | bytes 786464 | tf_op jit(solution)/shard_map/ppermute | solution.py:22
  154.1 9.8 %shard_map.355 = (bf16[1,512,384]{2,1,0:T(8,128)(2,1)}, f32[1,3,2,512]{3,2,1,0:T(2,128)}) custom-call(bf16[1,512,384]{2,1,0:T(8,128)(2,1)} %fusion.86.query_ref, bf16[1,512,384]{2,1,0:T(8,128)(2,1)} %fusion.94.refs_0_, bf16[1,512,384]{2,1,0:T(8,128)(2,1)} %fusion.95.refs_1_, bf16[1,512,384]{2,1,0:T(8,128)(2,1)} %fusion.96.refs_2_, ...), custom_call_target="tpu_custom_call" | custom-call | tf_op jit(solution)/shard_map/pallas_call | solution.py:295
  170.1 8.4 %collective-permute-start.41 = (bf16[1,768]{1,0:T(2,128)(2,1)S(1)}, bf16[1,768]{1,0:T(2,128)(2,1)S(1)}, u32[]{:S(2)}, u32[]{:S(2)}) collective-permute-start(bf16[1,768]{1,0:T(2,128)(2,1)S(1)} %bitcast.589), channel_id=1, source_target_pairs={{0,28},{4,0},{8,4},{12,8},{16,12},{20,16},{24,20},{28,24},{1,29},{... | collective-permute-start | bytes 4616 | tf_op jit(solution)/shard_map/ppermute | solution.py:22
  198.0 10.0 %shard_map.354 = (bf16[1,512,384]{2,1,0:T(8,128)(2,1)}, f32[1,3,2,512]{3,2,1,0:T(2,128)}) custom-call(bf16[1,512,384]{2,1,0:T(8,128)(2,1)} %fusion.87.query_ref, bf16[1,512,384]{2,1,0:T(8,128)(2,1)} %fusion.94.refs_0_, bf16[1,512,384]{2,1,0:T(8,128)(2,1)} %fusion.95.refs_1_, bf16[1,512,384]{2,1,0:T(8,128)(2,1)} %fusion.96.refs_2_, ...), custom_call_target="tpu_custom_call" | custom-call | tf_op jit(solution)/shard_map/pallas_call | solution.py:295
  212.3 8.3 %multiply_convert_fusion.1 = (bf16[512,1536]{1,0:T(8,128)(2,1)S(1)}, f32[512,1536]{1,0:T(8,128)S(1)}, f32[512,1536]{1,0:T(8,128)S(1)}) fusion(bf16[1,768,1536]{2,1,0:T(8,128)(2,1)S(1)} %copy-done, bf16[1,512,768]{2,1,0:T(8,128)(2,1)S(1)} %multiply_convert_fusion.3), kind=kOutput, calls=%fused_computation.25 | convolution fusion | flops 1259077632 | bytes 11010048 | tf_op jit(solution)/shard_map/csd,df->csf/dot_general | solution.py:44
  233.1 8.7 %multiply_convert_fusion = (bf16[512,1536]{1,0:T(8,128)(2,1)S(1)}, f32[512,1536]{1,0:T(8,128)S(1)}, f32[512,1536]{1,0:T(8,128)S(1)}) fusion(bf16[1,768,1536]{2,1,0:T(8,128)(2,1)S(1)} %copy-done, bf16[1,512,768]{2,1,0:T(8,128)(2,1)S(1)} %collective-permute-done.6), kind=kOutput, calls=%fused_computation.12 | convolution fusion | flops 1259077632 | bytes 11010048 | tf_op jit(solution)/shard_map/csd,df->csf/dot_general | solution.py:44
  282.8 10.9 %collective-permute-done.7 = bf16[1,512,768]{2,1,0:T(8,128)(2,1)} collective-permute-done((bf16[1,512,768]{2,1,0:T(8,128)(2,1)}, bf16[1,512,768]{2,1,0:T(8,128)(2,1)}, u32[]{:S(2)}, u32[]{:S(2)}) %collective-permute-start.7) | collective-permute-done | bytes 786464 | tf_op jit(solution)/shard_map/ppermute | solution.py:22
  299.2 10.5 %shard_map.356 = f32[32,1,768]{2,1,0:T(1,128)} custom-call(f32[1,768]{1,0:T(1,128)} %slice_bitcast_fusion.1.source), custom_call_target="tpu_custom_call" | custom-call | tf_op jit(solution)/shard_map/pallas_call | solution.py:108
  385.6 12.4 %shard_map.357 = (bf16[1,512,384]{2,1,0:T(8,128)(2,1)}, f32[1,512,384]{2,1,0:T(8,128)}, f32[1,512,384]{2,1,0:T(8,128)}, f32[1,512,384]{2,1,0:T(8,128)}, f32[1,512,384]{2,1,0:T(8,128)}) custom-call(bf16[1,512,384]{2,1,0:T(8,128)(2,1)} %fusion.87.query_ref, bf16[1,512,384]{2,1,0:T(8,128)(2,1)} %fusion.98.grad_ref, ...), custom_call_target="tpu_custom_call" | custom-call | tf_op jit(solution)/shard_map/pallas_call | solution.py:316
  408.8 12.4 %shard_map.358 = (bf16[1,512,384]{2,1,0:T(8,128)(2,1)}, bf16[1,512,384]{2,1,0:T(8,128)(2,1)}, bf16[1,512,384]{2,1,0:T(8,128)(2,1)}, bf16[1,512,384]{2,1,0:T(8,128)(2,1)}, bf16[1,512,384]{2,1,0:T(8,128)(2,1)}) custom-call(bf16[1,512,384]{2,1,0:T(8,128)(2,1)} %fusion.86.query_ref, bf16[1,512,384]{2,1,0:T(8,128)(2,1)} %fusion.99.grad_ref, ...), custom_call_target="tpu_custom_call" | custom-call | tf_op jit(solution)/shard_map/pallas_call | solution.py:316
  437.2 12.5 %collective-permute-done.18 = bf16[1,512,768]{2,1,0:T(8,128)(2,1)S(1)} collective-permute-done((bf16[1,512,768]{2,1,0:T(8,128)(2,1)S(1)}, bf16[1,512,768]{2,1,0:T(8,128)(2,1)S(1)}, u32[]{:S(2)}, u32[]{:S(2)}) %collective-permute-start.18) | collective-permute-done | bytes 786464 | tf_op jit(solution)/shard_map/ppermute | solution.py:22
  457.5 12.4 %shard_map.359 = (bf16[1,512,384]{2,1,0:T(8,128)(2,1)}, f32[1,512,384]{2,1,0:T(8,128)}, f32[1,512,384]{2,1,0:T(8,128)}, f32[1,512,384]{2,1,0:T(8,128)}, f32[1,512,384]{2,1,0:T(8,128)}) custom-call(bf16[1,512,384]{2,1,0:T(8,128)(2,1)} %fusion.89.query_ref, bf16[1,512,384]{2,1,0:T(8,128)(2,1)} %fusion.100.grad_ref, ...), custom_call_target="tpu_custom_call" | custom-call | tf_op jit(solution)/shard_map/pallas_call | solution.py:316
  476.8 12.2 %shard_map.360 = (bf16[1,512,384]{2,1,0:T(8,128)(2,1)}, bf16[1,512,384]{2,1,0:T(8,128)(2,1)}, bf16[1,512,384]{2,1,0:T(8,128)(2,1)}, bf16[1,512,384]{2,1,0:T(8,128)(2,1)}, bf16[1,512,384]{2,1,0:T(8,128)(2,1)}) custom-call(bf16[1,512,384]{2,1,0:T(8,128)(2,1)} %fusion.88.query_ref, bf16[1,512,384]{2,1,0:T(8,128)(2,1)} %fusion.101.grad_ref, ...), custom_call_target="tpu_custom_call" | custom-call | tf_op jit(solution)/shard_map/pallas_call | solution.py:316
  522.1 9.1 %collective-permute-done.20 = bf16[1,512,768]{2,1,0:T(8,128)(2,1)S(1)} collective-permute-done((bf16[1,512,768]{2,1,0:T(8,128)(2,1)S(1)}, bf16[1,512,768]{2,1,0:T(8,128)(2,1)S(1)}, u32[]{:S(2)}, u32[]{:S(2)}) %collective-permute-start.20) | collective-permute-done | bytes 786464 | tf_op jit(solution)/shard_map/ppermute | solution.py:22
  534.6 33.1 %shard_map.361 = bf16[8,1,64,768]{3,2,1,0:T(8,128)(2,1)} custom-call(bf16[8,1,64,768]{3,2,1,0:T(8,128)(2,1)} %bitcast.586), custom_call_target="tpu_custom_call" | custom-call | tf_op jit(solution)/shard_map/pallas_call | solution.py:108
  567.7 5.7 shard_map.362
  573.5 33.6 %shard_map.363 = bf16[8,1,64,768]{3,2,1,0:T(8,128)(2,1)} custom-call(bf16[8,1,64,768]{3,2,1,0:T(8,128)(2,1)} %bitcast.580), custom_call_target="tpu_custom_call" | custom-call | tf_op jit(solution)/shard_map/pallas_call | solution.py:108
  607.7 22.8 %shard_map.364 = f32[16,3,768]{2,1,0:T(4,128)} custom-call(f32[3,768]{1,0:T(4,128)} %pad_maximum_fusion.2.source), custom_call_target="tpu_custom_call" | custom-call | tf_op jit(solution)/shard_map/pallas_call | solution.py:108
  635.0 67.4 %all-reduce.5.cloned.1.call-done = (bf16[1,3,768,384]{3,2,1,0:T(8,128)(2,1)}, bf16[1,384,768]{2,1,0:T(8,128)(2,1)}, bf16[1,3,768,384]{3,2,1,0:T(8,128)(2,1)}, bf16[1,384,768]{2,1,0:T(8,128)(2,1)}) async-done(((bf16[1,3,768,384]{3,2,1,0:T(8,128)(2,1)}, bf16[1,384,768]{2,1,0:T(8,128)(2,1)}, bf16[1,3,768,384]{3,2,1,0:T(8,128)(2,1)}, bf16[1,384,768]{2,1,0:T(8,128)(2,1)}), (bf16[1,3,768,384]{3,2,1,0:T(8,128)(2,1)}, ...) | async-done | bytes 4718608 | tf_op jit(solution)/shard_map/psum | solution.py:643
  (588 shorter events, 311.8 us)
Async XLA Ops:
  7.2 494.1 %all-reduce.7.cloned.1.call-start = ((), (), s32[]{:S(2)}) async-start(), calls=%async_computation.1 | async-start | bytes 9437184 | tf_op jit(solution)/shard_map/psum | solution.py:536
  63.9 17.1 %collective-permute-start = (bf16[1,512,768]{2,1,0:T(8,128)(2,1)}, bf16[1,512,768]{2,1,0:T(8,128)(2,1)}, u32[]{:S(2)}, u32[]{:S(2)}) collective-permute-start(bf16[1,512,768]{2,1,0:T(8,128)(2,1)} %multiply_convert_fusion.5), channel_id=1, source_target_pairs={{0,1},{1,0},{2,3},{3,2},{4,5},{5,4},{6,7},{7,6},{8,9},{9,8},{10,11... | collective-permute-start | bytes 2359304 | tf_op jit(solution)/shard_map/ppermute | solution.py:22
  101.9 16.3 %collective-permute-start.1 = (bf16[1,512,768]{2,1,0:T(8,128)(2,1)}, bf16[1,512,768]{2,1,0:T(8,128)(2,1)}, u32[]{:S(2)}, u32[]{:S(2)}) collective-permute-start(bf16[1,512,768]{2,1,0:T(8,128)(2,1)} %fusion.64), channel_id=1, source_target_pairs={{0,1},{1,0},{2,3},{3,2},{4,5},{5,4},{6,7},{7,6},{8,9},{9,8},{10,11... | collective-permute-start | bytes 2359304 | tf_op jit(solution)/shard_map/ppermute | solution.py:22
  122.3 20.7 %collective-permute-start.3 = (bf16[1,512,768]{2,1,0:T(8,128)(2,1)}, bf16[1,512,768]{2,1,0:T(8,128)(2,1)}, u32[]{:S(2)}, u32[]{:S(2)}) collective-permute-start(bf16[1,512,768]{2,1,0:T(8,128)(2,1)} %multiply_convert_fusion.4), channel_id=1, source_target_pairs={{0,1},{1,0},{2,3},{3,2},{4,5},{5,4},{6,7},{7,6},{8,9},{9,8},{10,11... | collective-permute-start | bytes 2359304 | tf_op jit(solution)/shard_map/ppermute | solution.py:22
  123.8 19.3 %collective-permute-start.2 = (bf16[1,512,768]{2,1,0:T(8,128)(2,1)}, bf16[1,512,768]{2,1,0:T(8,128)(2,1)}, u32[]{:S(2)}, u32[]{:S(2)}) collective-permute-start(bf16[1,512,768]{2,1,0:T(8,128)(2,1)} %multiply_convert_fusion.4), channel_id=1, source_target_pairs={{0,2},{2,0},{1,3},{3,1},{4,6},{6,4},{5,7},{7,5},{8,10},{10,8},{9,1... | collective-permute-start | bytes 2359304 | tf_op jit(solution)/shard_map/ppermute | solution.py:22
  123.8 45.6 %collective-permute-start.12 = (bf16[1,512,768]{2,1,0:T(8,128)(2,1)}, bf16[1,512,768]{2,1,0:T(8,128)(2,1)}, u32[]{:S(2)}, u32[]{:S(2)}) collective-permute-start(bf16[1,512,768]{2,1,0:T(8,128)(2,1)} %bitcast.59), channel_id=1, source_target_pairs={{0,1},{1,0},{2,3},{3,2},{4,5},{5,4},{6,7},{7,6},{8,9},{9,8},{10,11... | collective-permute-start | bytes 2359304 | tf_op jit(solution)/shard_map/ppermute | solution.py:22
  166.6 41.5 %collective-permute-start.5 = (bf16[1,512,768]{2,1,0:T(8,128)(2,1)}, bf16[1,512,768]{2,1,0:T(8,128)(2,1)}, u32[]{:S(2)}, u32[]{:S(2)}) collective-permute-start(bf16[1,512,768]{2,1,0:T(8,128)(2,1)} %fusion.65), channel_id=1, source_target_pairs={{0,1},{1,0},{2,3},{3,2},{4,5},{5,4},{6,7},{7,6},{8,9},{9,8},{10,11... | collective-permute-start | bytes 2359304 | tf_op jit(solution)/shard_map/ppermute | solution.py:22
  170.1 12.4 %collective-permute-start.41 = (bf16[1,768]{1,0:T(2,128)(2,1)S(1)}, bf16[1,768]{1,0:T(2,128)(2,1)S(1)}, u32[]{:S(2)}, u32[]{:S(2)}) collective-permute-start(bf16[1,768]{1,0:T(2,128)(2,1)S(1)} %bitcast.589), channel_id=1, source_target_pairs={{0,28},{4,0},{8,4},{12,8},{16,12},{20,16},{24,20},{28,24},{1,29},{... | collective-permute-start | bytes 4616 | tf_op jit(solution)/shard_map/ppermute | solution.py:22
  211.8 16.8 %collective-permute-start.6 = (bf16[1,512,768]{2,1,0:T(8,128)(2,1)S(1)}, bf16[1,512,768]{2,1,0:T(8,128)(2,1)S(1)}, u32[]{:S(2)}, u32[]{:S(2)}) collective-permute-start(bf16[1,512,768]{2,1,0:T(8,128)(2,1)S(1)} %multiply_convert_fusion.3), channel_id=1, source_target_pairs={{0,1},{1,0},{2,3},{3,2},{4,5},{5,4},{6,7},{7,6},{8,9},{9,8},{10,11... | collective-permute-start | bytes 2359304 | tf_op jit(solution)/shard_map/ppermute | solution.py:22
  228.7 25.6 %collective-permute-start.27 = (bf16[1,768]{1,0:T(2,128)(2,1)S(1)}, bf16[1,768]{1,0:T(2,128)(2,1)S(1)}, u32[]{:S(2)}, u32[]{:S(2)}) collective-permute-start(bf16[1,768]{1,0:T(2,128)(2,1)S(1)} %fusion.348), channel_id=1, source_target_pairs={{0,28},{4,0},{8,4},{12,8},{16,12},{20,16},{24,20},{28,24},{1,29},{... | collective-permute-start | bytes 4616 | tf_op jit(solution)/shard_map/ppermute | solution.py:22
  228.8 27.5 %collective-permute-start.26 = (bf16[1,768]{1,0:T(2,128)(2,1)S(1)}, bf16[1,768]{1,0:T(2,128)(2,1)S(1)}, u32[]{:S(2)}, u32[]{:S(2)}) collective-permute-start(bf16[1,768]{1,0:T(2,128)(2,1)S(1)} %fusion.348), channel_id=1, source_target_pairs={{0,24},{4,28},{8,0},{12,4},{16,8},{20,12},{24,16},{28,20},{1,25},{... | collective-permute-start | bytes 4616 | tf_op jit(solution)/shard_map/ppermute | solution.py:22
  228.8 28.9 %collective-permute-start.25 = (bf16[1,768]{1,0:T(2,128)(2,1)S(1)}, bf16[1,768]{1,0:T(2,128)(2,1)S(1)}, u32[]{:S(2)}, u32[]{:S(2)}) collective-permute-start(bf16[1,768]{1,0:T(2,128)(2,1)S(1)} %fusion.348), channel_id=1, source_target_pairs={{0,20},{4,24},{8,28},{12,0},{16,4},{20,8},{24,12},{28,16},{1,21},{... | collective-permute-start | bytes 4616 | tf_op jit(solution)/shard_map/ppermute | solution.py:22
  230.2 30.8 %collective-permute-start.24 = (bf16[1,768]{1,0:T(2,128)(2,1)S(1)}, bf16[1,768]{1,0:T(2,128)(2,1)S(1)}, u32[]{:S(2)}, u32[]{:S(2)}) collective-permute-start(bf16[1,768]{1,0:T(2,128)(2,1)S(1)} %fusion.348), channel_id=1, source_target_pairs={{0,16},{4,20},{8,24},{12,28},{16,0},{20,4},{24,8},{28,12},{1,17},{... | collective-permute-start | bytes 4616 | tf_op jit(solution)/shard_map/ppermute | solution.py:22
  233.1 28.5 %collective-permute-start.23 = (bf16[1,768]{1,0:T(2,128)(2,1)S(1)}, bf16[1,768]{1,0:T(2,128)(2,1)S(1)}, u32[]{:S(2)}, u32[]{:S(2)}) collective-permute-start(bf16[1,768]{1,0:T(2,128)(2,1)S(1)} %fusion.348), channel_id=1, source_target_pairs={{0,12},{4,16},{8,20},{12,24},{16,28},{20,0},{24,4},{28,8},{1,13},{... | collective-permute-start | bytes 4616 | tf_op jit(solution)/shard_map/ppermute | solution.py:22
  254.2 12.4 %collective-permute-start.22 = (bf16[1,768]{1,0:T(2,128)(2,1)S(1)}, bf16[1,768]{1,0:T(2,128)(2,1)S(1)}, u32[]{:S(2)}, u32[]{:S(2)}) collective-permute-start(bf16[1,768]{1,0:T(2,128)(2,1)S(1)} %fusion.348), channel_id=1, source_target_pairs={{0,8},{4,12},{8,16},{12,20},{16,24},{20,28},{24,0},{28,4},{1,9},{5... | collective-permute-start | bytes 4616 | tf_op jit(solution)/shard_map/ppermute | solution.py:22
  256.3 12.7 %collective-permute-start.21 = (bf16[1,768]{1,0:T(2,128)(2,1)S(1)}, bf16[1,768]{1,0:T(2,128)(2,1)S(1)}, u32[]{:S(2)}, u32[]{:S(2)}) collective-permute-start(bf16[1,768]{1,0:T(2,128)(2,1)S(1)} %fusion.348), channel_id=1, source_target_pairs={{0,4},{4,8},{8,12},{12,16},{16,20},{20,24},{24,28},{28,0},{1,5},{5... | collective-permute-start | bytes 4616 | tf_op jit(solution)/shard_map/ppermute | solution.py:22
  273.0 20.7 %collective-permute-start.7 = (bf16[1,512,768]{2,1,0:T(8,128)(2,1)}, bf16[1,512,768]{2,1,0:T(8,128)(2,1)}, u32[]{:S(2)}, u32[]{:S(2)}) collective-permute-start(bf16[1,512,768]{2,1,0:T(8,128)(2,1)} %fusion.66), channel_id=1, source_target_pairs={{0,1},{1,0},{2,3},{3,2},{4,5},{5,4},{6,7},{7,6},{8,9},{9,8},{10,11... | collective-permute-start | bytes 2359304 | tf_op jit(solution)/shard_map/ppermute | solution.py:22
  276.7 425.7 %all-reduce.5.cloned.1.call-start = ((), (), s32[]{:S(2)}) async-start(), calls=%async_computation | async-start | bytes 9437184 | tf_op jit(solution)/shard_map/psum | solution.py:643
  278.3 43.1 %collective-permute-start.13 = (bf16[1,512,768]{2,1,0:T(8,128)(2,1)}, bf16[1,512,768]{2,1,0:T(8,128)(2,1)}, u32[]{:S(2)}, u32[]{:S(2)}) collective-permute-start(bf16[1,512,768]{2,1,0:T(8,128)(2,1)} %fusion.69), channel_id=1, source_target_pairs={{0,1},{1,0},{2,3},{3,2},{4,5},{5,4},{6,7},{7,6},{8,9},{9,8},{10,11... | collective-permute-start | bytes 2359304 | tf_op jit(solution)/shard_map/ppermute | solution.py:22
  339.3 20.8 %collective-permute-start.9 = (f32[16,768]{1,0:T(8,128)}, f32[16,768]{1,0:T(8,128)}, u32[]{:S(2)}, u32[]{:S(2)}) collective-permute-start(f32[16,768]{1,0:T(8,128)} %fusion.369), channel_id=1, source_target_pairs={{0,1},{1,0},{2,3},{3,2},{4,5},{5,4},{6,7},{7,6},{8,9},{9,8},{10,11... | collective-permute-start | bytes 147464 | tf_op jit(solution)/shard_map/ppermute | solution.py:22
  384.6 21.8 %collective-permute-start.15 = (bf16[1,512,768]{2,1,0:T(8,128)(2,1)}, bf16[1,512,768]{2,1,0:T(8,128)(2,1)}, u32[]{:S(2)}, u32[]{:S(2)}) collective-permute-start(bf16[1,512,768]{2,1,0:T(8,128)(2,1)} %get-tuple-element.136), channel_id=1, source_target_pairs={{0,1},{1,0},{2,3},{3,2},{4,5},{5,4},{6,7},{7,6},{8,9},{9,8},{10,11... | collective-permute-start | bytes 2359304 | tf_op jit(solution)/shard_map/ppermute | solution.py:22
  429.9 19.8 %collective-permute-start.18 = (bf16[1,512,768]{2,1,0:T(8,128)(2,1)S(1)}, bf16[1,512,768]{2,1,0:T(8,128)(2,1)S(1)}, u32[]{:S(2)}, u32[]{:S(2)}) collective-permute-start(bf16[1,512,768]{2,1,0:T(8,128)(2,1)S(1)} %fusion.41), channel_id=1, source_target_pairs={{0,1},{1,0},{2,3},{3,2},{4,5},{5,4},{6,7},{7,6},{8,9},{9,8},{10,11... | collective-permute-start | bytes 2359304 | tf_op jit(solution)/shard_map/ppermute | solution.py:22
  452.6 21.7 %collective-permute-start.19 = (bf16[1,512,768]{2,1,0:T(8,128)(2,1)}, bf16[1,512,768]{2,1,0:T(8,128)(2,1)}, u32[]{:S(2)}, u32[]{:S(2)}) collective-permute-start(bf16[1,512,768]{2,1,0:T(8,128)(2,1)} %get-tuple-element.133), channel_id=1, source_target_pairs={{0,1},{1,0},{2,3},{3,2},{4,5},{5,4},{6,7},{7,6},{8,9},{9,8},{10,11... | collective-permute-start | bytes 2359304 | tf_op jit(solution)/shard_map/ppermute | solution.py:22
  512.3 18.9 %collective-permute-start.20 = (bf16[1,512,768]{2,1,0:T(8,128)(2,1)S(1)}, bf16[1,512,768]{2,1,0:T(8,128)(2,1)S(1)}, u32[]{:S(2)}, u32[]{:S(2)}) collective-permute-start(bf16[1,512,768]{2,1,0:T(8,128)(2,1)S(1)} %fusion.74), channel_id=1, source_target_pairs={{0,1},{1,0},{2,3},{3,2},{4,5},{5,4},{6,7},{7,6},{8,9},{9,8},{10,11... | collective-permute-start | bytes 2359304 | tf_op jit(solution)/shard_map/ppermute | solution.py:22
  (162 other events, 1424.5 us)
Sparse Core Ops, SparseCore 0:
  276.8 170.9 all-reduce.6
  501.6 200.7 all-reduce.4

commit v4 on v3

--- a/solution.py
+++ b/solution.py
@@ -282,7 +282,11 @@
     return pl.BlockSpec((length, 2 * HEAD), lambda clip, pair: (0, 0))
 
 
-CHUNK = 256
+CHUNK = 512
+
+
+def piece_count(step, length):
+    return 2 if step > 0 and length % CHUNK == 0 else 1
 
 
 def attend(queries, keys, values, bias):
@@ -292,17 +296,45 @@
     heads = [None] * parts
     sums = [None] * parts
     for j in far_first(parts):
-        heads[j], sums[j] = pl.pallas_call(
-            functools.partial(attend_kernel, parts, min(CHUNK, length)),
-            grid=(clips, pairs),
-            out_shape=(
-                jax.ShapeDtypeStruct((clips, length, width), jnp.bfloat16),
-                jax.ShapeDtypeStruct((clips, pairs, 2, length), jnp.float32),
-            ),
-            in_specs=[pair_spec(length)] * (1 + 2 * parts) + [bias_spec(parts * length)],
-            out_specs=(pair_spec(length), sums_spec(length)),
-        )(queries[j], *keys, *values, bias)
+        count = piece_count(j, length)
+        rows = length // count
+        pieces = [
+            pl.pallas_call(
+                functools.partial(attend_kernel, parts, min(CHUNK, rows)),
+                grid=(clips, pairs),
+                out_shape=(
+                    jax.ShapeDtypeStruct((clips, rows, width), jnp.bfloat16),
+                    jax.ShapeDtypeStruct((clips, pairs, 2, rows), jnp.float32),
+                ),
+                in_specs=[
+                    pl.BlockSpec(
+                        (1, rows, 2 * HEAD), lambda clip, pair, place=place: (clip, place, pair)
+                    )
+                ]
+                + [pair_spec(length)] * (2 * parts)
+                + [bias_spec(parts * length)],
+                out_specs=(pair_spec(rows), sums_spec(rows)),
+            )(queries[j], *keys, *values, bias)
+            for place in range(count)
+        ]
+        heads[j] = [piece[0] for piece in pieces]
+        sums[j] = jnp.concatenate([piece[1] for piece in pieces], -1)
     return (heads, sums)
+
+
+def merge_sum(heads, weight):
+    total = product(heads[0][0], weight, "cse,ed->csd")
+    for step in range(1, len(heads)):
+        pieces = [
+            shifted(product(piece, weight, "cse,ed->csd").astype(jnp.bfloat16), "mp", step)
+            for piece in heads[step]
+        ]
+        total = total + jnp.concatenate(pieces, 1).astype(jnp.float32)
+    return total
+
+
+def whole_heads(heads):
+    return [jnp.concatenate(pieces, 1) for pieces in heads]
 
 
 def attend_back(queries, keys, values, bias, grads, heads, sums):
@@ -342,11 +374,6 @@
     return row
 
 
-def clip_ring(rows):
-    count = lax.axis_size("dp")
-    return jnp.concatenate([rows] + [shifted(rows, "dp", step) for step in range(1, count)])
-
-
 def with_class(rows, class_rows):
     return (rows.astype(jnp.float32) + class_rows).astype(jnp.bfloat16)
 
@@ -396,17 +423,14 @@
     top_hidden = gelu_exact(top_before).astype(jnp.bfloat16)
     summary_final = summary_mid + whole_sum(product(top_hidden, use_down, "csf,fd->csd")[0])
     down_input = top_grad.astype(jnp.bfloat16)[None]
-    down_grad = product(top_hidden, down_input, "csf,csd->fd")
     act_grad = jax.vjp(gelu_exact, top_before)[1](product(down_input, use_down, "csd,fd->csf"))[
         0
     ].astype(jnp.bfloat16)
-    up_grad = product(mid_low, act_grad, "csd,csf->df")
     mid_rows_grad, last_gain_grad = layer_norm_back(
         whole_sum(product(act_grad, use_up, "csf,df->csd")[0]), mid_unit, mid_inverse, gain_last
     )
     mid_grad = top_grad + mid_rows_grad
     merge_input = mid_grad.astype(jnp.bfloat16)[None]
-    merge_grad = product(top_flat, merge_input, "cse,csd->ed")
     top_heads_grad = product(merge_input, use_merge, "csd,ed->cse").astype(jnp.bfloat16)
     query_grad, key_grad, value_grad = attend_block_back(
         split_heads(top_query),
@@ -420,9 +444,6 @@
     key_grad = merge_heads(key_grad).astype(jnp.bfloat16)
     value_grad = merge_heads(value_grad).astype(jnp.bfloat16)
     query_grad = query_grad * HEAD ** (-0.5)
-    project_grad = jnp.stack(
-        [product(top_low, grad, "csd,cse->de") for grad in (query_grad, key_grad, value_grad)]
-    )
     project_terms = (
         back_rows(query_grad, use_project[0])
         + back_rows(key_grad, use_project[1])
@@ -435,7 +456,14 @@
     return (
         summary_final,
         class_grad,
-        (project_grad, merge_grad, up_grad, down_grad),
+        (
+            (top_low, query_grad),
+            (top_low, key_grad),
+            (top_low, value_grad),
+            (top_flat, merge_input),
+            (mid_low, act_grad),
+            (top_hidden, down_input),
+        ),
         top_gain_grad,
         last_gain_grad,
     )
@@ -498,9 +526,8 @@
         project_rows(block, self_weights[2]).astype(jnp.bfloat16) for block in self_blocks
     ]
     self_heads, self_sums = attend(self_queries, self_keys, self_values, own_bias)
-    first_rows = mixed_rows + own_sum(
-        [product(heads, self_merge[0], "cse,ed->csd") for heads in self_heads]
-    )
+    first_rows = mixed_rows + merge_sum(self_heads, self_merge[0])
+    self_heads = whole_heads(self_heads)
 
     normed_cross, unit_cross, inverse_cross = layer_norm(first_rows, norm_cross[0])
     cross_blocks = row_blocks(normed_cross.astype(jnp.bfloat16))
@@ -514,12 +541,17 @@
         project_rows(block, cross_weights[2]).astype(jnp.bfloat16) for block in next_blocks
     ]
     cross_heads, cross_sums = attend(cross_queries, cross_keys, cross_values, next_bias)
-    second_rows = first_rows + own_sum(
-        [product(heads, cross_merge[0], "cse,ed->csd") for heads in cross_heads]
-    )
+    second_rows = first_rows + merge_sum(cross_heads, cross_merge[0])
+    cross_heads = whole_heads(cross_heads)
 
     normed_hidden, unit_hidden, inverse_hidden = layer_norm(second_rows, norm_hidden[0])
     hidden_blocks = row_blocks(normed_hidden.astype(jnp.bfloat16))
+    normed_first = first_row(hidden_blocks, owners)
+    before_first = product(normed_first, hidden_up[0], "cd,df->cf")
+    raw_first = first_row(grad_blocks, owners)
+    class_term = whole_sum(
+        product(gelu_exact(before_first).astype(jnp.bfloat16), hidden_down[0], "cf,fd->cd")
+    )
     befores = [product(block, hidden_up[0], "csd,df->csf") for block in hidden_blocks]
     hiddens = [gelu_exact(before).astype(jnp.bfloat16) for before in befores]
     third_rows = second_rows + own_sum(
@@ -536,19 +568,14 @@
     up_sum, down_sum = lax.psum(
         (up_grad.astype(jnp.bfloat16), down_grad.astype(jnp.bfloat16)), "dp"
     )
-    rows_first = [
-        first_row(blocks, owners) for blocks in (hidden_blocks, befores, grad_blocks)
-    ]
-    clip_firsts = [clip_ring(rows) for rows in rows_first]
-
     everyone = ("dp", "view", "mp")
-    class_all = trade(third_rows[:, 0, :], everyone, False, 2)
+    class_all = trade(second_rows[:, 0] + class_term, everyone, False, 2)
     class_all = class_all.reshape(clip_total // clip_count, view_total, model_total, clip_count, D)
     class_grid = jnp.swapaxes(class_all[:, :, 0], 1, 2).reshape(clip_total, view_total, D)
     row_total = clip_total * view_total
     token_video = jnp.repeat(video_ids, view_total)
     summary_valid = (token_video[:, None] == token_video[None, :])[None, None]
-    summary_final, class_flat, summary_grads, summary_norm_self_grad, summary_norm_hidden_grad = (
+    summary_final, class_flat, summary_pairs, summary_norm_self_grad, summary_norm_hidden_grad = (
         summary_layer(
             class_grid.reshape(row_total, D),
             summary_cotangent.reshape(row_total, D),
@@ -558,7 +585,6 @@
             summary_valid,
         )
     )
-    summary_project_grad, summary_merge_grad, summary_up_grad, summary_down_grad = summary_grads
     summary_out = summary_final.reshape(clip_total, view_total, D)
     clip_match = (jnp.arange(clip_total, dtype=jnp.int32)[:, None] == own_clips[None, :]).astype(
         jnp.float32
@@ -571,9 +597,7 @@
     first_model = (model_index == 0).astype(jnp.float32)
     third_grad = tokens_cotangent[:, 0].astype(jnp.float32)
     third_grad = third_grad.at[:, 0].add(own_class * first_model)
-    true_act = act_back(
-        rows_first[1], with_class(rows_first[2], own_class), hidden_down[0]
-    )
+    true_act = act_back(before_first, with_class(raw_first, own_class), hidden_down[0])
     true_term = whole_sum(product(true_act, hidden_up[0], "cf,df->cd"))
     hidden_norm_grad = hidden_norm_grad.at[:, 0].set(
         jnp.where(model_index == 0, true_term, hidden_norm_grad[:, 0])
@@ -643,10 +667,27 @@
     (cross_project_sum, cross_merge_sum), (self_project_sum, self_merge_sum) = lax.psum(
         (cross_low, self_low), "dp"
     )
-    clip_order = (data_index - jnp.arange(clip_total // clip_count)) % (clip_total // clip_count)
-    class_ring = jnp.take(view_pick.reshape(-1, clip_count, D), clip_order, axis=0).reshape(-1, D)
-    normed_firsts, before_firsts, raw_firsts = clip_firsts
-    true_firsts = with_class(raw_firsts, class_ring)
+    rows_grad_self, gain_self_grad = layer_norm_back(
+        self_norm_grad, unit_self, inverse_self, norm_self[0]
+    )
+    mixed_grad = first_grad + rows_grad_self
+    summary_pairs, mixed_grad = lax.optimization_barrier((summary_pairs, mixed_grad))
+    summary_grads = [product(left, right, "csd,cse->de") for left, right in summary_pairs]
+    summary_project_grad = jnp.stack(summary_grads[:3])
+    summary_merge_grad, summary_up_grad, summary_down_grad = summary_grads[3:]
+    gains = jnp.stack([gain_self_grad, gain_cross_grad, gain_hidden_grad])
+    firsts = jnp.concatenate(
+        [normed_first.astype(jnp.float32), raw_first.astype(jnp.float32), before_first], 1
+    ).reshape(-1, D)
+    shared = trade(jnp.concatenate([gains, firsts]), ("dp", "mp"), False, 3)
+    gains = jnp.sum(shared[:, :3], 0)
+    clip_firsts = shared.reshape((-1, model_total) + shared.shape[1:])
+    clip_firsts = lax.dynamic_index_in_dim(clip_firsts, model_index, 1, False)[:, 3:]
+    clip_firsts = clip_firsts.reshape(clip_total, -1)
+    normed_firsts = clip_firsts[:, :D].astype(jnp.bfloat16)
+    raw_firsts = clip_firsts[:, D : 2 * D].astype(jnp.bfloat16)
+    before_firsts = clip_firsts[:, 2 * D :]
+    true_firsts = with_class(raw_firsts, view_pick)
     hidden_firsts = gelu_exact(before_firsts).astype(jnp.bfloat16)
     down_sum = down_sum.astype(jnp.float32) + replaced(
         hidden_firsts, true_firsts, raw_firsts
@@ -656,12 +697,6 @@
         act_back(before_firsts, true_firsts, hidden_down[0]),
         act_back(before_firsts, raw_firsts, hidden_down[0]),
     )
-    rows_grad_self, gain_self_grad = layer_norm_back(
-        self_norm_grad, unit_self, inverse_self, norm_self[0]
-    )
-    mixed_grad = first_grad + rows_grad_self
-    gains = jnp.stack([gain_self_grad, gain_cross_grad, gain_hidden_grad])
-    gains = jnp.sum(trade(gains, ("dp", "mp"), False, 3), 0)
 
     sent_rows = ((1.0 - mixing) * mixed_grad).astype(jnp.bfloat16)
     clips = jnp.arange(clip_total, dtype=jnp.int32)

time: 728 us -> 703 us (0.966)
  starting transfers between devices: 55.6 us -> 21.8 us
  Pallas kernels: 244 us -> 272 us
  waiting for transfers between devices: 134 us -> 121 us
  matrix products: 180 us -> 172 us
    ppermute x42 -> x24, starting transfers between devices: 55.3 us -> 21.5 us  [shifted(): return lax.ppermute(value, axis, pairs)]
    pallas_call x6, Pallas kernels: 144 us -> 169 us  [trade(): pl.pallas_call(functools.partial(trade_kernel, axes, total, split), out_s...]
    ppermute x42 -> x24, waiting for transfers between devices: 66.7 us -> 48.1 us  [shifted(): return lax.ppermute(value, axis, pairs)]
    dot_general x90 -> x94, matrix products: 180 us -> 172 us  [product(): return jnp.einsum(form, left, right, preferred_element_type=jnp.float32)]
    pallas_call x4 -> x6, Pallas kernels: 39.7 us -> 43.3 us  [attend(): pl.pallas_call(functools.partial(attend_kernel, parts, min(CHUNK, rows)),...]
  transfers between devices with their start and end apart: 44 -> 26, of which waited for: 13 -> 10; matrix products, arithmetic and copies ran while one was open for 31% -> 33% of each run, Pallas kernels for 26% -> 37%
where the time goes in v4:
time: 703 us; the launch traced here: 693 us
  Pallas kernels  272 us (39%)
  matrix products  172 us (24%)
  waiting for transfers between devices  121 us (17%)
  other arithmetic  62.2 us (9%)
  local copies, waits for them, and re-layouts  27.2 us (4%)
  starting transfers between devices  21.8 us (3%)
  between operations  17 us (2%)
    dot_general x94, matrix products, product(): return jnp.einsum(form, left, right, preferred_element_type=jnp.float32)  172 us
    pallas_call x6, Pallas kernels, trade(): pl.pallas_call(functools.partial(trade_kernel, axes, total, split), out_s...  169 us
    psum x1, waiting for transfers between devices, shards(): lax.psum((cross_low, self_low), 'dp')  72.8 us
    ppermute x24, waiting for transfers between devices, shifted(): return lax.ppermute(value, axis, pairs)  48.1 us
    pallas_call x4, Pallas kernels, attend_back(): pl.pallas_call(functools.partial(attend_back_kernel, parts, min(CHUNK, le...  47.8 us
    pallas_call x6, Pallas kernels, attend(): pl.pallas_call(functools.partial(attend_kernel, parts, min(CHUNK, rows)),...  43.3 us
    ppermute x24, starting transfers between devices, shifted(): return lax.ppermute(value, axis, pairs)  21.5 us
  transfers between devices with their start and end apart: 26, of which 10 were waited for; matrix products, arithmetic and copies ran while one was open for 33% of the time, Pallas kernels for 37%

profile of v4, /device:TPU:0, one launch (start us, length us, event | category | flops | bytes accessed | tf_op | source)
XLA Modules:
  0.0 692.8 jit_solution(5335905052570360427)
XLA Ops:
  11.0 19.2 %shard_map.349 = bf16[8,1,64,768]{3,2,1,0:T(8,128)(2,1)} custom-call(bf16[8,1,64,768]{3,2,1,0:T(8,128)(2,1)} %bitcast.661), custom_call_target="tpu_custom_call" | custom-call | tf_op jit(solution)/shard_map/pallas_call | solution.py:108
  30.1 5.7 shard_map.350
  35.9 22.7 %shard_map.351 = bf16[8,1,64,768]{3,2,1,0:T(8,128)(2,1)} custom-call(bf16[8,1,64,768]{3,2,1,0:T(8,128)(2,1)} %bitcast.669), custom_call_target="tpu_custom_call" | custom-call | tf_op jit(solution)/shard_map/pallas_call | solution.py:108
  75.9 6.3 collective-permute-done
  90.6 6.3 shard_map.354
  96.9 6.3 shard_map.353
  111.7 8.9 %shard_map.352 = (bf16[1,512,384]{2,1,0:T(8,128)(2,1)}, f32[1,3,2,512]{3,2,1,0:T(2,128)}) custom-call(bf16[1,512,384]{2,1,0:T(8,128)(2,1)} %fusion.102.query_ref, bf16[1,512,384]{2,1,0:T(8,128)(2,1)} %fusion.107.refs_0_, bf16[1,512,384]{2,1,0:T(8,128)(2,1)} %fusion.108.refs_1_, bf16[1,512,384]{2,1,0:T(8,128)(2,1)} %fusion.109.refs_2_, ...), custom_call_target="tpu_custom_call" | custom-call | tf_op jit(solution)/shard_map/pallas_call | solution.py:302
  130.6 12.2 %collective-permute-done.4 = bf16[1,512,768]{2,1,0:T(8,128)(2,1)S(1)} collective-permute-done((bf16[1,512,768]{2,1,0:T(8,128)(2,1)S(1)}, bf16[1,512,768]{2,1,0:T(8,128)(2,1)S(1)}, u32[]{:S(2)}, u32[]{:S(2)}) %collective-permute-start.4) | collective-permute-done | bytes 786464 | tf_op jit(solution)/shard_map/ppermute | solution.py:22
  151.7 6.3 shard_map.357
  158.0 6.3 shard_map.356
  173.3 9.1 %shard_map.355 = (bf16[1,512,384]{2,1,0:T(8,128)(2,1)}, f32[1,3,2,512]{3,2,1,0:T(2,128)}) custom-call(bf16[1,512,384]{2,1,0:T(8,128)(2,1)} %fusion.100.query_ref, bf16[1,512,384]{2,1,0:T(8,128)(2,1)} %fusion.111.refs_0_, bf16[1,512,384]{2,1,0:T(8,128)(2,1)} %fusion.112.refs_1_, bf16[1,512,384]{2,1,0:T(8,128)(2,1)} %fusion.113.refs_2_, ...), custom_call_target="tpu_custom_call" | custom-call | tf_op jit(solution)/shard_map/pallas_call | solution.py:302
  193.1 7.8 %multiply_convert_fusion.1 = (bf16[512,1536]{1,0:T(8,128)(2,1)S(1)}, f32[512,1536]{1,0:T(8,128)S(1)}, f32[512,1536]{1,0:T(8,128)S(1)}) fusion(bf16[1,768,1536]{2,1,0:T(8,128)(2,1)S(1)} %copy-done, f32[512,768]{1,0:T(8,128)S(1)} %get-tuple-element.202, f32[768]{0:T(1024)S(1)} %reduce.45, f32[512]{0:T(512)S(1)} %add_rsqrt_fusion.2, ...), kind=kOutput, calls=%fused_computation.24 | convolution fusion | flops 1260650496 | bytes 11803648 | tf_op jit(solution)/shard_map/csd,df->csf/dot_general | solution.py:44
  216.9 8.3 %multiply_convert_fusion = (bf16[512,1536]{1,0:T(8,128)(2,1)S(1)}, f32[512,1536]{1,0:T(8,128)S(1)}, f32[512,1536]{1,0:T(8,128)S(1)}) fusion(bf16[1,768,1536]{2,1,0:T(8,128)(2,1)S(1)} %copy-done, bf16[1,512,768]{2,1,0:T(8,128)(2,1)S(1)} %copy-done.68), kind=kOutput, calls=%fused_computation.11 | convolution fusion | flops 1259077632 | bytes 11010048 | tf_op jit(solution)/shard_map/csd,df->csf/dot_general | solution.py:44
  243.9 27.1 %shard_map.358 = f32[32,1,768]{2,1,0:T(1,128)} custom-call(f32[1,768]{1,0:T(1,128)} %fusion.382.source), custom_call_target="tpu_custom_call" | custom-call | tf_op jit(solution)/shard_map/pallas_call | solution.py:108
  340.8 11.8 %shard_map.359 = (bf16[1,512,384]{2,1,0:T(8,128)(2,1)}, f32[1,512,384]{2,1,0:T(8,128)}, f32[1,512,384]{2,1,0:T(8,128)}, f32[1,512,384]{2,1,0:T(8,128)}, f32[1,512,384]{2,1,0:T(8,128)}) custom-call(bf16[1,512,384]{2,1,0:T(8,128)(2,1)} %fusion.100.query_ref, bf16[1,512,384]{2,1,0:T(8,128)(2,1)} %fusion.115.grad_ref, ...), custom_call_target="tpu_custom_call" | custom-call | tf_op jit(solution)/shard_map/pallas_call | solution.py:348
  366.0 12.6 %shard_map.360 = (bf16[1,512,384]{2,1,0:T(8,128)(2,1)}, bf16[1,512,384]{2,1,0:T(8,128)(2,1)}, bf16[1,512,384]{2,1,0:T(8,128)(2,1)}, bf16[1,512,384]{2,1,0:T(8,128)(2,1)}, bf16[1,512,384]{2,1,0:T(8,128)(2,1)}) custom-call(bf16[1,512,384]{2,1,0:T(8,128)(2,1)} %fusion.99.query_ref, bf16[1,512,384]{2,1,0:T(8,128)(2,1)} %fusion.116.grad_ref, ...), custom_call_target="tpu_custom_call" | custom-call | tf_op jit(solution)/shard_map/pallas_call | solution.py:348
  393.1 13.0 %collective-permute-done.21 = bf16[1,512,768]{2,1,0:T(8,128)(2,1)S(1)} collective-permute-done((bf16[1,512,768]{2,1,0:T(8,128)(2,1)S(1)}, bf16[1,512,768]{2,1,0:T(8,128)(2,1)S(1)}, u32[]{:S(2)}, u32[]{:S(2)}) %collective-permute-start.21) | collective-permute-done | bytes 786464 | tf_op jit(solution)/shard_map/ppermute | solution.py:22
  412.3 11.3 %shard_map.361 = (bf16[1,512,384]{2,1,0:T(8,128)(2,1)}, f32[1,512,384]{2,1,0:T(8,128)}, f32[1,512,384]{2,1,0:T(8,128)}, f32[1,512,384]{2,1,0:T(8,128)}, f32[1,512,384]{2,1,0:T(8,128)}) custom-call(bf16[1,512,384]{2,1,0:T(8,128)(2,1)} %fusion.102.query_ref, bf16[1,512,384]{2,1,0:T(8,128)(2,1)} %fusion.117.grad_ref, ...), custom_call_target="tpu_custom_call" | custom-call | tf_op jit(solution)/shard_map/pallas_call | solution.py:348
  433.3 12.1 %shard_map.362 = (bf16[1,512,384]{2,1,0:T(8,128)(2,1)}, bf16[1,512,384]{2,1,0:T(8,128)(2,1)}, bf16[1,512,384]{2,1,0:T(8,128)(2,1)}, bf16[1,512,384]{2,1,0:T(8,128)(2,1)}, bf16[1,512,384]{2,1,0:T(8,128)(2,1)}) custom-call(bf16[1,512,384]{2,1,0:T(8,128)(2,1)} %fusion.101.query_ref, bf16[1,512,384]{2,1,0:T(8,128)(2,1)} %fusion.118.grad_ref, ...), custom_call_target="tpu_custom_call" | custom-call | tf_op jit(solution)/shard_map/pallas_call | solution.py:348
  474.6 26.9 %shard_map.366 = f32[16,7,768]{2,1,0:T(8,128)} custom-call(f32[7,768]{1,0:T(8,128)} %pad_maximum_fusion.2.source), custom_call_target="tpu_custom_call" | custom-call | tf_op jit(solution)/shard_map/pallas_call | solution.py:108
  504.9 38.0 %shard_map.363 = bf16[8,1,64,768]{3,2,1,0:T(8,128)(2,1)} custom-call(bf16[8,1,64,768]{3,2,1,0:T(8,128)(2,1)} %bitcast.666), custom_call_target="tpu_custom_call" | custom-call | tf_op jit(solution)/shard_map/pallas_call | solution.py:108
  542.9 5.8 shard_map.364
  548.8 35.1 %shard_map.365 = bf16[8,1,64,768]{3,2,1,0:T(8,128)(2,1)} custom-call(bf16[8,1,64,768]{3,2,1,0:T(8,128)(2,1)} %bitcast.668), custom_call_target="tpu_custom_call" | custom-call | tf_op jit(solution)/shard_map/pallas_call | solution.py:108
  605.1 72.8 %all-reduce.5.cloned.1.call-done = (bf16[1,3,768,384]{3,2,1,0:T(8,128)(2,1)}, bf16[1,384,768]{2,1,0:T(8,128)(2,1)}, bf16[1,3,768,384]{3,2,1,0:T(8,128)(2,1)}, bf16[1,384,768]{2,1,0:T(8,128)(2,1)}) async-done(((bf16[1,3,768,384]{3,2,1,0:T(8,128)(2,1)}, bf16[1,384,768]{2,1,0:T(8,128)(2,1)}, bf16[1,3,768,384]{3,2,1,0:T(8,128)(2,1)}, bf16[1,384,768]{2,1,0:T(8,128)(2,1)}), (bf16[1,3,768,384]{3,2,1,0:T(8,128)(2,1)}, ...) | async-done | bytes 4718608 | tf_op jit(solution)/shard_map/psum | solution.py:667
  (556 shorter events, 283.8 us)
Async XLA Ops:
  7.2 462.7 %all-reduce.7.cloned.1.call-start = ((), (), s32[]{:S(2)}) async-start(), calls=%async_computation.1 | async-start | bytes 9437184 | tf_op jit(solution)/shard_map/psum | solution.py:568
  7.3 122.5 %collective-permute-start.15 = (bf16[1,512,768]{2,1,0:T(8,128)(2,1)}, bf16[1,512,768]{2,1,0:T(8,128)(2,1)}, u32[]{:S(2)}, u32[]{:S(2)}) collective-permute-start(bf16[1,512,768]{2,1,0:T(8,128)(2,1)} %bitcast.663), channel_id=1, source_target_pairs={{0,1},{1,0},{2,3},{3,2},{4,5},{5,4},{6,7},{7,6},{8,9},{9,8},{10,11... | collective-permute-start | bytes 2359304 | tf_op jit(solution)/shard_map/ppermute | solution.py:22
  65.1 17.1 %collective-permute-start = (bf16[1,512,768]{2,1,0:T(8,128)(2,1)}, bf16[1,512,768]{2,1,0:T(8,128)(2,1)}, u32[]{:S(2)}, u32[]{:S(2)}) collective-permute-start(bf16[1,512,768]{2,1,0:T(8,128)(2,1)} %multiply_convert_fusion.5), channel_id=1, source_target_pairs={{0,1},{1,0},{2,3},{3,2},{4,5},{5,4},{6,7},{7,6},{8,9},{9,8},{10,11... | collective-permute-start | bytes 2359304 | tf_op jit(solution)/shard_map/ppermute | solution.py:22
  107.8 12.8 %collective-permute-start.1 = (bf16[1,256,768]{2,1,0:T(8,128)(2,1)}, bf16[1,256,768]{2,1,0:T(8,128)(2,1)}, u32[]{:S(2)}, u32[]{:S(2)}) collective-permute-start(bf16[1,256,768]{2,1,0:T(8,128)(2,1)} %fusion.103), channel_id=1, source_target_pairs={{0,1},{1,0},{2,3},{3,2},{4,5},{5,4},{6,7},{7,6},{8,9},{9,8},{10,11... | collective-permute-start | bytes 1179656 | tf_op jit(solution)/shard_map/ppermute | solution.py:22
  108.5 15.6 %collective-permute-start.2 = (bf16[1,256,768]{2,1,0:T(8,128)(2,1)}, bf16[1,256,768]{2,1,0:T(8,128)(2,1)}, u32[]{:S(2)}, u32[]{:S(2)}) collective-permute-start(bf16[1,256,768]{2,1,0:T(8,128)(2,1)} %fusion.104), channel_id=1, source_target_pairs={{0,1},{1,0},{2,3},{3,2},{4,5},{5,4},{6,7},{7,6},{8,9},{9,8},{10,11... | collective-permute-start | bytes 1179656 | tf_op jit(solution)/shard_map/ppermute | solution.py:22
  127.6 15.2 %collective-permute-start.4 = (bf16[1,512,768]{2,1,0:T(8,128)(2,1)S(1)}, bf16[1,512,768]{2,1,0:T(8,128)(2,1)S(1)}, u32[]{:S(2)}, u32[]{:S(2)}) collective-permute-start(bf16[1,512,768]{2,1,0:T(8,128)(2,1)S(1)} %fusion.464), channel_id=1, source_target_pairs={{0,1},{1,0},{2,3},{3,2},{4,5},{5,4},{6,7},{7,6},{8,9},{9,8},{10,11... | collective-permute-start | bytes 2359304 | tf_op jit(solution)/shard_map/ppermute | solution.py:22
  129.0 14.9 %collective-permute-start.3 = (bf16[1,512,768]{2,1,0:T(8,128)(2,1)S(1)}, bf16[1,512,768]{2,1,0:T(8,128)(2,1)S(1)}, u32[]{:S(2)}, u32[]{:S(2)}) collective-permute-start(bf16[1,512,768]{2,1,0:T(8,128)(2,1)S(1)} %fusion.464), channel_id=1, source_target_pairs={{0,2},{2,0},{1,3},{3,1},{4,6},{6,4},{5,7},{7,5},{8,10},{10,8},{9,1... | collective-permute-start | bytes 2359304 | tf_op jit(solution)/shard_map/ppermute | solution.py:22
  142.8 5.2 collective-permute-start.5
  168.9 15.0 %collective-permute-start.6 = (bf16[1,256,768]{2,1,0:T(8,128)(2,1)}, bf16[1,256,768]{2,1,0:T(8,128)(2,1)}, u32[]{:S(2)}, u32[]{:S(2)}) collective-permute-start(bf16[1,256,768]{2,1,0:T(8,128)(2,1)} %fusion.105), channel_id=1, source_target_pairs={{0,1},{1,0},{2,3},{3,2},{4,5},{5,4},{6,7},{7,6},{8,9},{9,8},{10,11... | collective-permute-start | bytes 1179656 | tf_op jit(solution)/shard_map/ppermute | solution.py:22
  169.6 19.6 %collective-permute-start.7 = (bf16[1,256,768]{2,1,0:T(8,128)(2,1)}, bf16[1,256,768]{2,1,0:T(8,128)(2,1)}, u32[]{:S(2)}, u32[]{:S(2)}) collective-permute-start(bf16[1,256,768]{2,1,0:T(8,128)(2,1)} %fusion.106), channel_id=1, source_target_pairs={{0,1},{1,0},{2,3},{3,2},{4,5},{5,4},{6,7},{7,6},{8,9},{9,8},{10,11... | collective-permute-start | bytes 1179656 | tf_op jit(solution)/shard_map/ppermute | solution.py:22
  192.3 19.2 %collective-permute-start.8 = (bf16[1,512,768]{2,1,0:T(8,128)(2,1)S(1)}, bf16[1,512,768]{2,1,0:T(8,128)(2,1)S(1)}, u32[]{:S(2)}, u32[]{:S(2)}) collective-permute-start(bf16[1,512,768]{2,1,0:T(8,128)(2,1)S(1)} %fusion.463), channel_id=1, source_target_pairs={{0,1},{1,0},{2,3},{3,2},{4,5},{5,4},{6,7},{7,6},{8,9},{9,8},{10,11... | collective-permute-start | bytes 2359304 | tf_op jit(solution)/shard_map/ppermute | solution.py:22
  216.2 26.4 %collective-permute-start.10 = (f32[1,768]{1,0:T(1,128)S(1)}, f32[1,768]{1,0:T(1,128)S(1)}, u32[]{:S(2)}, u32[]{:S(2)}) collective-permute-start(f32[1,768]{1,0:T(1,128)S(1)} %fusion.22), channel_id=1, source_target_pairs={{0,1},{1,0},{2,3},{3,2},{4,5},{5,4},{6,7},{7,6},{8,9},{9,8},{10,11... | collective-permute-start | bytes 9224 | tf_op jit(solution)/shard_map/ppermute | solution.py:22
  233.2 126.8 %collective-permute-start.9 = (bf16[1,512,768]{2,1,0:T(8,128)(2,1)}, bf16[1,512,768]{2,1,0:T(8,128)(2,1)}, u32[]{:S(2)}, u32[]{:S(2)}) collective-permute-start(bf16[1,512,768]{2,1,0:T(8,128)(2,1)} %fusion.76), channel_id=1, source_target_pairs={{0,1},{1,0},{2,3},{3,2},{4,5},{5,4},{6,7},{7,6},{8,9},{9,8},{10,11... | collective-permute-start | bytes 2359304 | tf_op jit(solution)/shard_map/ppermute | solution.py:22
  234.6 90.9 %collective-permute-start.16 = (bf16[1,512,768]{2,1,0:T(8,128)(2,1)}, bf16[1,512,768]{2,1,0:T(8,128)(2,1)}, u32[]{:S(2)}, u32[]{:S(2)}) collective-permute-start(bf16[1,512,768]{2,1,0:T(8,128)(2,1)} %fusion.79), channel_id=1, source_target_pairs={{0,1},{1,0},{2,3},{3,2},{4,5},{5,4},{6,7},{7,6},{8,9},{9,8},{10,11... | collective-permute-start | bytes 2359304 | tf_op jit(solution)/shard_map/ppermute | solution.py:22
  242.3 435.6 %all-reduce.5.cloned.1.call-start = ((), (), s32[]{:S(2)}) async-start(), calls=%async_computation | async-start | bytes 9437184 | tf_op jit(solution)/shard_map/psum | solution.py:667
  290.4 4.4 collective-permute-start.13
  293.3 19.4 %collective-permute-start.12 = (f32[16,768]{1,0:T(8,128)}, f32[16,768]{1,0:T(8,128)}, u32[]{:S(2)}, u32[]{:S(2)}) collective-permute-start(f32[16,768]{1,0:T(8,128)} %fusion.402), channel_id=1, source_target_pairs={{0,1},{1,0},{2,3},{3,2},{4,5},{5,4},{6,7},{7,6},{8,9},{9,8},{10,11... | collective-permute-start | bytes 147464 | tf_op jit(solution)/shard_map/ppermute | solution.py:22
  305.6 8.0 %collective-permute-start.14 = (f32[16,768]{1,0:T(8,128)}, f32[16,768]{1,0:T(8,128)}, u32[]{:S(2)}, u32[]{:S(2)}) collective-permute-start(f32[16,768]{1,0:T(8,128)} %convolution_add_fusion.8), channel_id=1, source_target_pairs={{0,1},{1,0},{2,3},{3,2},{4,5},{5,4},{6,7},{7,6},{8,9},{9,8},{10,11... | collective-permute-start | bytes 147464 | tf_op jit(solution)/shard_map/ppermute | solution.py:22
  323.8 4.7 collective-permute-start.17
  339.8 23.7 %collective-permute-start.18 = (bf16[1,512,768]{2,1,0:T(8,128)(2,1)}, bf16[1,512,768]{2,1,0:T(8,128)(2,1)}, u32[]{:S(2)}, u32[]{:S(2)}) collective-permute-start(bf16[1,512,768]{2,1,0:T(8,128)(2,1)} %get-tuple-element.168), channel_id=1, source_target_pairs={{0,1},{1,0},{2,3},{3,2},{4,5},{5,4},{6,7},{7,6},{8,9},{9,8},{10,11... | collective-permute-start | bytes 2359304 | tf_op jit(solution)/shard_map/ppermute | solution.py:22
  382.9 10.2 %collective-permute-start.19 = (bf16[1,512,768]{2,1,0:T(8,128)(2,1)S(1)}, bf16[1,512,768]{2,1,0:T(8,128)(2,1)S(1)}, u32[]{:S(2)}, u32[]{:S(2)}) collective-permute-start(bf16[1,512,768]{2,1,0:T(8,128)(2,1)S(1)} %fusion.85), channel_id=1, source_target_pairs={{0,2},{2,0},{1,3},{3,1},{4,6},{6,4},{5,7},{7,5},{8,10},{10,8},{9,1... | collective-permute-start | bytes 2359304 | tf_op jit(solution)/shard_map/ppermute | solution.py:22
  386.4 19.7 %collective-permute-start.21 = (bf16[1,512,768]{2,1,0:T(8,128)(2,1)S(1)}, bf16[1,512,768]{2,1,0:T(8,128)(2,1)S(1)}, u32[]{:S(2)}, u32[]{:S(2)}) collective-permute-start(bf16[1,512,768]{2,1,0:T(8,128)(2,1)S(1)} %fusion.49), channel_id=1, source_target_pairs={{0,1},{1,0},{2,3},{3,2},{4,5},{5,4},{6,7},{7,6},{8,9},{9,8},{10,11... | collective-permute-start | bytes 2359304 | tf_op jit(solution)/shard_map/ppermute | solution.py:22
  411.5 19.3 %collective-permute-start.22 = (bf16[1,512,768]{2,1,0:T(8,128)(2,1)}, bf16[1,512,768]{2,1,0:T(8,128)(2,1)}, u32[]{:S(2)}, u32[]{:S(2)}) collective-permute-start(bf16[1,512,768]{2,1,0:T(8,128)(2,1)} %get-tuple-element.165), channel_id=1, source_target_pairs={{0,1},{1,0},{2,3},{3,2},{4,5},{5,4},{6,7},{7,6},{8,9},{9,8},{10,11... | collective-permute-start | bytes 2359304 | tf_op jit(solution)/shard_map/ppermute | solution.py:22
  448.9 18.6 %collective-permute-start.23 = (bf16[1,512,768]{2,1,0:T(8,128)(2,1)S(1)}, bf16[1,512,768]{2,1,0:T(8,128)(2,1)S(1)}, u32[]{:S(2)}, u32[]{:S(2)}) collective-permute-start(bf16[1,512,768]{2,1,0:T(8,128)(2,1)S(1)} %fusion.87), channel_id=1, source_target_pairs={{0,1},{1,0},{2,3},{3,2},{4,5},{5,4},{6,7},{7,6},{8,9},{9,8},{10,11... | collective-permute-start | bytes 2359304 | tf_op jit(solution)/shard_map/ppermute | solution.py:22
  (136 other events, 1095.6 us)
Sparse Core Ops, SparseCore 0:
  242.4 179.1 all-reduce.6
  470.0 207.8 all-reduce.4
